TPU v7x, 8 devices: a whole 2x2x1 slice. The times are simulated.
8 devices in a mesh: tp: 4 (over z, y, x), cp: 2 (over core).
Axes of the slice: x: 2, y: 2, z: 1, core: 2. Of those that a mesh axis runs over, the one named last changes fastest.
Arguments:
- hidden: bfloat16 [12, 1024, 2560], P(None, 'cp')
- grad_out: bfloat16 [12, 1024, 2560], P(None, 'cp')
- w_dq: bfloat16 [2560, 768], replicated
- g_q: bfloat16 [768], replicated
- w_dkv: bfloat16 [2560, 288], replicated
- g_kv: bfloat16 [256], replicated
- w_uq: bfloat16 [768, 40, 96], P(None, 'tp')
- w_uk: bfloat16 [256, 40, 64], P(None, 'tp')
- w_uv: bfloat16 [256, 40, 64], P(None, 'tp')
- w_o: bfloat16 [40, 64, 2560], P('tp')
Outputs:
- output 1: bfloat16 [12, 1024, 2560], P(None, 'cp')
- output 2: bfloat16 [12, 1024, 2560], P(None, 'cp')
- output 3: float32 [2560, 768], replicated
- output 4: float32 [768], replicated
- output 5: float32 [2560, 288], replicated
- output 6: float32 [256], replicated
- output 7: float32 [768, 40, 96], P(None, 'tp')
- output 8: float32 [256, 40, 64], P(None, 'tp')
- output 9: float32 [256, 40, 64], P(None, 'tp')
- output 10: float32 [40, 64, 2560], P('tp')
All inputs are finite; a program needn't handle non-finite values.
Results may differ from a plain program's by a relative error of at most 0.0156823.
Values are sent between devices in bfloat16 or wider.
A program may use at most 1 GiB of HBM per device.

v0:
```python
import jax
import jax.numpy as jnp
from jax import lax
from jax.sharding import PartitionSpec as P

EPS = 1e-6
THETA = 10000.0
NEG_BIG = -1e30


def layout_positions(seq_local, cp_size, cp_rank):
    half_len = seq_local // 2
    local_idx = jnp.arange(seq_local, dtype=jnp.int32)
    block_id = jnp.where(local_idx < half_len, cp_rank, 2 * cp_size - 1 - cp_rank)
    return block_id * half_len + local_idx % half_len


def rope_tables(positions, rope_dim):
    inv_freq = 1.0 / (THETA ** (jnp.arange(rope_dim // 2, dtype=jnp.float32) * 2.0 / rope_dim))
    angles = positions.astype(jnp.float32)[:, None] * inv_freq[None, :]
    return jnp.cos(angles), jnp.sin(angles)


def apply_rope(values, cos_tab, sin_tab):
    half_dim = values.shape[-1] // 2
    lead_half = values[..., :half_dim]
    tail_half = values[..., half_dim:]
    return jnp.concatenate([lead_half * cos_tab - tail_half * sin_tab, tail_half * cos_tab + lead_half * sin_tab], axis=-1)


def unrope(grad_vals, cos_tab, sin_tab):
    half_dim = grad_vals.shape[-1] // 2
    lead_half = grad_vals[..., :half_dim]
    tail_half = grad_vals[..., half_dim:]
    return jnp.concatenate([lead_half * cos_tab + tail_half * sin_tab, tail_half * cos_tab - lead_half * sin_tab], axis=-1)


def norm_f32(raw_vals, gain_vec):
    inv_rms = lax.rsqrt(jnp.mean(raw_vals * raw_vals, axis=-1, keepdims=True) + EPS)
    return raw_vals * inv_rms * gain_vec


def solution(mesh):
    cp_size = mesh.shape['cp']
    next_pairs = [(src_idx, (src_idx + 1) % cp_size) for src_idx in range(cp_size)]

    def per_device(hidden, grad_out, w_dq, g_q, w_dkv, g_kv, w_uq, w_uk, w_uv, w_o):
        cp_rank = lax.axis_index('cp')
        n_batch = hidden.shape[0]
        seq_local = hidden.shape[1]
        value_a6 = w_dq.shape[1]
        value_a7 = g_kv.shape[0]
        nope_dim = w_uk.shape[2]
        qk_dim = w_uq.shape[2]
        heads_dev = w_uq.shape[1]
        v_dim = w_uv.shape[2]
        score_scale = qk_dim ** -0.5
        positions = layout_positions(seq_local, cp_size, cp_rank)
        cos_tab, sin_tab = rope_tables(positions, qk_dim - nope_dim)
        cos_head = cos_tab[:, None, :]
        sin_head = sin_tab[:, None, :]

        cq_raw = jnp.einsum('btd,dq->btq', hidden, w_dq, preferred_element_type=jnp.float32).astype(jnp.bfloat16)
        kv_raw = jnp.einsum('btd,dc->btc', hidden, w_dkv, preferred_element_type=jnp.float32).astype(jnp.bfloat16)
        cq_f32 = cq_raw.astype(jnp.float32)
        ckv_f32 = kv_raw[..., :value_a7].astype(jnp.float32)
        gq_f32 = g_q.astype(jnp.float32)
        gkv_f32 = g_kv.astype(jnp.float32)
        c_q = norm_f32(cq_f32, gq_f32).astype(jnp.bfloat16)
        c_kv = norm_f32(ckv_f32, gkv_f32).astype(jnp.bfloat16)
        k_pe = apply_rope(kv_raw[..., value_a7:].astype(jnp.float32), cos_tab, sin_tab).astype(jnp.bfloat16)
        q_all = jnp.einsum('btq,qhe->bthe', c_q, w_uq, preferred_element_type=jnp.float32).astype(jnp.bfloat16)
        q_nope = q_all[..., :nope_dim]
        q_pe = apply_rope(q_all[..., nope_dim:].astype(jnp.float32), cos_head, sin_head).astype(jnp.bfloat16)
        k_nope = jnp.einsum('btc,chn->bthn', c_kv, w_uk, preferred_element_type=jnp.float32).astype(jnp.bfloat16)
        v_heads = jnp.einsum('btc,chv->bthv', c_kv, w_uv, preferred_element_type=jnp.float32).astype(jnp.bfloat16)

        def block_scores(kn_blk, kp_blk, src_rank):
            key_pos = layout_positions(seq_local, cp_size, src_rank)
            scores = jnp.einsum('bqhn,bkhn->bhqk', q_nope, kn_blk, preferred_element_type=jnp.float32) + jnp.einsum('bqhr,bkr->bhqk', q_pe, kp_blk, preferred_element_type=jnp.float32)
            return jnp.where(key_pos[None, :] <= positions[:, None], scores * score_scale, NEG_BIG)

        def attend(soft_stats, kn_blk, kp_blk, v_blk, src_rank):
            row_max, row_sum, out_acc = soft_stats
            scores = block_scores(kn_blk, kp_blk, src_rank)
            new_max = jnp.maximum(row_max, jnp.max(scores, axis=-1))
            rescale = jnp.exp(row_max - new_max)
            prob_blk = jnp.exp(scores - new_max[..., None])
            row_sum = row_sum * rescale + jnp.sum(prob_blk, axis=-1)
            out_acc = out_acc * rescale[..., None] + jnp.einsum('bhqk,bkhv->bhqv', prob_blk.astype(jnp.bfloat16), v_blk, preferred_element_type=jnp.float32)
            return new_max, row_sum, out_acc

        soft_stats = (jnp.full((n_batch, heads_dev, seq_local), NEG_BIG, jnp.float32), jnp.zeros((n_batch, heads_dev, seq_local), jnp.float32), jnp.zeros((n_batch, heads_dev, seq_local, v_dim), jnp.float32))
        soft_stats = attend(soft_stats, k_nope, k_pe, v_heads, cp_rank)

        def fwd_step(step_idx, loop_state):
            kn_blk, kp_blk, v_blk, soft_stats = loop_state
            kn_blk, kp_blk, v_blk = lax.ppermute((kn_blk, kp_blk, v_blk), 'cp', next_pairs)
            soft_stats = attend(soft_stats, kn_blk, kp_blk, v_blk, (cp_rank - step_idx) % cp_size)
            return kn_blk, kp_blk, v_blk, soft_stats

        loop_state = lax.fori_loop(1, cp_size, fwd_step, (k_nope, k_pe, v_heads, soft_stats))
        row_max, row_sum, out_acc = loop_state[3]
        o_heads = (out_acc / row_sum[..., None]).astype(jnp.bfloat16)
        log_sum = row_max + jnp.log(row_sum)
        attn_out = lax.psum(jnp.einsum('bhtv,hvd->btd', o_heads, w_o, preferred_element_type=jnp.float32), 'tp').astype(jnp.bfloat16)

        grad_o = jnp.einsum('btd,hvd->bhtv', grad_out, w_o, preferred_element_type=jnp.float32).astype(jnp.bfloat16)
        grad_w_o = jnp.einsum('bhtv,btd->hvd', o_heads, grad_out, preferred_element_type=jnp.float32)
        row_dot = jnp.einsum('bhtv,bhtv->bht', grad_o, o_heads, preferred_element_type=jnp.float32)

        def grad_block(kn_blk, kp_blk, v_blk, src_rank):
            prob_blk = jnp.exp(block_scores(kn_blk, kp_blk, src_rank) - log_sum[..., None])
            dv_part = jnp.einsum('bhqk,bhqv->bkhv', prob_blk.astype(jnp.bfloat16), grad_o, preferred_element_type=jnp.float32)
            dp_blk = jnp.einsum('bhqv,bkhv->bhqk', grad_o, v_blk, preferred_element_type=jnp.float32)
            ds_blk = (prob_blk * (dp_blk - row_dot[..., None]) * score_scale).astype(jnp.bfloat16)
            dqn_part = jnp.einsum('bhqk,bkhn->bqhn', ds_blk, kn_blk, preferred_element_type=jnp.float32)
            dqp_part = jnp.einsum('bhqk,bkr->bqhr', ds_blk, kp_blk, preferred_element_type=jnp.float32)
            dkn_part = jnp.einsum('bhqk,bqhn->bkhn', ds_blk, q_nope, preferred_element_type=jnp.float32)
            dkp_part = jnp.einsum('bhqk,bqhr->bkr', ds_blk, q_pe, preferred_element_type=jnp.float32)
            return dqn_part, dqp_part, dkn_part, dkp_part, dv_part

        own_parts = grad_block(k_nope, k_pe, v_heads, cp_rank)
        init_state = (k_nope, k_pe, v_heads, own_parts[2].astype(jnp.bfloat16), own_parts[3].astype(jnp.bfloat16), own_parts[4].astype(jnp.bfloat16), own_parts[0], own_parts[1])

        def bwd_step(step_idx, loop_state):
            kn_blk, kp_blk, v_blk, dkn_blk, dkp_blk, dv_blk, dq_nope, dq_pe = loop_state
            kn_blk, kp_blk, v_blk, dkn_blk, dkp_blk, dv_blk = lax.ppermute((kn_blk, kp_blk, v_blk, dkn_blk, dkp_blk, dv_blk), 'cp', next_pairs)
            step_parts = grad_block(kn_blk, kp_blk, v_blk, (cp_rank - step_idx) % cp_size)
            return (kn_blk, kp_blk, v_blk,
                    (dkn_blk.astype(jnp.float32) + step_parts[2]).astype(jnp.bfloat16),
                    (dkp_blk.astype(jnp.float32) + step_parts[3]).astype(jnp.bfloat16),
                    (dv_blk.astype(jnp.float32) + step_parts[4]).astype(jnp.bfloat16),
                    dq_nope + step_parts[0], dq_pe + step_parts[1])

        loop_state = lax.fori_loop(1, cp_size, bwd_step, init_state)
        grad_k_nope, grad_k_pe, grad_v = lax.ppermute((loop_state[3], loop_state[4], loop_state[5]), 'cp', next_pairs)
        grad_q = jnp.concatenate([loop_state[6], unrope(loop_state[7], cos_head, sin_head)], axis=-1).astype(jnp.bfloat16)

        grad_w_uq = jnp.einsum('btq,bthe->qhe', c_q, grad_q, preferred_element_type=jnp.float32)
        grad_w_uk = jnp.einsum('btc,bthn->chn', c_kv, grad_k_nope, preferred_element_type=jnp.float32)
        grad_w_uv = jnp.einsum('btc,bthv->chv', c_kv, grad_v, preferred_element_type=jnp.float32)
        latent_part = jnp.concatenate([
            jnp.einsum('bthe,qhe->btq', grad_q, w_uq, preferred_element_type=jnp.float32),
            jnp.einsum('bthn,chn->btc', grad_k_nope, w_uk, preferred_element_type=jnp.float32) + jnp.einsum('bthv,chv->btc', grad_v, w_uv, preferred_element_type=jnp.float32),
            grad_k_pe.astype(jnp.float32)], axis=-1)
        latent_grad = lax.psum(latent_part, 'tp')

        norm_q_pull = jax.vjp(norm_f32, cq_f32, gq_f32)[1]
        grad_cq_raw, grad_g_q = norm_q_pull(latent_grad[..., :value_a6])
        norm_kv_pull = jax.vjp(norm_f32, ckv_f32, gkv_f32)[1]
        grad_ckv_raw, grad_g_kv = norm_kv_pull(latent_grad[..., value_a6:value_a6 + value_a7])
        grad_kv_raw = jnp.concatenate([grad_ckv_raw, unrope(latent_grad[..., value_a6 + value_a7:], cos_tab, sin_tab)], axis=-1).astype(jnp.bfloat16)
        grad_cq_raw = grad_cq_raw.astype(jnp.bfloat16)
        grad_w_dq = jnp.einsum('btd,btq->dq', hidden, grad_cq_raw, preferred_element_type=jnp.float32)
        grad_w_dkv = jnp.einsum('btd,btc->dc', hidden, grad_kv_raw, preferred_element_type=jnp.float32)
        grad_hidden = (jnp.einsum('btq,dq->btd', grad_cq_raw, w_dq, preferred_element_type=jnp.float32) + jnp.einsum('btc,dc->btd', grad_kv_raw, w_dkv, preferred_element_type=jnp.float32)).astype(jnp.bfloat16)
        weight_grads = lax.psum((grad_w_dq, grad_g_q, grad_w_dkv, grad_g_kv, grad_w_uq, grad_w_uk, grad_w_uv, grad_w_o), 'cp')
        return (attn_out, grad_hidden) + tuple(weight_grads)

    seq_spec = P(None, 'cp', None)
    full_spec = P()
    head_spec = P(None, 'tp', None)
    out_head_spec = P('tp', None, None)
    all_specs = (seq_spec, seq_spec, full_spec, full_spec, full_spec, full_spec, head_spec, head_spec, head_spec, out_head_spec)
    return jax.shard_map(per_device, mesh=mesh, in_specs=all_specs, out_specs=all_specs, check_vma=False)
```

profile of v0, /device:TPU:0, one launch (start us, length us, event | category | flops | bytes accessed | tf_op | source)
XLA Modules:
  0.0 3873.2 jit_solution(13973303288016195667)
XLA Ops:
  11.2 21.4 convolution_convert_fusion.4
  45.9 6.2 convolution_convert_fusion.3
  57.2 30.5 fusion.31
  88.3 12.0 convolution_convert_fusion.1
  100.3 6.5 slice_convert_fusion
  106.8 48.1 %fusion.56 = f32[12,10,512,512]{2,3,1,0:T(8,128)} fusion(bf16[12,512,10,64]{1,3,2,0:T(8,128)(2,1)} %convolution_convert_fusion.3, bf16[12,512,10,96]{1,3,2,0:T(8,128)(2,1)} %convolution_convert_fusion.1), kind=kOutput, calls=%fused_computation.84 | convolution fusion | flops 4026531840 | bytes 141557760 | tf_op jit(solution)/shard_map/bqhn,bkhn->bhqk/dot_general | solution.py:80
  155.0 6.6 subtract_convert_fusion.1
  162.6 81.5 %fusion.107 = (f32[12,10,512]{2,1,0:T(8,128)}, f32[12,10,512,512]{2,3,1,0:T(8,128)}) fusion(f32[12,10,512,512]{2,3,1,0:T(8,128)} %fusion.56, bf16[12,512,10,16]{1,3,2,0:T(8,128)(2,1)} %get-tuple-element.149, bf16[12,512,10,16]{1,3,2,0:T(8,128)(2,1)} %get-tuple-element.148, bf16[12,512,16]{1,2,0:T(8,128)(2,1)} %copy.95, ...), kind=kOutput, calls=%fused_computation.165 | convolution fusion | flops 2147684352 | bytes 256491520 | tf_op jit(solution)/shard_map/bqhr,bkr->bhqk/dot_general | solution.py:80
  244.0 28.1 fusion.106
  272.1 44.2 %fusion.80 = f32[12,512,512,10]{2,1,3,0:T(8,128)} fusion(bf16[12,512,32]{1,2,0:T(8,128)(2,1)} %collective-permute-done.1, bf16[12,512,10,16]{1,3,2,0:T(8,128)(2,1)} %get-tuple-element.149, bf16[12,512,10,16]{1,3,2,0:T(8,128)(2,1)} %get-tuple-element.148), kind=kOutput, calls=%fused_computation.126 | convolution fusion | flops 2021130240 | bytes 130154496 | tf_op jit(solution)/shard_map/while/body/eval_jaxpr/bqhr,bkr->bhqk/dot_general | solution.py:80
  316.4 85.8 %fusion.108 = (f32[12,10,512]{2,1,0:T(8,128)}, f32[12,10,512,512]{2,3,1,0:T(8,128)}) fusion(f32[12,512,512,10]{2,1,3,0:T(8,128)} %fusion.80, bf16[12,512,10,64]{1,3,2,0:T(8,128)(2,1)} %collective-permute-done, bf16[12,512,10,96]{1,3,2,0:T(8,128)(2,1)} %convolution_convert_fusion.1, pred[512,512]{0,1:T(8,128)(4,1)S(1)} %copy-done.4), kind=kOutput, calls=%fused_computation.166 | convolution fusion | flops 4152299520 | bytes 267894784 | tf_op jit(solution)/shard_map/while/body/eval_jaxpr/bqhn,bkhn->bhqk/dot_general | solution.py:80
  404.3 39.3 %fusion.4 = f32[12,10,512]{2,1,0:T(8,128)} fusion(f32[12,10,512,512]{2,3,1,0:T(8,128)} %get-tuple-element.164, f32[12,10,512]{2,1,0:T(8,128)} %get-tuple-element.154), kind=kLoop, calls=%fused_computation.12 | loop fusion | flops 62853120 | bytes 126320640 | tf_op jit(solution)/shard_map/reduce_sum | solution.py:89
  443.6 39.2 %fusion.6 = f32[12,10,512]{2,1,0:T(8,128)} fusion(f32[12,10,512,512]{2,3,1,0:T(8,128)} %get-tuple-element.166, f32[12,10,512]{2,1,0:T(8,128)} %get-tuple-element.153), kind=kLoop, calls=%fused_computation.14 | loop fusion | flops 62853120 | bytes 126320640 | tf_op jit(solution)/shard_map/while/body/eval_jaxpr/reduce_sum | solution.py:89
  485.4 45.4 %convert_bitcast_fusion = bf16[12,512,10,64]{1,3,2,0:T(8,128)(2,1)} fusion(f32[12,10,512,512]{2,3,1,0:T(8,128)} %get-tuple-element.164, f32[12,10,512]{2,1,0:T(8,128)} %get-tuple-element.139, bf16[12,10,512,64]{2,3,0,1:T(8,128)(2,1)} %get-tuple-element.160), kind=kOutput, calls=%fused_computation.61 | convolution fusion | flops 4093378560 | bytes 141803520 | tf_op jit(solution)/shard_map/bhqk,bhqv->bkhv/dot_general | solution.py:114
  530.8 48.6 %fusion.16 = f32[12,10,512,64]{2,3,1,0:T(8,128)} fusion(bf16[12,512,10,64]{1,3,2,0:T(8,128)(2,1)} %convolution_convert_fusion.2, f32[12,10,512,512]{2,3,1,0:T(8,128)} %get-tuple-element.164, f32[12,10,512]{2,1,0:T(8,128)} %get-tuple-element.154), kind=kOutput, calls=%fused_computation.21 | convolution fusion | flops 4089446400 | bytes 149667840 | tf_op jit(solution)/shard_map/bhqk,bkhv->bhqv/dot_general | solution.py:90
  579.3 57.0 %multiply_reduce_fusion = (f32[12,10,512]{2,1,0:T(8,128)}, bf16[12,10,512,64]{2,3,1,0:T(8,128)(2,1)}) fusion(f32[12,10,512,64]{2,3,0,1:T(8,128)} %get-tuple-element.159, f32[12,10,512]{2,1,0:T(8,128)} %get-tuple-element.140, f32[12,10,512]{2,1,0:T(8,128)} %get-tuple-element.141, f32[12,10,512,64]{2,3,1,0:T(8,128)} %fusion.16, ...), kind=kOutput, calls=%fused_computation.50 | convolution fusion | flops 4120842240 | bytes 174243840 | tf_op jit(solution)/shard_map/while/body/eval_jaxpr/bhqk,bkhv->bhqv/dot_general | solution.py:90
  636.3 68.0 %multiply_convert_fusion.1 = bf16[12,10,512,512]{2,3,1,0:T(8,128)(2,1)} fusion(f32[12,10,512,512]{2,3,1,0:T(8,128)} %get-tuple-element.164, f32[12,10,512]{2,1,0:T(8,128)} %get-tuple-element.142, f32[12,10,512]{2,1,0:T(8,128)} %get-tuple-element.139, bf16[12,512,10,64]{1,3,2,0:T(8,128)(2,1)} %convolution_convert_fusion.2, ...), kind=kOutput, calls=%fused_computation.8 | convolution fusion | flops 4183818240 | bytes 204963840 | tf_op jit(solution)/shard_map/bhqv,bkhv->bhqk/dot_general | solution.py:115
  704.3 26.6 fusion.78
  731.0 25.5 fusion.82
  756.5 30.3 convert_bitcast_fusion.1
  786.8 30.1 fusion.109
  817.5 33.5 convolution_bitcast_fusion
  851.0 68.0 %multiply_convert_fusion = bf16[12,10,512,512]{2,3,1,0:T(8,128)(2,1)} fusion(f32[12,10,512,512]{2,3,1,0:T(8,128)} %get-tuple-element.166, f32[12,10,512]{2,1,0:T(8,128)} %get-tuple-element.142, f32[12,10,512]{2,1,0:T(8,128)} %get-tuple-element.139, bf16[12,512,10,64]{1,3,2,0:T(8,128)(2,1)} %collective-permute-done.2, ...), kind=kOutput, calls=%fused_computation.6 | convolution fusion | flops 4183818240 | bytes 204963840 | tf_op jit(solution)/shard_map/while/body/eval_jaxpr/bhqv,bkhv->bhqk/dot_general | solution.py:115
  919.1 32.0 fusion.52
  951.1 27.5 add_bitcast_fusion
  978.6 31.7 fusion.34
  1010.8 47.6 %fusion.33 = bf16[12,512,10,64]{1,3,2,0:T(8,128)(2,1)} fusion(bf16[12,512,10,64]{1,3,2,0:T(8,128)(2,1)} %collective-permute-done.5, f32[12,10,512,512]{2,3,1,0:T(8,128)} %get-tuple-element.166, f32[12,10,512]{2,1,0:T(8,128)S(1)} %copy-done.7, bf16[12,10,512,64]{2,3,0,1:T(8,128)(2,1)} %get-tuple-element.160), kind=kOutput, calls=%fused_computation.47 | convolution fusion | flops 4101242880 | bytes 149667840 | tf_op jit(solution)/shard_map/while/body/eval_jaxpr/bhqk,bhqv->bkhv/dot_general | solution.py:114
  1058.4 6.8 add_convert_fusion.2
  1065.2 25.7 add_convert_fusion.5
  1091.3 17.6 convolution_bitcast_fusion.1
  1110.5 8.8 fusion.87
  1119.3 7.9 bitcast_add_fusion.4
  1127.3 9.8 pad_maximum_fusion
  1137.2 32.0 fusion.49
  1169.2 14.9 fusion.70
  1184.1 7.4 convolution_bitcast_fusion.6
  1191.5 7.4 convolution_bitcast_fusion.7
  1198.8 421.2 %all-reduce.6.cloned.1.call-done = f32[12,512,1056]{2,1,0:T(8,128)} async-done(((f32[12,512,1056]{2,1,0:T(8,128)}), f32[12,512,1056]{2,1,0:T(8,128)}) %all-reduce.6.cloned.1.call-update) | async-done | bytes 25952272 | tf_op jit(solution)/shard_map/psum | solution.py:147
  1620.1 4.9 fusion.45
  1625.0 13.3 fusion.29
  1642.3 11.2 fusion.30
  1653.6 32.1 convolution_bitcast_fusion.2
  1689.8 5.7 fusion.46
  1695.5 16.2 convolution_bitcast_fusion.3
  1711.8 2062.1 %all-reduce.9 = bf16[12,512,2560]{2,1,0:T(8,128)(2,1)} all-reduce(f32[12,512,2560]{2,1,0:T(8,128)} %convolution_bitcast_fusion), channel_id=1, replica_groups=mesh['tp'=4,'cp'=2] {'tp'}, use_global_device_ids=true, to_apply=%region_6.7 | all-reduce | flops 15728640 | bytes 94371840 | tf_op jit(solution)/shard_map/psum | solution.py:106
  3777.1 27.3 fusion.73
  3804.5 41.7 %add_convert_fusion = bf16[12,512,2560]{2,1,0:T(8,128)(2,1)} fusion(f32[12,512,2560]{2,1,0:T(8,128)} %fusion.73, bf16[12,512,768]{2,1,0:T(8,128)(2,1)} %fusion.30, bf16[2560,768]{1,0:T(8,128)(2,1)} %param.12), kind=kOutput, calls=%fused_computation.22 | convolution fusion | flops 24190648320 | bytes 107741184 | tf_op jit(solution)/shard_map/btq,dq->btd/dot_general | solution.py:157
  3846.2 9.2 copy.123
  (165 shorter events, 53.8 us)
Async XLA Ops:
  7.2 236.9 %copy-start = (bf16[10,64,2560]{2,1,0:T(8,128)(2,1)S(1)}, bf16[10,64,2560]{2,1,0:T(8,128)(2,1)}, u32[]{:S(2)}) copy-start(bf16[10,64,2560]{2,1,0:T(8,128)(2,1)} %param.19) | copy-start | bytes 9830404
  7.2 1612.9 %all-reduce.6.cloned.1.call-start = ((), (), s32[]{:S(2)}) async-start(), calls=%async_computation | async-start | bytes 56623104 | tf_op jit(solution)/shard_map/psum | solution.py:147
  9.6 23.3 copy-start.13
  11.2 21.7 copy-start.15
  32.9 12.3 copy-start.42
  37.4 14.7 copy-start.10
  41.4 230.7 %collective-permute-start.1 = (bf16[12,512,32]{1,2,0:T(8,128)(2,1)}, bf16[12,512,32]{1,2,0:T(8,128)(2,1)}, u32[]{:S(2)}, u32[]{:S(2)}) collective-permute-start(bf16[12,512,32]{1,2,0:T(8,128)(2,1)} %pad_maximum_fusion.10), channel_id=1, source_target_pairs={{0,1},{1,0},{2,3},{3,2},{4,5},{5,4},{6,7},{7,6}} | collective-permute-start | bytes 1179656 | tf_op jit(solution)/shard_map/while/body/eval_jaxpr/ppermute | solution.py:98
  42.3 9.8 slice-start
  52.0 264.3 %collective-permute-start = (bf16[12,512,10,64]{1,3,2,0:T(8,128)(2,1)}, bf16[12,512,10,64]{1,3,2,0:T(8,128)(2,1)}, u32[]{:S(2)}, u32[]{:S(2)}) collective-permute-start(bf16[12,512,10,64]{1,3,2,0:T(8,128)(2,1)} %convolution_convert_fusion.3), channel_id=1, source_target_pairs={{0,1},{1,0},{2,3},{3,2},{4,5},{5,4},{6,7},{7,6}} | collective-permute-start | bytes 23592968 | tf_op jit(solution)/shard_map/while/body/eval_jaxpr/ppermute | solution.py:98
  56.7 522.6 %collective-permute-start.2 = (bf16[12,512,10,64]{1,3,2,0:T(8,128)(2,1)}, bf16[12,512,10,64]{1,3,2,0:T(8,128)(2,1)}, u32[]{:S(2)}, u32[]{:S(2)}) collective-permute-start(bf16[12,512,10,64]{1,3,2,0:T(8,128)(2,1)} %convolution_convert_fusion.2), channel_id=1, source_target_pairs={{0,1},{1,0},{2,3},{3,2},{4,5},{5,4},{6,7},{7,6}} | collective-permute-start | bytes 23592968 | tf_op jit(solution)/shard_map/while/body/eval_jaxpr/ppermute | solution.py:98
  57.2 31.1 copy-start.33
  57.2 31.1 copy-start.39
  87.7 12.6 copy-start.5
  88.3 12.0 copy-start.29
  106.8 48.2 %copy-start.21 = (f32[512,16]{0,1:T(8,128)S(1)}, f32[512,16]{0,1:T(8,128)}, u32[]{:S(2)}) copy-start(f32[512,16]{0,1:T(8,128)} %get-tuple-element.155) | copy-start | bytes 98308
  106.8 48.2 %copy-start.23 = (f32[512,16]{0,1:T(8,128)S(1)}, f32[512,16]{0,1:T(8,128)}, u32[]{:S(2)}) copy-start(f32[512,16]{0,1:T(8,128)} %get-tuple-element.156) | copy-start | bytes 98308
  272.1 44.2 %copy-start.4 = (pred[512,512]{0,1:T(8,128)(4,1)S(1)}, pred[512,512]{0,1:T(8,128)(4,1)}, u32[]{:S(2)}) copy-start(pred[512,512]{0,1:T(8,128)(4,1)} %get-tuple-element.158) | copy-start | bytes 786436
  704.3 26.6 copy-start.11
  816.9 193.8 %collective-permute-start.5 = (bf16[12,512,10,64]{1,3,2,0:T(8,128)(2,1)}, bf16[12,512,10,64]{1,3,2,0:T(8,128)(2,1)}, u32[]{:S(2)}, u32[]{:S(2)}) collective-permute-start(bf16[12,512,10,64]{1,3,2,0:T(8,128)(2,1)} %convert_bitcast_fusion), channel_id=1, source_target_pairs={{0,1},{1,0},{2,3},{3,2},{4,5},{5,4},{6,7},{7,6}} | collective-permute-start | bytes 23592968 | tf_op jit(solution)/shard_map/while/body/eval_jaxpr/ppermute | solution.py:128
  817.0 248.2 %collective-permute-start.7 = (bf16[12,512,32]{1,2,0:T(8,128)(2,1)}, bf16[12,512,32]{1,2,0:T(8,128)(2,1)}, u32[]{:S(2)}, u32[]{:S(2)}) collective-permute-start(bf16[12,512,32]{1,2,0:T(8,128)(2,1)} %fusion.78), channel_id=1, source_target_pairs={{0,1},{1,0},{2,3},{3,2},{4,5},{5,4},{6,7},{7,6}} | collective-permute-start | bytes 1179656 | tf_op jit(solution)/shard_map/while/body/eval_jaxpr/ppermute | solution.py:128
  817.5 161.2 %collective-permute-start.3 = (bf16[12,512,10,64]{1,3,2,0:T(8,128)(2,1)}, bf16[12,512,10,64]{1,3,2,0:T(8,128)(2,1)}, u32[]{:S(2)}, u32[]{:S(2)}) collective-permute-start(bf16[12,512,10,64]{1,3,2,0:T(8,128)(2,1)} %convert_bitcast_fusion.1), channel_id=1, source_target_pairs={{0,1},{1,0},{2,3},{3,2},{4,5},{5,4},{6,7},{7,6}} | collective-permute-start | bytes 23592968 | tf_op jit(solution)/shard_map/while/body/eval_jaxpr/ppermute | solution.py:128
  978.6 32.1 copy-start.7
  1010.3 48.1 %copy-start.22 = (f32[512,16]{0,1:T(8,128)S(1)}, f32[512,16]{0,1:T(8,128)}, u32[]{:S(2)}) copy-start(f32[512,16]{0,1:T(8,128)} %get-tuple-element.155) | copy-start | bytes 98308
  1010.3 48.1 %copy-start.24 = (f32[512,16]{0,1:T(8,128)S(1)}, f32[512,16]{0,1:T(8,128)}, u32[]{:S(2)}) copy-start(f32[512,16]{0,1:T(8,128)} %get-tuple-element.156) | copy-start | bytes 98308
  1010.3 100.2 %collective-permute-start.4 = (bf16[12,512,10,64]{1,3,2,0:T(8,128)(2,1)}, bf16[12,512,10,64]{1,3,2,0:T(8,128)(2,1)}, u32[]{:S(2)}, u32[]{:S(2)}) collective-permute-start(bf16[12,512,10,64]{1,3,2,0:T(8,128)(2,1)} %fusion.34), channel_id=1, source_target_pairs={{0,1},{1,0},{2,3},{3,2},{4,5},{5,4},{6,7},{7,6}} | collective-permute-start | bytes 23592968 | tf_op jit(solution)/shard_map/ppermute | solution.py:137
  1058.3 60.9 %collective-permute-start.6 = (bf16[12,512,10,64]{1,3,2,0:T(8,128)(2,1)}, bf16[12,512,10,64]{1,3,2,0:T(8,128)(2,1)}, u32[]{:S(2)}, u32[]{:S(2)}) collective-permute-start(bf16[12,512,10,64]{1,3,2,0:T(8,128)(2,1)} %fusion.33), channel_id=1, source_target_pairs={{0,1},{1,0},{2,3},{3,2},{4,5},{5,4},{6,7},{7,6}} | collective-permute-start | bytes 23592968 | tf_op jit(solution)/shard_map/ppermute | solution.py:137
  1090.8 18.1 collective-permute-start.8
  1110.4 8.8 copy-start.41
  1110.5 16.8 slice-start.4
  1110.5 16.8 slice-start.5
  1110.5 16.8 slice-start.6
  1119.3 8.0 slice-start.8
  1137.1 32.1 copy-start.17
  1137.1 32.1 copy-start.30
  1137.1 32.1 copy-start.34
  1137.1 2709.0 %all-reduce.8.cloned.1.call-start = ((), (), s32[]{:S(2)}) async-start(), calls=%async_computation.1 | async-start | bytes 43253760 | tf_op jit(solution)/shard_map/psum | solution.py:158
  1137.2 32.0 copy-start.18
  1169.2 14.9 copy-start.26
  1169.2 14.9 copy-start.37
  1198.8 426.1 %copy-start.28 = (f32[12,512]{1,0:T(8,128)S(1)}, f32[12,512]{1,0:T(8,128)}, u32[]{:S(2)}) copy-start(f32[12,512]{1,0:T(8,128)} %copy-done.27) | copy-start | bytes 73732
  1625.0 13.3 copy-start.32
  1625.0 17.3 copy-start.2
  1642.3 47.5 %slice-start.2 = ((s8[4718592]{0:T(1024)(128)(4,1)}), s8[524288]{0:T(1024)(128)(4,1)S(1)}, s32[]{:S(2)}) async-start(s8[4718592]{0:T(1024)(128)(4,1)} %bitcast.197), calls=%async_computation.4 | async-start | bytes 1048576
  1653.5 32.1 copy-start.14
  1653.6 32.1 copy-start.16
  1653.6 36.2 slice-start.3
  3846.2 9.2 copy-start.12
  3857.0 8.9 copy-start.1
  (17 other events, 94.0 us)
Sparse Core Ops, SparseCore 0:
  1137.2 482.8 all-reduce.5
  1711.9 60.4 all-reduce.7
where the time goes:
time: 3880 us; the launch traced here: 3870 us
  blocking collectives  2070 us (53%)
  matrix products  1170 us (30%)
  waiting for transfers between devices  421 us (11%)
  other arithmetic  162 us (4%)
    psum x1, blocking collectives, per_device(): lax.psum(jnp.einsum('bhtv,hvd->btd', o_heads, w_o, preferred_element_type...  2060 us
    psum x1, waiting for transfers between devices, per_device(): latent_grad = lax.psum(latent_part, 'tp')  421 us
    dot_general x2, matrix products, grad_block(): jnp.einsum('bhqv,bkhv->bhqk', grad_o, v_blk, preferred_element_type=jnp.f...  136 us
    dot_general x2, matrix products, block_scores(): jnp.einsum('bqhn,bkhn->bhqk', q_nope, kn_blk, preferred_element_type=jnp....  134 us
    dot_general x2, matrix products, block_scores(): jnp.einsum('bqhr,bkr->bhqk', q_pe, kp_blk, preferred_element_type=jnp.flo...  126 us
    dot_general x2, matrix products, attend(): jnp.einsum('bhqk,bkhv->bhqv', prob_blk.astype(jnp.bfloat16), v_blk, prefe...  106 us
    dot_general x2, matrix products, grad_block(): jnp.einsum('bhqk,bhqv->bkhv', prob_blk.astype(jnp.bfloat16), grad_o, pref...  93 us
    reduce_sum x2, other arithmetic, attend(): row_sum = row_sum * rescale + jnp.sum(prob_blk, axis=-1)  78.5 us
  transfers between devices with their start and end apart: 11, of which 1 were waited for; matrix products, arithmetic and copies ran while one was open for 25% of the time, Pallas kernels for 0%

commit v1 on v0

v1 whole, which is shorter than its diff:
```python
import functools

import jax
import jax.numpy as jnp
from jax import lax
from jax.experimental import pallas as pl
from jax.experimental.pallas import tpu as pltpu
from jax.sharding import PartitionSpec as P

EPS = 1e-6
THETA = 10000.0
NEG_BIG = -1e30
LOG2E = 1.4426950408889634
F32 = jnp.float32
BF16 = jnp.bfloat16

NN = (((1,), (0,)), ((), ()))
NT = (((1,), (1,)), ((), ()))


def mm(a, b, dims=NN):
    return lax.dot_general(a, b, dims, preferred_element_type=F32)


def rope_tables(positions, rope_dim):
    inv_freq = 1.0 / (THETA ** (jnp.arange(rope_dim // 2, dtype=F32) * 2.0 / rope_dim))
    angles = positions.astype(F32)[:, None] * inv_freq[None, :]
    return jnp.cos(angles), jnp.sin(angles)


def apply_rope(values, cos_tab, sin_tab):
    half_dim = values.shape[-1] // 2
    lead_half = values[..., :half_dim]
    tail_half = values[..., half_dim:]
    return jnp.concatenate([lead_half * cos_tab - tail_half * sin_tab, tail_half * cos_tab + lead_half * sin_tab], axis=-1)


def unrope(grad_vals, cos_tab, sin_tab):
    half_dim = grad_vals.shape[-1] // 2
    lead_half = grad_vals[..., :half_dim]
    tail_half = grad_vals[..., half_dim:]
    return jnp.concatenate([lead_half * cos_tab + tail_half * sin_tab, tail_half * cos_tab - lead_half * sin_tab], axis=-1)


def norm_f32(raw_vals, gain_vec):
    inv_rms = lax.rsqrt(jnp.mean(raw_vals * raw_vals, axis=-1, keepdims=True) + EPS)
    return raw_vals * inv_rms * gain_vec


def attn_kernel(first, blk, scale, *refs):
    (rank_ref, qn_ref, qp_ref, do_ref, ckv_ref, ckvt_ref, kpe_ref, kpet_ref, wuk_ref, wuv_ref, cos_ref, sin_ref) = refs[:12]
    refs = refs[12:]
    if not first:
        dwk_in, dwv_in = refs[:2]
        refs = refs[6:]
    (o_ref, dqn_ref, dqp_ref, dc_ref, dkp_ref, dwk_ref, dwv_ref,
     k_s, kt_s, v_s, vt_s, e_s, g_s, p_s, ds_s, qm_s, dom_s, dk_s, dv_s) = refs
    step = pl.program_id(0)
    nkeys = ckv_ref.shape[1]
    qrows = qn_ref.shape[1]
    nope = 64
    lane128 = lax.broadcasted_iota(jnp.int32, (1, 128), 1)
    lane256 = lax.broadcasted_iota(jnp.int32, (1, 256), 1)
    coef = scale * LOG2E

    ckv = ckv_ref[0]
    ckvt = ckvt_ref[0]
    wuk = wuk_ref[...]
    wuv = wuv_ref[...]
    k_s[:, :256] = mm(ckv, wuk, NT).astype(BF16)
    v_s[...] = mm(ckv, wuv, NT).astype(BF16)
    kt_s[...] = mm(wuk, ckvt).astype(BF16)
    vt_s[...] = mm(wuv, ckvt).astype(BF16)

    def swap(u):
        return jnp.where(lane128 % 32 < 16, pltpu.roll(u, 112, 1), pltpu.roll(u, 16, 1))

    qpu = qp_ref[0].astype(F32)
    cos = cos_ref[...]
    sin = sin_ref[...]
    qpr = (qpu * cos + swap(qpu) * sin).astype(BF16)
    qn = qn_ref[0]
    do = do_ref[0]
    zero = jnp.zeros((), BF16)
    for h in range(4):
        pair = h // 2
        sel = (lane128 >= 64 * (h % 2)) & (lane128 < 64 * (h % 2) + 64)
        qm_s[h, :, :128] = jnp.where(sel, qn[:, pair * 128:pair * 128 + 128], zero)
        selp = (lane128 >= 32 * h) & (lane128 < 32 * h + 32)
        qm_s[h, :, 128:] = jnp.where(selp, qpr, zero)
        selo = (lane256 >= 64 * h) & (lane256 < 64 * h + 64)
        dom_s[h] = jnp.where(selo, do, zero)

    def one_block(row0, nk, add):
        rows = slice(row0, row0 + blk)
        nch = nk // blk
        dqp_parts = []
        for pair in range(2):
            kops = [jnp.concatenate([k_s[c * blk:(c + 1) * blk, pair * 128:pair * 128 + 128], kpe_ref[0, c * blk:(c + 1) * blk, :]], axis=1) for c in range(nch)]
            o_parts = []
            dq_parts = []
            for hh in range(2):
                h = 2 * pair + hh
                slot = h % 2
                qm = qm_s[h, rows, :]
                dom = dom_s[h, rows, :]
                mx = None
                for c in range(nch):
                    st = mm(kops[c], qm, NT)
                    if c == nch - 1:
                        keep = lax.broadcasted_iota(jnp.int32, (blk, blk), 0) <= lax.broadcasted_iota(jnp.int32, (blk, blk), 1)
                        st = jnp.where(keep, st, NEG_BIG)
                    e_s[slot, c * blk:(c + 1) * blk, :] = st
                    cm = jnp.max(st.reshape(blk // 8, 8, blk), axis=0)
                    mx = cm if mx is None else jnp.maximum(mx, cm)
                mx = jnp.max(mx, axis=0, keepdims=True)
                tot = None
                for c in range(nch):
                    ks = slice(c * blk, (c + 1) * blk)
                    e = jnp.exp2((e_s[slot, ks, :] - mx) * coef)
                    e_s[slot, ks, :] = e
                    dp = mm(v_s[ks, :], dom, NT)
                    g_s[slot, ks, :] = dp
                    ce = jnp.sum(e.reshape(blk // 8, 8, blk), axis=0)
                    cd = jnp.sum((e * dp).reshape(blk // 8, 8, blk), axis=0)
                    tot = (ce, cd) if tot is None else (tot[0] + ce, tot[1] + cd)
                inv = 1.0 / jnp.sum(tot[0], axis=0, keepdims=True)
                dot = jnp.sum(tot[1], axis=0, keepdims=True) * inv
                cols = slice(h * blk, (h + 1) * blk)
                for c in range(nch):
                    ks = slice(c * blk, (c + 1) * blk)
                    p = e_s[slot, ks, :] * inv
                    p_s[ks, cols] = p.astype(BF16)
                    ds_s[ks, cols] = (p * (g_s[slot, ks, :] - dot)).astype(BF16)
                hr = slice(h * nope, (h + 1) * nope)
                o_parts.append(mm(vt_s[hr, :nk], p_s[:nk, cols]))
                dqt = mm(jnp.concatenate([kt_s[hr, :nk], kpet_ref[0, :, :nk]], axis=0), ds_s[:nk, cols])
                dq_parts.append(dqt[:nope])
                dqp_parts.append(dqt[nope:])
            lanes = slice(pair * 128, pair * 128 + 128)
            o_ref[0, rows, lanes] = jnp.concatenate(o_parts, axis=0).T.astype(BF16)
            dqn_ref[0, rows, lanes] = (jnp.concatenate(dq_parts, axis=0).T * scale).astype(BF16)
            qcat = jnp.concatenate([qm_s[2 * pair, rows, :], qm_s[2 * pair + 1, rows, :]], axis=0)
            for c in range(nch):
                ks = slice(c * blk, (c + 1) * blk)
                dk = mm(ds_s[ks, pair * 2 * blk:(pair + 1) * 2 * blk], qcat)
                if add:
                    dk_s[pair, ks, :] += dk
                else:
                    dk_s[pair, ks, :] = dk
        dqp = jnp.concatenate(dqp_parts, axis=0).T * scale
        dqp_ref[0, rows, :] = (dqp * cos[rows] - swap(dqp) * sin[rows]).astype(BF16)
        docat = jnp.concatenate([dom_s[h, rows, :] for h in range(4)], axis=0)
        for c in range(nch):
            ks = slice(c * blk, (c + 1) * blk)
            dv = mm(p_s[ks, :], docat)
            if add:
                dv_s[ks, :] += dv
            else:
                dv_s[ks, :] = dv

    rank = rank_ref[0]
    hi = qrows - blk

    @pl.when(rank == 0)
    def _():
        one_block(hi, 4 * blk, False)
        one_block(0, blk, True)

    @pl.when(rank == 1)
    def _():
        one_block(hi, 3 * blk, False)
        dk_s[:, 3 * blk:, :] = jnp.zeros_like(dk_s[:, 3 * blk:, :])
        dv_s[3 * blk:, :] = jnp.zeros_like(dv_s[3 * blk:, :])
        one_block(0, 2 * blk, True)

    dkb = (jnp.concatenate([dk_s[0, :, :128], dk_s[1, :, :128]], axis=1) * scale).astype(BF16)
    dvb = dv_s[...].astype(BF16)
    dkp = (dk_s[0, :, 128:] + dk_s[1, :, 128:]) * scale
    dc = mm(dkb, wuk) + mm(dvb, wuv)
    dwk = mm(ckvt, dkb)
    dwv = mm(ckvt, dvb)
    if first:
        dwk_ref[...] = dwk
        dwv_ref[...] = dwv
    else:
        dwk_ref[...] = dwk_in[...] + dwk
        dwv_ref[...] = dwv_in[...] + dwv

    @pl.when(step == 0)
    def _():
        dc_ref[0] = dc
        dkp_ref[0] = dkp

    @pl.when(step > 0)
    def _():
        dc_ref[0] += dc
        dkp_ref[0] += dkp


def attention(j, rank_arr, qn, qp, do, ckv, ckvt, kpe4, kpet, wuk, wuv, cos, sin, prev, scale):
    nb, qrows, width = qn.shape
    nkeys, latent = ckv.shape[1:]
    groups = width // 256
    blk = qrows // 2
    first = prev is None
    row = lambda i: (j, 0, i)
    whole = lambda i: (j, 0, 0)
    in_specs = [
        pl.BlockSpec(memory_space=pltpu.SMEM),
        pl.BlockSpec((1, qrows, 256), row),
        pl.BlockSpec((1, qrows, 128), row),
        pl.BlockSpec((1, qrows, 256), row),
        pl.BlockSpec((1, nkeys, latent), whole),
        pl.BlockSpec((1, latent, nkeys), whole),
        pl.BlockSpec((1, nkeys, 128), whole),
        pl.BlockSpec((1, 32, nkeys), whole),
        pl.BlockSpec((256, latent), lambda i: (i, 0)),
        pl.BlockSpec((256, latent), lambda i: (i, 0)),
        pl.BlockSpec((qrows, 128), lambda i: (0, 0)),
        pl.BlockSpec((qrows, 128), lambda i: (0, 0)),
    ]
    args = [rank_arr, qn, qp, do, ckv, ckvt, kpe4, kpet, wuk, wuv, cos, sin]
    aliases = {}
    if not first:
        dqn, dqp, dc, dkp, dwk, dwv = prev
        in_specs += [pl.BlockSpec((latent, 256), lambda i: (0, i))] * 2 + [pl.BlockSpec(memory_space=pl.ANY)] * 4
        args += [dwk, dwv, dqn, dqp, dc, dkp]
        aliases = {12: 5, 13: 6, 14: 1, 15: 2, 16: 3, 17: 4}
    out_specs = [
        pl.BlockSpec((1, qrows, 256), lambda i: (0, 0, i)),
        pl.BlockSpec((1, qrows, 256), row),
        pl.BlockSpec((1, qrows, 128), row),
        pl.BlockSpec((1, nkeys, latent), whole),
        pl.BlockSpec((1, nkeys, 128), whole),
        pl.BlockSpec((latent, 256), lambda i: (0, i)),
        pl.BlockSpec((latent, 256), lambda i: (0, i)),
    ]
    out_shape = [
        jax.ShapeDtypeStruct((1, qrows, width), BF16),
        jax.ShapeDtypeStruct((nb, qrows, width), BF16),
        jax.ShapeDtypeStruct((nb, qrows, width // 2), BF16),
        jax.ShapeDtypeStruct((nb, nkeys, latent), F32),
        jax.ShapeDtypeStruct((nb, nkeys, 128), F32),
        jax.ShapeDtypeStruct((latent, width), F32),
        jax.ShapeDtypeStruct((latent, width), F32),
    ]
    scratch = [
        pltpu.VMEM((nkeys, 256), BF16), pltpu.VMEM((256, nkeys), BF16),
        pltpu.VMEM((nkeys, 256), BF16), pltpu.VMEM((256, nkeys), BF16),
        pltpu.VMEM((2, nkeys, blk), F32), pltpu.VMEM((2, nkeys, blk), F32),
        pltpu.VMEM((nkeys, 4 * blk), BF16), pltpu.VMEM((nkeys, 4 * blk), BF16),
        pltpu.VMEM((4, qrows, 256), BF16), pltpu.VMEM((4, qrows, 256), BF16),
        pltpu.VMEM((2, nkeys, 256), F32), pltpu.VMEM((nkeys, 256), F32),
    ]
    pairs = 5 * 4 * groups * blk * blk
    return pl.pallas_call(
        functools.partial(attn_kernel, first, blk, scale),
        grid=(groups,),
        in_specs=in_specs,
        out_specs=out_specs,
        out_shape=out_shape,
        scratch_shapes=scratch,
        input_output_aliases=aliases,
        name="attn_fwd_bwd",
        compiler_params=pltpu.CompilerParams(dimension_semantics=("arbitrary",), vmem_limit_bytes=56 * 1024 * 1024),
        cost_estimate=pl.CostEstimate(flops=pairs * 6 * 2 * 256, bytes_accessed=40 * 1024 * 1024, transcendentals=pairs),
    )(*args)


def out_kernel(o_ref, w_ref, *rest):
    y_ref = rest[-1]
    w = w_ref[...]
    for t in range(o_ref.shape[0]):
        y_ref[t, 0] = mm(o_ref[t], w).astype(BF16)


def out_proj(j, nb, o_all, w_o, prev):
    tp, rows, width = o_all.shape
    dim = w_o.shape[1]
    in_specs = [pl.BlockSpec((tp, rows, width), lambda i: (0, 0, 0)), pl.BlockSpec((width, 256), lambda i: (0, i))]
    args = [o_all, w_o]
    aliases = {}
    if prev is not None:
        in_specs.append(pl.BlockSpec(memory_space=pl.ANY))
        args.append(prev)
        aliases = {2: 0}
    return pl.pallas_call(
        out_kernel,
        grid=(dim // 256,),
        in_specs=in_specs,
        out_specs=pl.BlockSpec((tp, 1, rows, 256), lambda i: (0, j, 0, i)),
        out_shape=jax.ShapeDtypeStruct((tp, nb, rows, dim), BF16),
        input_output_aliases=aliases,
        name="out_proj",
        compiler_params=pltpu.CompilerParams(dimension_semantics=("arbitrary",), vmem_limit_bytes=56 * 1024 * 1024),
        cost_estimate=pl.CostEstimate(flops=2 * tp * rows * width * dim, bytes_accessed=2 * (2 * tp * rows * width + width * dim), transcendentals=0),
    )(*args)


def solution(mesh):
    cp_size = mesh.shape['cp']
    tp_size = mesh.shape['tp']
    swap_pairs = [(0, 1), (1, 0)]

    def per_device(hidden, grad_out, w_dq, g_q, w_dkv, g_kv, w_uq, w_uk, w_uv, w_o):
        cp_rank = lax.axis_index('cp')
        tp_rank = lax.axis_index('tp')
        n_batch, seq_local, dim = hidden.shape
        nb = n_batch // tp_size
        q_lora = w_dq.shape[1]
        kv_lora = g_kv.shape[0]
        nope = w_uk.shape[2]
        qk_dim = w_uq.shape[2]
        rope_dim = qk_dim - nope
        heads_dev = w_uq.shape[1]
        heads = heads_dev * tp_size
        v_dim = w_uv.shape[2]
        scale = qk_dim ** -0.5
        half_len = seq_local // 2
        half_heads = heads_dev // 2

        def gather_weight(w):
            half = lax.dynamic_slice_in_dim(w, cp_rank * half_heads, half_heads, 0)
            return lax.all_gather(half, ('tp', 'cp'), axis=0, tiled=True)

        wq_all = gather_weight(jnp.transpose(w_uq, (1, 2, 0)))
        wkv_all = gather_weight(jnp.concatenate([jnp.transpose(w_uk, (1, 2, 0)), jnp.transpose(w_uv, (1, 2, 0))], axis=1))
        wo_all = gather_weight(w_o).reshape(heads * v_dim, dim)
        wqn = wq_all[:, :nope].reshape(heads * nope, q_lora)
        wqp = wq_all[:, nope:].reshape(heads * rope_dim, q_lora)
        wuk = wkv_all[:, :nope].reshape(heads * nope, kv_lora)
        wuv = wkv_all[:, nope:].reshape(heads * v_dim, kv_lora)

        local_idx = jnp.arange(seq_local, dtype=jnp.int32)
        block_id = jnp.where(local_idx < half_len, cp_rank, 2 * cp_size - 1 - cp_rank)
        positions = block_id * half_len + local_idx % half_len
        cos_tab, sin_tab = rope_tables(positions, rope_dim)
        cos128 = jnp.tile(cos_tab, (1, 8))
        sin128 = jnp.tile(jnp.concatenate([-sin_tab, sin_tab], axis=1), (1, 4))

        w_cat = jnp.concatenate([w_dq, w_dkv], axis=1)
        x_own = lax.dynamic_slice_in_dim(hidden, tp_rank * nb, nb, 0)
        dy_own = lax.dynamic_slice_in_dim(grad_out, tp_rank * nb, nb, 0)

        raw = jnp.einsum('btd,dq->btq', x_own, w_cat, preferred_element_type=F32).astype(BF16)
        cq_f32 = raw[..., :q_lora].astype(F32)
        ckv_f32 = raw[..., q_lora:q_lora + kv_lora].astype(F32)
        gq_f32 = g_q.astype(F32)
        gkv_f32 = g_kv.astype(F32)
        c_q = norm_f32(cq_f32, gq_f32).astype(BF16)
        c_kv = norm_f32(ckv_f32, gkv_f32).astype(BF16)
        k_pe = apply_rope(raw[..., q_lora + kv_lora:].astype(F32), cos_tab, sin_tab).astype(BF16)

        def by_position(own, other):
            lo = jnp.where(cp_rank == 0, own[:, :half_len], other[:, :half_len])
            lo2 = jnp.where(cp_rank == 0, other[:, :half_len], own[:, :half_len])
            hi = jnp.where(cp_rank == 0, other[:, half_len:], own[:, half_len:])
            hi2 = jnp.where(cp_rank == 0, own[:, half_len:], other[:, half_len:])
            return jnp.concatenate([lo, lo2, hi, hi2], axis=1)

        other_kv, other_pe = lax.ppermute((c_kv, k_pe), 'cp', swap_pairs)
        ckv_seq = by_position(c_kv, other_kv)
        kpe_seq = by_position(k_pe, other_pe)
        ckvt_seq = jnp.swapaxes(ckv_seq, 1, 2)
        kpet_seq = jnp.swapaxes(kpe_seq, 1, 2)
        kpe4 = jnp.tile(kpe_seq, (1, 1, 4))

        qn = jnp.einsum('btq,fq->btf', c_q, wqn, preferred_element_type=F32).astype(BF16)
        qp = jnp.einsum('btq,fq->btf', c_q, wqp, preferred_element_type=F32).astype(BF16)
        grad_o = jnp.einsum('btd,fd->btf', dy_own, wo_all, preferred_element_type=F32).astype(BF16)

        rank_arr = cp_rank.astype(jnp.int32).reshape(1)
        prev = None
        o_all = []
        for j in range(nb):
            res = attention(j, rank_arr, qn, qp, grad_o, ckv_seq, ckvt_seq, kpe4, kpet_seq, wuk, wuv, cos128, sin128, prev, scale)
            o_all.append(lax.all_gather(res[0], 'tp', axis=0, tiled=True))
            prev = res[1:]
        dqn, dqp, dc_seq, dkp_seq, dwk, dwv = prev

        dkp_seq = dkp_seq[..., :32] + dkp_seq[..., 32:64] + dkp_seq[..., 64:96] + dkp_seq[..., 96:]
        lat = jnp.concatenate([dc_seq, dkp_seq], axis=-1)
        b0, b1, b2, b3 = (lat[:, i * half_len:(i + 1) * half_len] for i in range(4))
        outer = jnp.concatenate([b0, b3], axis=1)
        inner = jnp.concatenate([b1, b2], axis=1)
        mine = jnp.where(cp_rank == 0, outer, inner)
        theirs = jnp.where(cp_rank == 0, inner, outer)
        lat = mine + lax.ppermute(theirs, 'cp', swap_pairs)
        grad_cq = jnp.einsum('btf,fq->btq', dqn, wqn, preferred_element_type=F32) + jnp.einsum('btf,fq->btq', dqp, wqp, preferred_element_type=F32)

        norm_q_pull = jax.vjp(norm_f32, cq_f32, gq_f32)[1]
        grad_cq_raw, grad_g_q = norm_q_pull(grad_cq)
        norm_kv_pull = jax.vjp(norm_f32, ckv_f32, gkv_f32)[1]
        grad_ckv_raw, grad_g_kv = norm_kv_pull(lat[..., :kv_lora])
        grad_raw = jnp.concatenate([grad_cq_raw, grad_ckv_raw, unrope(lat[..., kv_lora:], cos_tab, sin_tab)], axis=-1).astype(BF16)
        grad_raw = lax.all_gather(grad_raw, 'tp', axis=0, tiled=True)
        grad_g = lax.psum(jnp.concatenate([grad_g_q, grad_g_kv]), ('tp', 'cp'))

        q_half = q_lora // 2
        cq_mine = lax.dynamic_slice_in_dim(c_q, cp_rank * q_half, q_half, 2)
        cq_theirs = lax.dynamic_slice_in_dim(c_q, (1 - cp_rank) * q_half, q_half, 2)

        def dw_of(dq, cq):
            return jnp.einsum('btf,btq->fq', dq, cq, preferred_element_type=F32)

        dwqn = dw_of(dqn, cq_mine) + lax.ppermute(dw_of(dqn, cq_theirs), 'cp', swap_pairs)
        dwqp = dw_of(dqp, cq_mine) + lax.ppermute(dw_of(dqp, cq_theirs), 'cp', swap_pairs)
        c_half = kv_lora // 2
        dw_kv = jnp.stack([dwk, dwv])
        kv_mine = lax.dynamic_slice_in_dim(dw_kv, cp_rank * c_half, c_half, 1)
        kv_theirs = lax.dynamic_slice_in_dim(dw_kv, (1 - cp_rank) * c_half, c_half, 1)
        dw_kv = kv_mine + lax.ppermute(kv_theirs, 'cp', swap_pairs)
        dwqn = lax.psum_scatter(dwqn, 'tp', scatter_dimension=0, tiled=True)
        dwqp = lax.psum_scatter(dwqp, 'tp', scatter_dimension=0, tiled=True)
        dw_kv = lax.psum_scatter(dw_kv, 'tp', scatter_dimension=2, tiled=True)
        dwq = jnp.concatenate([dwqn.reshape(heads_dev, nope, q_half), dwqp.reshape(heads_dev, rope_dim, q_half)], axis=1)

        def join(part, axis):
            other = lax.ppermute(part, 'cp', swap_pairs)
            return jnp.concatenate([jnp.where(cp_rank == 0, part, other), jnp.where(cp_rank == 0, other, part)], axis=axis)

        grad_w_uq = jnp.transpose(join(dwq, 2), (2, 0, 1))
        dw_kv = join(dw_kv, 1)
        grad_w_uk = dw_kv[0].reshape(kv_lora, heads_dev, nope)
        grad_w_uv = dw_kv[1].reshape(kv_lora, heads_dev, v_dim)

        y = None
        for j in range(nb):
            y = out_proj(j, nb, o_all[j], wo_all, y)
        attn_out = y.reshape(n_batch, seq_local, dim)
        cols = heads_dev * v_dim
        o_mine = jnp.stack([lax.dynamic_slice_in_dim(o, tp_rank * cols, cols, 2) for o in o_all], axis=1).reshape(n_batch, seq_local, cols)
        dwo = jnp.einsum('btf,btd->fd', o_mine, grad_out, preferred_element_type=F32)
        grad_w_o = (dwo + lax.ppermute(dwo, 'cp', swap_pairs)).reshape(heads_dev, v_dim, dim)

        dw_cat = jnp.einsum('btd,btq->dq', hidden, grad_raw, preferred_element_type=F32)
        dw_other = lax.ppermute(dw_cat, 'cp', swap_pairs)
        grad_w_dq = dw_cat[:, :q_lora] + dw_other[:, :q_lora]
        grad_w_dkv = dw_cat[:, q_lora:] + dw_other[:, q_lora:]
        grad_hidden = jnp.einsum('btq,dq->btd', grad_raw, w_cat, preferred_element_type=F32).astype(BF16)
        return (attn_out, grad_hidden, grad_w_dq, grad_g[:q_lora], grad_w_dkv, grad_g[q_lora:], grad_w_uq, grad_w_uk, grad_w_uv, grad_w_o)

    seq_spec = P(None, 'cp', None)
    full_spec = P()
    head_spec = P(None, 'tp', None)
    out_head_spec = P('tp', None, None)
    all_specs = (seq_spec, seq_spec, full_spec, full_spec, full_spec, full_spec, head_spec, head_spec, head_spec, out_head_spec)
    return jax.shard_map(per_device, mesh=mesh, in_specs=all_specs, out_specs=all_specs, check_vma=False)
```

time: 3880 us -> 1220 us (0.31)
  blocking collectives: 2070 us -> 23 us
  matrix products: 1170 us -> 233 us
  Pallas kernels: 0 us -> 368 us
  other arithmetic: 162 us -> 59.8 us
    psum x2 -> x1, blocking collectives: 2070 us -> 23 us  [per_device(): grad_g = lax.psum(jnp.concatenate([grad_g_q, grad_g_kv]), ('tp', 'cp'))]
    dot_general x36 -> x13, matrix products: 1170 us -> 233 us  [the longest x1 46.4 us: per_device(): jnp.einsum('btq,dq->btd', grad_raw, w_cat, preferred_element_type=F32)]
    psum x2 -> x0, waiting for transfers between devices: 421 us -> none  [the longest x1 421 us: per_device(): latent_grad = lax.psum(latent_part, 'tp')]
    all_gather x0 -> x7, waiting for transfers between devices: none -> 385 us  [the longest x3 268 us: per_device(): o_all.append(lax.all_gather(res[0], 'tp', axis=0, tiled=True))]
    pallas_call x0 -> x6, Pallas kernels: none -> 368 us  [the longest x3 265 us: attention(): pl.pallas_call(functools.partial(attn_kernel, first, blk, scale), grid=(g...]
    reduce_sum x2 -> x0, other arithmetic: 78.5 us -> none  [attend(): row_sum = row_sum * rescale + jnp.sum(prob_blk, axis=-1)]
    reduce_scatter x0 -> x3, waiting for transfers between devices: none -> 51.9 us  [the longest x1 34.6 us: per_device(): dw_kv = lax.psum_scatter(dw_kv, 'tp', scatter_dimension=2, tiled=True)]
  transfers between devices with their start and end apart: 11 -> 20, of which waited for: 1 -> 10; matrix products, arithmetic and copies ran while one was open for 25% -> 23% of each run, Pallas kernels for 0% -> 8%
where the time goes in v1:
time: 1220 us
  waiting for transfers between devices  444 us (36%)
  Pallas kernels  368 us (30%)
  matrix products  233 us (19%)
  local copies, waits for them, and re-layouts  63.5 us (5%)
  other arithmetic  59.8 us (5%)
  blocking collectives  23 us (2%)
  between operations  15.3 us (1%)
    all_gather x3, waiting for transfers between devices, per_device(): o_all.append(lax.all_gather(res[0], 'tp', axis=0, tiled=True))  268 us
    pallas_call x3, Pallas kernels, attention(): pl.pallas_call(functools.partial(attn_kernel, first, blk, scale), grid=(g...  265 us
    pallas_call x3, Pallas kernels, out_proj(): pl.pallas_call(out_kernel, grid=(dim // 256,), in_specs=in_specs, out_spe...  103 us
    all_gather x3, waiting for transfers between devices, gather_weight(): return lax.all_gather(half, ('tp', 'cp'), axis=0, tiled=True)  78.4 us
    dot_general x1, matrix products, per_device(): jnp.einsum('btq,dq->btd', grad_raw, w_cat, preferred_element_type=F32)  46.4 us
    dot_general x1, matrix products, per_device(): jnp.einsum('btd,btq->dq', hidden, grad_raw, preferred_element_type=F32)  42.6 us
    all_gather x1, waiting for transfers between devices, per_device(): grad_raw = lax.all_gather(grad_raw, 'tp', axis=0, tiled=True)  38.7 us
    dot_general x1, matrix products, per_device(): jnp.einsum('btd,fd->btf', dy_own, wo_all, preferred_element_type=F32)  38.3 us
  transfers between devices with their start and end apart: 20, of which 10 were waited for; matrix products, arithmetic and copies ran while one was open for 23% of the time, Pallas kernels for 8%

profile of v1, /device:TPU:0, one launch (start us, length us, event | category | flops | bytes accessed | tf_op | source)
XLA Modules:
  0.0 1216.2 jit_solution(6895528468427232716)
XLA Ops:
  9.2 2.0 dynamic-slice_bitcast_fusion.3
  12.7 6.3 copy.95
  19.3 12.7 %fusion.14 = bf16[3,512,1056]{1,2,0:T(8,128)(2,1)S(1)} fusion(bf16[12,512,2560]{2,1,0:T(8,128)(2,1)} %param.10, s32[]{:T(128)S(6)} %select_n.121, bf16[2560,288]{0,1:T(8,128)(2,1)} %param.14, bf16[2560,768]{0,1:T(8,128)(2,1)} %copy.95), kind=kOutput, calls=%fused_computation.29 | convolution fusion | flops 8317157376 | bytes 16515076 | tf_op jit(solution)/shard_map/btd,dq->btq/dot_general | solution.py:346
  48.2 3.5 fusion.56
  51.7 26.0 %all-gather.8.cloned.1.call-done = bf16[40,96,768]{2,1,0:T(8,128)(2,1)} async-done(((bf16[5,96,768]{2,1,0:T(8,128)(2,1)}), bf16[40,96,768]{2,1,0:T(8,128)(2,1)}) %all-gather.8.cloned.1.call-update) | async-done | bytes 5898256 | tf_op jit(solution)/shard_map/all_gather | solution.py:325
  79.4 3.1 slice.151
  83.0 4.8 convolution_convert_fusion.2.refs_2_
  87.7 8.5 convolution_convert_fusion.1.refs_1_
  96.2 52.4 %all-gather.10.cloned.1.call-done = bf16[40,64,2560]{2,1,0:T(8,128)(2,1)} async-done(((bf16[5,64,2560]{2,1,0:T(8,128)(2,1)}), bf16[40,64,2560]{2,1,0:T(8,128)(2,1)}) %all-gather.10.cloned.1.call-update) | async-done | bytes 13107216 | tf_op jit(solution)/shard_map/all_gather | solution.py:325
  148.6 38.3 %fusion.4.refs_3_ = bf16[3,512,2560]{2,1,0:T(8,128)(2,1)} fusion(bf16[2560,2560,1]{1,0,2:T(8,128)(2,1)} %bitcast.112, bf16[12,512,2560]{2,1,0:T(8,128)(2,1)} %param.11, s32[]{:T(128)S(6)} %select_n.121), kind=kOutput, calls=%fused_computation.13 | convolution fusion | flops 20136591360 | bytes 28835844 | tf_op jit(solution)/shard_map/btd,fd->btf/dot_general | solution.py:371
  186.9 87.8 %attn_fwd_bwd.3 = (bf16[1,512,2560]{2,1,0:T(8,128)(2,1)}, bf16[3,512,2560]{2,1,0:T(8,128)(2,1)}, bf16[3,512,1280]{2,1,0:T(8,128)(2,1)}, f32[3,1024,256]{2,1,0:T(...) custom-call(s32[1]{0:T(128)} %bitcast.refs_0_, ...), custom_call_target="tpu_custom_call" | custom-call | flops 40265318400 | bytes 41943040 | tf_op jit(solution)/shard_map/attn_fwd_bwd/pallas_call | solution.py:257
  274.8 88.6 %attn_fwd_bwd.4 = (bf16[1,512,2560]{2,1,0:T(8,128)(2,1)}, bf16[3,512,2560]{2,1,0:T(8,128)(2,1)}, bf16[3,512,1280]{2,1,0:T(8,128)(2,1)}, f32[3,1024,256]{2,1,0:T(...) custom-call(s32[1]{0:T(128)} %bitcast.refs_0_, ...), custom_call_target="tpu_custom_call", output_to_operand_aliasing={{5}: (12, {}), {6}: (13, {}), {1}: (14, {}), {2}: (15, {}),... | custom-call | flops 40265318400 | bytes 41943040 | tf_op jit(solution)/shard_map/attn_fwd_bwd/pallas_call | solution.py:257
  363.4 88.9 %attn_fwd_bwd.5 = (bf16[1,512,2560]{2,1,0:T(8,128)(2,1)}, bf16[3,512,2560]{2,1,0:T(8,128)(2,1)}, bf16[3,512,1280]{2,1,0:T(8,128)(2,1)}, f32[3,1024,256]{2,1,0:T(...) custom-call(s32[1]{0:T(128)} %bitcast.refs_0_, ...), custom_call_target="tpu_custom_call", output_to_operand_aliasing={{5}: (12, {}), {6}: (13, {}), {1}: (14, {}), {2}: (15, {}),... | custom-call | flops 40265318400 | bytes 41943040 | tf_op jit(solution)/shard_map/attn_fwd_bwd/pallas_call | solution.py:257
  452.3 5.8 convolution_bitcast_fusion.4
  458.1 6.8 collective-permute-start.5
  465.0 6.2 convolution_bitcast_fusion.2
  471.2 6.3 fusion.18
  477.9 9.8 fusion.17
  489.4 3.0 fusion.19
  492.6 4.7 collective-permute-done.7
  497.3 3.9 fusion.21
  505.1 2.4 copy.116
  507.5 2.6 slice_add_fusion.2
  512.2 11.1 fusion.57
  523.3 8.3 fusion.10
  536.9 17.3 %reduce-scatter.4.cloned.1.call-done = f32[640,384]{1,0:T(8,128)} async-done(((f32[2560,384]{1,0:T(8,128)}), f32[640,384]{1,0:T(8,128)}) %reduce-scatter.4.cloned.1.call-update) | async-done | bytes 983056 | tf_op jit(solution)/shard_map/reduce_scatter | solution.py:414
  554.2 2.6 pad_maximum_fusion.4
  556.8 34.6 %reduce-scatter.8.cloned.1.call-done = f32[2,128,640]{2,1,0:T(8,128)} async-done(((f32[2,128,2560]{2,1,0:T(8,128)}), f32[2,128,640]{2,1,0:T(8,128)}) %reduce-scatter.8.cloned.1.call-update) | async-done | bytes 655376 | tf_op jit(solution)/shard_map/reduce_scatter | solution.py:416
  591.4 23.0 %psum.7 = f32[1024]{0:T(1024)S(1)} all-reduce(f32[1024]{0:T(1024)S(1)} %pad_maximum_fusion.9), channel_id=1, replica_groups=mesh['tp'=4,'cp'=2] {'tp','cp'}, use_global_device_ids=true, to_apply=%region_6.7 | all-reduce | flops 1024 | bytes 8192 | tf_op jit(solution)/shard_map/psum | solution.py:398
  618.4 2.0 broadcast_select_fusion.2
  622.3 71.6 %all-gather.18.cloned.1.call-done.o_ref = bf16[4,512,2560]{2,1,0:T(8,128)(2,1)} async-done(((bf16[1,512,2560]{2,1,0:T(8,128)(2,1)}), bf16[4,512,2560]{2,1,0:T(8,128)(2,1)}) %all-gather.18.cloned.1.call-update) | async-done | bytes 10485776 | tf_op jit(solution)/shard_map/all_gather | solution.py:378
  695.9 99.2 %all-gather.16.cloned.1.call-done.o_ref = bf16[4,512,2560]{2,1,0:T(8,128)(2,1)} async-done(((bf16[1,512,2560]{2,1,0:T(8,128)(2,1)}), bf16[4,512,2560]{2,1,0:T(8,128)(2,1)}) %all-gather.16.cloned.1.call-update) | async-done | bytes 10485776 | tf_op jit(solution)/shard_map/all_gather | solution.py:378
  795.0 3.5 dynamic-slice_bitcast_fusion.1
  798.5 97.7 %all-gather.14.cloned.1.call-done.o_ref = bf16[4,512,2560]{2,1,0:T(8,128)(2,1)} async-done(((bf16[1,512,2560]{2,1,0:T(8,128)(2,1)}), bf16[4,512,2560]{2,1,0:T(8,128)(2,1)}) %all-gather.14.cloned.1.call-update) | async-done | bytes 10485776 | tf_op jit(solution)/shard_map/all_gather | solution.py:378
  896.2 2.1 dynamic-slice_bitcast_fusion
  898.7 3.7 pad_maximum_fusion
  902.4 10.8 copy.127
  913.2 31.8 %convolution_bitcast_fusion.1 = f32[640,2560]{1,0:T(8,128)} fusion(bf16[12,512,640]{1,2,0:T(8,128)(2,1)} %bitcast.88, bf16[12,512,2560]{2,1,0:T(8,128)(2,1)} %param.11), kind=kOutput, calls=%fused_computation.22 | convolution fusion | flops 20132659200 | bytes 45875200 | tf_op jit(solution)/shard_map/btf,btd->fd/dot_general | solution.py:434
  945.0 34.3 %out_proj.3.rest_0_ = bf16[4,3,512,2560]{3,2,1,0:T(8,128)(2,1)} custom-call(bf16[4,512,2560]{2,1,0:T(8,128)(2,1)} %all-gather.18.cloned.1.call-done.o_ref, bf16[2560,2560]{1,0:T(8,128)(2,1)} %bitcast.113), custom_call_target="tpu_custom_call" | custom-call | flops 26843545600 | bytes 34078720 | tf_op jit(solution)/shard_map/out_proj/pallas_call | solution.py:288
  979.3 38.7 %all-gather.20.cloned.1.call-done = bf16[12,512,1056]{1,2,0:T(8,128)(2,1)} async-done(((bf16[3,512,1056]{1,2,0:T(8,128)(2,1)}), bf16[12,512,1056]{1,2,0:T(8,128)(2,1)}) %all-gather.20.cloned.1.call-update) | async-done | bytes 12976144 | tf_op jit(solution)/shard_map/all_gather | solution.py:397
  1017.9 42.6 %convolution_bitcast_fusion = f32[2560,1056]{0,1:T(8,128)} fusion(bf16[12,512,1056]{1,2,0:T(8,128)(2,1)} %all-gather.20.cloned.1.call-done, bf16[12,512,2560]{2,1,0:T(8,128)(2,1)} %param.10), kind=kOutput, calls=%fused_computation.1 | convolution fusion | flops 33218887680 | bytes 55246848 | tf_op jit(solution)/shard_map/btd,btq->dq/dot_general | solution.py:437
  1060.5 34.5 %out_proj.4.rest_0_ = bf16[4,3,512,2560]{3,2,1,0:T(8,128)(2,1)} custom-call(bf16[4,512,2560]{2,1,0:T(8,128)(2,1)} %all-gather.16.cloned.1.call-done.o_ref, bf16[2560,2560]{1,0:T(8,128)(2,1)} %bitcast.114, bf16[4,3,512,2560]{3,2,1,0:T(8,128)(2,1)} %out_proj.3.rest_0_), custom_call_target="tpu_custom_call", output_to_operand_aliasing={{}: (2, {})} | custom-call | flops 26843545600 | bytes 34078720 | tf_op jit(solution)/shard_map/out_proj/pallas_call | solution.py:288
  1095.0 34.4 %out_proj.5 = bf16[4,3,512,2560]{3,2,1,0:T(8,128)(2,1)} custom-call(bf16[4,512,2560]{2,1,0:T(8,128)(2,1)} %all-gather.14.cloned.1.call-done.o_ref, bf16[2560,2560]{1,0:T(8,128)(2,1)} %bitcast.115, bf16[4,3,512,2560]{3,2,1,0:T(8,128)(2,1)} %out_proj.4.rest_0_), custom_call_target="tpu_custom_call", output_to_operand_aliasing={{}: (2, {})} | custom-call | flops 26843545600 | bytes 34078720 | tf_op jit(solution)/shard_map/out_proj/pallas_call | solution.py:288
  1129.4 46.4 %convolution_convert_fusion = bf16[12,512,2560]{2,1,0:T(8,128)(2,1)} fusion(bf16[12,512,1056]{1,2,0:T(8,128)(2,1)} %all-gather.20.cloned.1.call-done, bf16[2560,288]{0,1:T(8,128)(2,1)S(1)} %copy-done.34, bf16[2560,768]{0,1:T(8,128)(2,1)S(1)} %copy-done.8), kind=kOutput, calls=%fused_computation | convolution fusion | flops 33245429760 | bytes 49840128 | tf_op jit(solution)/shard_map/btq,dq->btd/dot_general | solution.py:441
  1175.9 8.8 add.135
  1184.7 10.2 slice_add_fusion
  1194.9 9.2 copy.128
  1204.1 4.7 slice_add_fusion.1
  (163 shorter events, 43.5 us)
Async XLA Ops:
  7.2 4.2 copy-start
  7.2 41.0 %all-gather.12.cloned.1.call-start = ((), (), s32[]{:S(2)}) async-start(), calls=%async_computation.5 | async-start | bytes 2949120 | tf_op jit(solution)/shard_map/all_gather | solution.py:325
  9.2 68.5 %all-gather.8.cloned.1.call-start = ((), (), s32[]{:S(2)}) async-start(), calls=%async_computation.3 | async-start | bytes 6635520 | tf_op jit(solution)/shard_map/all_gather | solution.py:325
  11.3 137.4 %all-gather.10.cloned.1.call-start = ((), (), s32[]{:S(2)}) async-start(), calls=%async_computation.4 | async-start | bytes 14745600 | tf_op jit(solution)/shard_map/all_gather | solution.py:325
  12.7 524.3 %reduce-scatter.6.cloned.1.call-start = ((), (), s32[]{:S(2)}) async-start(), calls=%async_computation.11 | async-start | bytes 2457600 | tf_op jit(solution)/shard_map/reduce_scatter | solution.py:415
  19.2 19.7 %copy-start.18 = (f32[512,16]{0,1:T(8,128)}, f32[512,16]{0,1:T(8,128)S(1)}, u32[]{:S(2)}) copy-start(f32[512,16]{0,1:T(8,128)S(1)} %get-tuple-element.111) | copy-start | bytes 98308
  19.2 20.6 %copy-start.16 = (f32[512,16]{0,1:T(8,128)}, f32[512,16]{0,1:T(8,128)S(1)}, u32[]{:S(2)}) copy-start(f32[512,16]{0,1:T(8,128)S(1)} %get-tuple-element.112) | copy-start | bytes 98308
  19.3 13.7 %copy-start.35 = (bf16[256]{0:T(256)(128)(2,1)S(1)}, bf16[256]{0:T(256)(128)(2,1)}, u32[]{:S(2)}) copy-start(bf16[256]{0:T(256)(128)(2,1)} %param.15) | copy-start | bytes 1540
  32.0 6.9 copy-start.2
  32.0 3.8 copy-start.33
  32.1 8.6 collective-permute-start.1
  33.0 2.5 copy-start.30
  35.5 8.1 collective-permute-start
  35.8 3.1 copy-start.28
  36.9 2.1 copy-start.26
  79.4 3.2 copy-start.13
  79.4 3.6 copy-start.11
  82.5 5.2 copy-start.9
  363.4 88.9 %copy-start.12 = (bf16[3,512,768]{1,2,0:T(8,128)(2,1)S(1)}, bf16[3,512,768]{1,2,0:T(8,128)(2,1)}, u32[]{:S(2)}) copy-start(bf16[3,512,768]{1,2,0:T(8,128)(2,1)} %fusion.9) | copy-start | bytes 7077892
  452.3 12.6 %copy-start.37 = (bf16[3,512,2560]{2,1,0:T(8,128)(2,1)S(1)}, bf16[3,512,2560]{2,1,0:T(8,128)(2,1)}, u32[]{:S(2)}) copy-start(bf16[3,512,2560]{2,1,0:T(8,128)(2,1)} %get-tuple-element.46) | copy-start | bytes 23592964
  458.1 13.1 %collective-permute-start.5 = (f32[1280,384]{1,0:T(8,128)}, f32[1280,384]{1,0:T(8,128)}, u32[]{:S(2)}, u32[]{:S(2)}) collective-permute-start(f32[1280,384]{1,0:T(8,128)} %convolution_bitcast_fusion.4), channel_id=1, source_target_pairs={{0,1},{1,0},{2,3},{3,2},{4,5},{5,4},{6,7},{7,6}} | collective-permute-start | bytes 5898248 | tf_op jit(solution)/shard_map/ppermute | solution.py:408
  471.2 6.7 collective-permute-start.4
  477.5 76.7 %reduce-scatter.4.cloned.1.call-start = ((), (), s32[]{:S(2)}) async-start(), calls=%async_computation.10 | async-start | bytes 4915200 | tf_op jit(solution)/shard_map/reduce_scatter | solution.py:414
  487.7 103.7 %reduce-scatter.8.cloned.1.call-start = ((), (), s32[]{:S(2)}) async-start(), calls=%async_computation.12 | async-start | bytes 3276800 | tf_op jit(solution)/shard_map/reduce_scatter | solution.py:416
  492.4 4.9 collective-permute-start.7
  501.2 192.7 %all-gather.18.cloned.1.call-start = ((), (), s32[]{:S(2)}) async-start(), calls=%async_computation.8 | async-start | bytes 13107200 | tf_op jit(solution)/shard_map/all_gather | solution.py:378
  502.0 293.1 %all-gather.16.cloned.1.call-start = ((), (), s32[]{:S(2)}) async-start(), calls=%async_computation.7 | async-start | bytes 13107200 | tf_op jit(solution)/shard_map/all_gather | solution.py:378
  502.7 393.5 %all-gather.14.cloned.1.call-start = ((), (), s32[]{:S(2)}) async-start(), calls=%async_computation.6 | async-start | bytes 13107200 | tf_op jit(solution)/shard_map/all_gather | solution.py:378
  503.4 514.5 %all-gather.20.cloned.1.call-start = ((), (), s32[]{:S(2)}) async-start(), calls=%async_computation.9 | async-start | bytes 16220160 | tf_op jit(solution)/shard_map/all_gather | solution.py:397
  507.5 2.6 copy-start.4
  510.1 2.1 copy-start.10
  510.4 12.9 %copy-start.3 = (bf16[3,512,1056]{1,2,0:T(8,128)(2,1)S(1)}, bf16[3,512,1056]{1,2,0:T(8,128)(2,1)}, u32[]{:S(2)}) copy-start(bf16[3,512,1056]{1,2,0:T(8,128)(2,1)} %copy-done.2) | copy-start | bytes 9732100
  510.4 12.9 %copy-start.14 = (bf16[40,32,768]{2,1,0:T(8,128)(2,1)S(1)}, bf16[40,32,768]{2,1,0:T(8,128)(2,1)}, u32[]{:S(2)}) copy-start(bf16[40,32,768]{2,1,0:T(8,128)(2,1)} %copy-done.13) | copy-start | bytes 5898244
  510.4 12.9 %copy-start.27 = (f32[3,512]{1,0:T(4,128)S(1)}, f32[3,512]{1,0:T(4,128)}, u32[]{:S(2)}) copy-start(f32[3,512]{1,0:T(4,128)} %copy-done.26) | copy-start | bytes 18436
  510.4 12.9 %copy-start.29 = (f32[768]{0:T(1024)S(1)}, f32[768]{0:T(1024)}, u32[]{:S(2)}) copy-start(f32[768]{0:T(1024)} %copy-done.28) | copy-start | bytes 9220
  510.4 12.9 %copy-start.36 = (bf16[3,512,1280]{2,1,0:T(8,128)(2,1)S(1)}, bf16[3,512,1280]{2,1,0:T(8,128)(2,1)}, u32[]{:S(2)}) copy-start(bf16[3,512,1280]{2,1,0:T(8,128)(2,1)} %get-tuple-element.47) | copy-start | bytes 11796484
  510.4 22.4 %collective-permute-start.2 = (f32[3,512,288]{1,2,0:T(8,128)S(1)}, f32[3,512,288]{1,2,0:T(8,128)S(1)}, u32[]{:S(2)}, u32[]{:S(2)}) collective-permute-start(f32[3,512,288]{1,2,0:T(8,128)S(1)} %broadcast_select_fusion), channel_id=1, source_target_pairs={{0,1},{1,0},{2,3},{3,2},{4,5},{5,4},{6,7},{7,6}} | collective-permute-start | bytes 5308424 | tf_op jit(solution)/shard_map/ppermute | solution.py:389
  523.3 8.3 copy-start.25
  531.7 1.9 copy-start.5
  556.8 61.6 %collective-permute-start.6 = (f32[10,96,384]{2,1,0:T(8,128)}, f32[10,96,384]{2,1,0:T(8,128)}, u32[]{:S(2)}, u32[]{:S(2)}) collective-permute-start(f32[10,96,384]{2,1,0:T(8,128)} %pad_maximum_fusion.4), channel_id=1, source_target_pairs={{0,1},{1,0},{2,3},{3,2},{4,5},{5,4},{6,7},{7,6}} | collective-permute-start | bytes 4423688 | tf_op jit(solution)/shard_map/ppermute | solution.py:420
  591.4 23.6 %collective-permute-start.8 = (f32[2,128,640]{2,1,0:T(8,128)}, f32[2,128,640]{2,1,0:T(8,128)S(1)}, u32[]{:S(2)}, u32[]{:S(2)}) collective-permute-start(f32[2,128,640]{2,1,0:T(8,128)} %reduce-scatter.8.cloned.1.call-done), channel_id=1, source_target_pairs={{0,1},{1,0},{2,3},{3,2},{4,5},{5,4},{6,7},{7,6}} | collective-permute-start | bytes 1966088 | tf_op jit(solution)/shard_map/ppermute | solution.py:420
  614.4 1.8 copy-start.32
  896.2 2.5 copy-start.7
  945.0 230.8 %collective-permute-start.9 = (f32[640,2560]{1,0:T(8,128)}, f32[640,2560]{1,0:T(8,128)}, u32[]{:S(2)}, u32[]{:S(2)}) collective-permute-start(f32[640,2560]{1,0:T(8,128)} %convolution_bitcast_fusion.1), channel_id=1, source_target_pairs={{0,1},{1,0},{2,3},{3,2},{4,5},{5,4},{6,7},{7,6}} | collective-permute-start | bytes 19660808 | tf_op jit(solution)/shard_map/ppermute | solution.py:435
  1060.5 124.2 %collective-permute-start.3 = (f32[2560,1056]{0,1:T(8,128)}, f32[2560,1056]{0,1:T(8,128)}, u32[]{:S(2)}, u32[]{:S(2)}) collective-permute-start(f32[2560,1056]{0,1:T(8,128)} %convolution_bitcast_fusion), channel_id=1, source_target_pairs={{0,1},{1,0},{2,3},{3,2},{4,5},{5,4},{6,7},{7,6}} | collective-permute-start | bytes 32440328 | tf_op jit(solution)/shard_map/ppermute | solution.py:438
  1095.0 34.4 %copy-start.8 = (bf16[2560,768]{0,1:T(8,128)(2,1)S(1)}, bf16[2560,768]{0,1:T(8,128)(2,1)}, u32[]{:S(2)}) copy-start(bf16[2560,768]{0,1:T(8,128)(2,1)} %copy.95) | copy-start | bytes 11796484
  1095.0 34.4 %copy-start.34 = (bf16[2560,288]{0,1:T(8,128)(2,1)S(1)}, bf16[2560,288]{0,1:T(8,128)(2,1)}, u32[]{:S(2)}) copy-start(bf16[2560,288]{0,1:T(8,128)(2,1)} %param.14) | copy-start | bytes 4423684
  1194.9 13.9 %copy-start.1 = (bf16[10,64,2560]{2,1,0:T(8,128)(2,1)S(1)}, bf16[10,64,2560]{2,1,0:T(8,128)(2,1)}, u32[]{:S(2)}) copy-start(bf16[10,64,2560]{2,1,0:T(8,128)(2,1)} %param.19) | copy-start | bytes 9830404
  (10 other events, 12.7 us)
Sparse Core Ops, SparseCore 0:
  10.4 27.1 all-gather.11
  39.9 37.7 all-gather.7
  80.1 68.4 all-gather.9
  477.6 28.4 reduce-scatter.5
  509.6 44.6 reduce-scatter.3
  557.6 33.7 reduce-scatter.7
  593.8 100.0 all-gather.17
  695.7 99.3 all-gather.15
  796.8 99.3 all-gather.13
  897.8 120.1 all-gather.19

commit v2 on v1

--- a/solution.py
+++ b/solution.py
@@ -6,6 +6,7 @@
 from jax.experimental import pallas as pl
 from jax.experimental.pallas import tpu as pltpu
 from jax.sharding import PartitionSpec as P
+
 
 EPS = 1e-6
 THETA = 10000.0
@@ -56,7 +57,6 @@
     (o_ref, dqn_ref, dqp_ref, dc_ref, dkp_ref, dwk_ref, dwv_ref,
      k_s, kt_s, v_s, vt_s, e_s, g_s, p_s, ds_s, qm_s, dom_s, dk_s, dv_s) = refs
     step = pl.program_id(0)
-    nkeys = ckv_ref.shape[1]
     qrows = qn_ref.shape[1]
     nope = 64
     lane128 = lax.broadcasted_iota(jnp.int32, (1, 128), 1)
@@ -196,6 +196,106 @@
     def _():
         dc_ref[0] += dc
         dkp_ref[0] += dkp
+
+
+def fwd_kernel(blk, scale, rank_ref, qn_ref, qp_ref, ckv_ref, ckvt_ref, kpe_ref, wuk_ref, wuv_ref, cos_ref, sin_ref, o_ref, k_s, vt_s, e_s, p_s, qm_s):
+    lane128 = lax.broadcasted_iota(jnp.int32, (1, 128), 1)
+    coef = scale * LOG2E
+    qrows = qn_ref.shape[1]
+    k_s[...] = mm(ckv_ref[0], wuk_ref[...], NT).astype(BF16)
+    vt_s[...] = mm(wuv_ref[...], ckvt_ref[0]).astype(BF16)
+    qpu = qp_ref[0].astype(F32)
+    swapped = jnp.where(lane128 % 32 < 16, pltpu.roll(qpu, 112, 1), pltpu.roll(qpu, 16, 1))
+    qpr = (qpu * cos_ref[...] + swapped * sin_ref[...]).astype(BF16)
+    zero = jnp.zeros((), BF16)
+    for h in range(4):
+        pair = h // 2
+        sel = (lane128 >= 64 * (h % 2)) & (lane128 < 64 * (h % 2) + 64)
+        qm_s[h, :, :128] = jnp.where(sel, qn_ref[0, :, pair * 128:pair * 128 + 128], zero)
+        selp = (lane128 >= 32 * h) & (lane128 < 32 * h + 32)
+        qm_s[h, :, 128:] = jnp.where(selp, qpr, zero)
+
+    def one_block(row0, nk):
+        rows = slice(row0, row0 + blk)
+        nch = nk // blk
+        for pair in range(2):
+            o_parts = []
+            for hh in range(2):
+                h = 2 * pair + hh
+                slot = h % 2
+                qm = qm_s[h, rows, :]
+                mx = None
+                for c in range(nch):
+                    ks = slice(c * blk, (c + 1) * blk)
+                    st = mm(jnp.concatenate([k_s[ks, pair * 128:pair * 128 + 128], kpe_ref[0, ks, :]], axis=1), qm, NT)
+                    if c == nch - 1:
+                        keep = lax.broadcasted_iota(jnp.int32, (blk, blk), 0) <= lax.broadcasted_iota(jnp.int32, (blk, blk), 1)
+                        st = jnp.where(keep, st, NEG_BIG)
+                    e_s[slot, ks, :] = st
+                    cm = jnp.max(st.reshape(blk // 8, 8, blk), axis=0)
+                    mx = cm if mx is None else jnp.maximum(mx, cm)
+                mx = jnp.max(mx, axis=0, keepdims=True)
+                tot = None
+                for c in range(nch):
+                    ks = slice(c * blk, (c + 1) * blk)
+                    e = jnp.exp2((e_s[slot, ks, :] - mx) * coef)
+                    e_s[slot, ks, :] = e
+                    ce = jnp.sum(e.reshape(blk // 8, 8, blk), axis=0)
+                    tot = ce if tot is None else tot + ce
+                inv = 1.0 / jnp.sum(tot, axis=0, keepdims=True)
+                for c in range(nch):
+                    ks = slice(c * blk, (c + 1) * blk)
+                    p_s[slot, ks, :] = (e_s[slot, ks, :] * inv).astype(BF16)
+                o_parts.append(mm(vt_s[h * 64:(h + 1) * 64, :nk], p_s[slot, :nk, :]))
+            o_ref[0, rows, pair * 128:pair * 128 + 128] = jnp.concatenate(o_parts, axis=0).T.astype(BF16)
+
+    rank = rank_ref[0]
+
+    @pl.when(rank == 0)
+    def _():
+        one_block(qrows - blk, 4 * blk)
+        one_block(0, blk)
+
+    @pl.when(rank == 1)
+    def _():
+        one_block(qrows - blk, 3 * blk)
+        one_block(0, 2 * blk)
+
+
+def attention_fwd(j, rank_arr, qn, qp, ckv, ckvt, kpe4, wuk, wuv, cos, sin, scale):
+    _, qrows, width = qn.shape
+    nkeys, latent = ckv.shape[1:]
+    groups = width // 256
+    blk = qrows // 2
+    row = lambda i: (j, 0, i)
+    whole = lambda i: (j, 0, 0)
+    pairs = 5 * 4 * groups * blk * blk
+    return pl.pallas_call(
+        functools.partial(fwd_kernel, blk, scale),
+        grid=(groups,),
+        in_specs=[
+            pl.BlockSpec(memory_space=pltpu.SMEM),
+            pl.BlockSpec((1, qrows, 256), row),
+            pl.BlockSpec((1, qrows, 128), row),
+            pl.BlockSpec((1, nkeys, latent), whole),
+            pl.BlockSpec((1, latent, nkeys), whole),
+            pl.BlockSpec((1, nkeys, 128), whole),
+            pl.BlockSpec((256, latent), lambda i: (i, 0)),
+            pl.BlockSpec((256, latent), lambda i: (i, 0)),
+            pl.BlockSpec((qrows, 128), lambda i: (0, 0)),
+            pl.BlockSpec((qrows, 128), lambda i: (0, 0)),
+        ],
+        out_specs=pl.BlockSpec((1, qrows, 256), lambda i: (0, 0, i)),
+        out_shape=jax.ShapeDtypeStruct((1, qrows, width), BF16),
+        scratch_shapes=[
+            pltpu.VMEM((nkeys, 256), BF16), pltpu.VMEM((256, nkeys), BF16),
+            pltpu.VMEM((2, nkeys, blk), F32), pltpu.VMEM((2, nkeys, blk), BF16),
+            pltpu.VMEM((4, qrows, 256), BF16),
+        ],
+        name="attn_fwd",
+        compiler_params=pltpu.CompilerParams(dimension_semantics=("arbitrary",), vmem_limit_bytes=40 * 1024 * 1024),
+        cost_estimate=pl.CostEstimate(flops=pairs * 2 * 2 * 256, bytes_accessed=10 * 1024 * 1024, transcendentals=pairs),
+    )(rank_arr, qn, qp, ckv, ckvt, kpe4, wuk, wuv, cos, sin)
 
 
 def attention(j, rank_arr, qn, qp, do, ckv, ckvt, kpe4, kpet, wuk, wuv, cos, sin, prev, scale):
@@ -372,11 +472,14 @@
 
         rank_arr = cp_rank.astype(jnp.int32).reshape(1)
         prev = None
-        o_all = []
-        for j in range(nb):
+        o_all = [None] * nb
+        o_first = attention_fwd(0, rank_arr, qn, qp, ckv_seq, ckvt_seq, kpe4, wuk, wuv, cos128, sin128, scale)
+        o_all[0] = lax.all_gather(o_first, 'tp', axis=0, tiled=True)
+        for j in (*range(1, nb), 0):
             res = attention(j, rank_arr, qn, qp, grad_o, ckv_seq, ckvt_seq, kpe4, kpet_seq, wuk, wuv, cos128, sin128, prev, scale)
-            o_all.append(lax.all_gather(res[0], 'tp', axis=0, tiled=True))
             prev = res[1:]
+            if j:
+                o_all[j] = lax.all_gather(res[0], 'tp', axis=0, tiled=True)
         dqn, dqp, dc_seq, dkp_seq, dwk, dwv = prev
 
         dkp_seq = dkp_seq[..., :32] + dkp_seq[..., 32:64] + dkp_seq[..., 64:96] + dkp_seq[..., 96:]
@@ -395,7 +498,10 @@
         grad_ckv_raw, grad_g_kv = norm_kv_pull(lat[..., :kv_lora])
         grad_raw = jnp.concatenate([grad_cq_raw, grad_ckv_raw, unrope(lat[..., kv_lora:], cos_tab, sin_tab)], axis=-1).astype(BF16)
         grad_raw = lax.all_gather(grad_raw, 'tp', axis=0, tiled=True)
-        grad_g = lax.psum(jnp.concatenate([grad_g_q, grad_g_kv]), ('tp', 'cp'))
+        part = jnp.concatenate([grad_g_q, grad_g_kv])
+        part = part + lax.ppermute(part, 'cp', swap_pairs)
+        parts = jnp.stack([part] + [lax.ppermute(part, 'tp', [(s, (s + k) % tp_size) for s in range(tp_size)]) for k in range(1, tp_size)])
+        grad_g = sum(lax.dynamic_index_in_dim(parts, (tp_rank - s) % tp_size, 0, keepdims=False) for s in range(tp_size))
 
         q_half = q_lora // 2
         cq_mine = lax.dynamic_slice_in_dim(c_q, cp_rank * q_half, q_half, 2)

time: 1220 us -> 1220 us (level)
  waiting for transfers between devices: 444 us -> 392 us
  Pallas kernels: 368 us -> 417 us
  blocking collectives: 23 us -> 0 us
  starting transfers between devices: 9.07 us -> 23.3 us
    pallas_call x0 -> x1, Pallas kernels: none -> 39.4 us  [attention_fwd(): pl.pallas_call(functools.partial(fwd_kernel, blk, scale), grid=(groups,),...]
    all_gather x3, waiting for transfers between devices: 268 us -> 231 us  [the longest x2 153 us: per_device(): o_all[j] = lax.all_gather(res[0], 'tp', axis=0, tiled=True)]
    reduce_scatter x1, waiting for transfers between devices: 34.6 us -> 0.01 us  [per_device(): dw_kv = lax.psum_scatter(dw_kv, 'tp', scatter_dimension=2, tiled=True)]
    all_gather x1, waiting for transfers between devices: 38.7 us -> 72.5 us  [per_device(): grad_raw = lax.all_gather(grad_raw, 'tp', axis=0, tiled=True)]
    psum x1 -> x0, blocking collectives: 23 us -> none  [per_device(): grad_g = lax.psum(jnp.concatenate([grad_g_q, grad_g_kv]), ('tp', 'cp'))]
    reduce_scatter x1, waiting for transfers between devices: 17.3 us -> 0.01 us  [per_device(): dwqn = lax.psum_scatter(dwqn, 'tp', scatter_dimension=0, tiled=True)]
    unnamed x78 -> x90, local copies, waits for them, and re-layouts: 22.2 us -> 28.2 us
  transfers between devices with their start and end apart: 20 -> 24, of which waited for: 10 -> 12; matrix products, arithmetic and copies ran while one was open for 23% -> 24% of each run, Pallas kernels for 8% -> 12%
where the time goes in v2:
time: 1220 us; the launch traced here: 1210 us
  Pallas kernels  417 us (34%)
  waiting for transfers between devices  392 us (32%)
  matrix products  225 us (18%)
  local copies, waits for them, and re-layouts  75.1 us (6%)
  other arithmetic  61.4 us (5%)
  starting transfers between devices  23.3 us (2%)
  between operations  15.3 us (1%)
    pallas_call x3, Pallas kernels, attention(): pl.pallas_call(functools.partial(attn_kernel, first, blk, scale), grid=(g...  274 us
    all_gather x2, waiting for transfers between devices, per_device(): o_all[j] = lax.all_gather(res[0], 'tp', axis=0, tiled=True)  153 us
    pallas_call x3, Pallas kernels, out_proj(): pl.pallas_call(out_kernel, grid=(dim // 256,), in_specs=in_specs, out_spe...  103 us
    all_gather x1, waiting for transfers between devices, per_device(): o_all[0] = lax.all_gather(o_first, 'tp', axis=0, tiled=True)  78.5 us
    all_gather x3, waiting for transfers between devices, gather_weight(): return lax.all_gather(half, ('tp', 'cp'), axis=0, tiled=True)  78.1 us
    all_gather x1, waiting for transfers between devices, per_device(): grad_raw = lax.all_gather(grad_raw, 'tp', axis=0, tiled=True)  72.5 us
    dot_general x1, matrix products, per_device(): jnp.einsum('btq,dq->btd', grad_raw, w_cat, preferred_element_type=F32)  46.4 us
    dot_general x1, matrix products, per_device(): jnp.einsum('btd,btq->dq', hidden, grad_raw, preferred_element_type=F32)  42.5 us
  transfers between devices with their start and end apart: 24, of which 12 were waited for; matrix products, arithmetic and copies ran while one was open for 24% of the time, Pallas kernels for 12%

profile of v2, /device:TPU:0, one launch (start us, length us, event | category | flops | bytes accessed | tf_op | source)
XLA Modules:
  0.0 1208.5 jit_solution(17694832223160114581)
XLA Ops:
  12.7 6.3 copy.100
  19.3 12.7 %fusion.14 = bf16[3,512,1056]{1,2,0:T(8,128)(2,1)S(1)} fusion(bf16[12,512,2560]{2,1,0:T(8,128)(2,1)} %param.10, s32[]{:T(128)S(6)} %select_n.152, bf16[2560,288]{0,1:T(8,128)(2,1)} %param.14, bf16[2560,768]{0,1:T(8,128)(2,1)} %copy.100), kind=kOutput, calls=%fused_computation.29 | convolution fusion | flops 8317157376 | bytes 16515076 | tf_op jit(solution)/shard_map/btd,dq->btq/dot_general | solution.py:446
  48.3 3.5 fusion.59
  51.8 26.4 %all-gather.8.cloned.1.call-done = bf16[40,96,768]{2,1,0:T(8,128)(2,1)} async-done(((bf16[5,96,768]{2,1,0:T(8,128)(2,1)}), bf16[40,96,768]{2,1,0:T(8,128)(2,1)}) %all-gather.8.cloned.1.call-update) | async-done | bytes 5898256 | tf_op jit(solution)/shard_map/all_gather | solution.py:425
  78.2 2.4 slice.159
  80.6 3.1 slice.160
  84.4 4.8 convolution_convert_fusion.2.refs_2_.qp_ref
  89.1 8.5 convolution_convert_fusion.1.refs_1_.qn_ref
  97.6 51.7 %all-gather.10.cloned.1.call-done = bf16[40,64,2560]{2,1,0:T(8,128)(2,1)} async-done(((bf16[5,64,2560]{2,1,0:T(8,128)(2,1)}), bf16[40,64,2560]{2,1,0:T(8,128)(2,1)}) %all-gather.10.cloned.1.call-update) | async-done | bytes 13107216 | tf_op jit(solution)/shard_map/all_gather | solution.py:425
  149.3 26.9 %fusion.4.refs_3_ = bf16[3,512,2560]{2,1,0:T(8,128)(2,1)} fusion(bf16[2560,2560,1]{1,0,2:T(8,128)(2,1)} %bitcast.122, bf16[12,512,2560]{2,1,0:T(8,128)(2,1)} %param.11, s32[]{:T(128)S(6)} %select_n.152), kind=kOutput, calls=%fused_computation.13 | convolution fusion | flops 20136591360 | bytes 28835844 | tf_op jit(solution)/shard_map/btd,fd->btf/dot_general | solution.py:471
  176.2 87.7 %attn_fwd_bwd.3 = (bf16[1,512,2560]{2,1,0:T(8,128)(2,1)}, bf16[3,512,2560]{2,1,0:T(8,128)(2,1)}, bf16[3,512,1280]{2,1,0:T(8,128)(2,1)}, f32[3,1024,256]{2,1,0:T(...) custom-call(s32[1]{0:T(128)} %bitcast.refs_0_.rank_ref, ...), custom_call_target="tpu_custom_call" | custom-call | flops 40265318400 | bytes 41943040 | tf_op jit(solution)/shard_map/attn_fwd_bwd/pallas_call | solution.py:357
  263.9 98.4 %attn_fwd_bwd.4 = (bf16[1,512,2560]{2,1,0:T(8,128)(2,1)}, bf16[3,512,2560]{2,1,0:T(8,128)(2,1)}, bf16[3,512,1280]{2,1,0:T(8,128)(2,1)}, f32[3,1024,256]{2,1,0:T(...) custom-call(s32[1]{0:T(128)} %bitcast.refs_0_.rank_ref, ...), custom_call_target="tpu_custom_call", output_to_operand_aliasing={{5}: (12, {}), {6}: (13, {}), {1}: (14, {}), {2}: (15, {}),... | custom-call | flops 40265318400 | bytes 41943040 | tf_op jit(solution)/shard_map/attn_fwd_bwd/pallas_call | solution.py:357
  362.4 88.2 %attn_fwd_bwd.5 = (bf16[1,512,2560]{2,1,0:T(8,128)(2,1)}, bf16[3,512,2560]{2,1,0:T(8,128)(2,1)}, bf16[3,512,1280]{2,1,0:T(8,128)(2,1)}, f32[3,1024,256]{2,1,0:T(...) custom-call(s32[1]{0:T(128)} %bitcast.refs_0_.rank_ref, ...), custom_call_target="tpu_custom_call", output_to_operand_aliasing={{5}: (12, {}), {6}: (13, {}), {1}: (14, {}), {2}: (15, {}),... | custom-call | flops 40265318400 | bytes 41943040 | tf_op jit(solution)/shard_map/attn_fwd_bwd/pallas_call | solution.py:357
  450.6 3.5 fusion.19
  454.1 7.0 collective-permute-start.11
  461.1 4.9 collective-permute-done.11
  466.0 4.0 fusion.21
  470.0 6.1 convolution_bitcast_fusion.4
  476.5 9.5 convolution_bitcast_fusion.2
  486.3 6.4 fusion.18
  493.2 10.0 fusion.17
  509.8 2.4 copy-done.9
  512.2 39.4 %attn_fwd.1 = bf16[1,512,2560]{2,1,0:T(8,128)(2,1)} custom-call(s32[1]{0:T(128)} %bitcast.refs_0_.rank_ref, bf16[3,512,2560]{2,1,0:T(8,128)(2,1)} %convolution_convert_fusion.1.refs_1_.qn_ref, bf16[3,512,1280]{2,1,0:T(8,128)(2,1)S(1)} %copy-done.9, bf16[3,1024,256]{2,1,0:T(8,128)(2,1)S(1)} %copy-done.2, bf16[3,256,1024]{2,1,0:T(8,128)(2,1)S(1)} %copy-done.3, ...), custom_call_target="tpu_custom_call" | custom-call | flops 13421772800 | bytes 10485760 | tf_op jit(solution)/shard_map/attn_fwd/pallas_call | solution.py:273
  553.2 2.6 copy.125
  555.9 4.2 copy.121
  561.9 6.8 collective-permute-start.2
  568.6 10.9 fusion.60
  579.6 8.3 fusion.10
  593.3 2.8 collective-permute-start.4
  604.2 2.6 pad_maximum_fusion.4
  607.3 78.5 %all-gather.18.cloned.1.call-done.o_ref = bf16[4,512,2560]{2,1,0:T(8,128)(2,1)} async-done(((bf16[1,512,2560]{2,1,0:T(8,128)(2,1)}), bf16[4,512,2560]{2,1,0:T(8,128)(2,1)}) %all-gather.18.cloned.1.call-update) | async-done | bytes 10485776 | tf_op jit(solution)/shard_map/all_gather | solution.py:477
  685.8 34.4 %out_proj.3.rest_0_ = bf16[4,3,512,2560]{3,2,1,0:T(8,128)(2,1)} custom-call(bf16[4,512,2560]{2,1,0:T(8,128)(2,1)} %all-gather.18.cloned.1.call-done.o_ref, bf16[2560,2560]{1,0:T(8,128)(2,1)} %bitcast.123), custom_call_target="tpu_custom_call" | custom-call | flops 26843545600 | bytes 34078720 | tf_op jit(solution)/shard_map/out_proj/pallas_call | solution.py:388
  727.6 2.9 broadcast_select_fusion.2
  732.3 54.7 %all-gather.14.cloned.1.call-done.o_ref = bf16[4,512,2560]{2,1,0:T(8,128)(2,1)} async-done(((bf16[1,512,2560]{2,1,0:T(8,128)(2,1)}), bf16[4,512,2560]{2,1,0:T(8,128)(2,1)}) %all-gather.14.cloned.1.call-update) | async-done | bytes 10485776 | tf_op jit(solution)/shard_map/all_gather | solution.py:482
  787.0 3.5 dynamic-slice_bitcast_fusion
  790.4 98.3 %all-gather.16.cloned.1.call-done.o_ref = bf16[4,512,2560]{2,1,0:T(8,128)(2,1)} async-done(((bf16[1,512,2560]{2,1,0:T(8,128)(2,1)}), bf16[4,512,2560]{2,1,0:T(8,128)(2,1)}) %all-gather.16.cloned.1.call-update) | async-done | bytes 10485776 | tf_op jit(solution)/shard_map/all_gather | solution.py:482
  891.3 3.9 pad_maximum_fusion
  895.2 11.2 copy.136
  906.4 31.7 %convolution_bitcast_fusion.1 = f32[640,2560]{1,0:T(8,128)} fusion(bf16[12,512,640]{1,2,0:T(8,128)(2,1)} %bitcast.100, bf16[12,512,2560]{2,1,0:T(8,128)(2,1)} %param.11), kind=kOutput, calls=%fused_computation.22 | convolution fusion | flops 20132659200 | bytes 45875200 | tf_op jit(solution)/shard_map/btf,btd->fd/dot_general | solution.py:540
  938.0 72.5 %all-gather.20.cloned.1.call-done = bf16[12,512,1056]{1,2,0:T(8,128)(2,1)} async-done(((bf16[3,512,1056]{1,2,0:T(8,128)(2,1)}), bf16[12,512,1056]{1,2,0:T(8,128)(2,1)}) %all-gather.20.cloned.1.call-update) | async-done | bytes 12976144 | tf_op jit(solution)/shard_map/all_gather | solution.py:500
  1010.5 42.5 %convolution_bitcast_fusion = f32[2560,1056]{0,1:T(8,128)} fusion(bf16[12,512,1056]{1,2,0:T(8,128)(2,1)} %all-gather.20.cloned.1.call-done, bf16[12,512,2560]{2,1,0:T(8,128)(2,1)} %param.10), kind=kOutput, calls=%fused_computation.1 | convolution fusion | flops 33218887680 | bytes 55246848 | tf_op jit(solution)/shard_map/btd,btq->dq/dot_general | solution.py:543
  1053.0 34.5 %out_proj.4.rest_0_ = bf16[4,3,512,2560]{3,2,1,0:T(8,128)(2,1)} custom-call(bf16[4,512,2560]{2,1,0:T(8,128)(2,1)} %all-gather.16.cloned.1.call-done.o_ref, bf16[2560,2560]{1,0:T(8,128)(2,1)} %bitcast.124, bf16[4,3,512,2560]{3,2,1,0:T(8,128)(2,1)} %out_proj.3.rest_0_), custom_call_target="tpu_custom_call", output_to_operand_aliasing={{}: (2, {})} | custom-call | flops 26843545600 | bytes 34078720 | tf_op jit(solution)/shard_map/out_proj/pallas_call | solution.py:388
  1087.4 34.4 %out_proj.5 = bf16[4,3,512,2560]{3,2,1,0:T(8,128)(2,1)} custom-call(bf16[4,512,2560]{2,1,0:T(8,128)(2,1)} %all-gather.14.cloned.1.call-done.o_ref, bf16[2560,2560]{1,0:T(8,128)(2,1)} %bitcast.125, bf16[4,3,512,2560]{3,2,1,0:T(8,128)(2,1)} %out_proj.4.rest_0_), custom_call_target="tpu_custom_call", output_to_operand_aliasing={{}: (2, {})} | custom-call | flops 26843545600 | bytes 34078720 | tf_op jit(solution)/shard_map/out_proj/pallas_call | solution.py:388
  1121.8 46.4 %convolution_convert_fusion = bf16[12,512,2560]{2,1,0:T(8,128)(2,1)} fusion(bf16[12,512,1056]{1,2,0:T(8,128)(2,1)} %all-gather.20.cloned.1.call-done, bf16[2560,288]{0,1:T(8,128)(2,1)S(1)} %copy-done.41, bf16[2560,768]{0,1:T(8,128)(2,1)S(1)} %copy-done.16), kind=kOutput, calls=%fused_computation | convolution fusion | flops 33245429760 | bytes 49840128 | tf_op jit(solution)/shard_map/btq,dq->btd/dot_general | solution.py:547
  1168.2 8.8 add.189
  1177.0 10.2 slice_add_fusion
  1187.3 9.2 copy.137
  1196.5 4.7 slice_add_fusion.1
  (187 shorter events, 59.1 us)
Async XLA Ops:
  7.2 4.2 copy-start
  7.2 41.1 %all-gather.12.cloned.1.call-start = ((), (), s32[]{:S(2)}) async-start(), calls=%async_computation.5 | async-start | bytes 2949120 | tf_op jit(solution)/shard_map/all_gather | solution.py:425
  9.2 69.1 %all-gather.8.cloned.1.call-start = ((), (), s32[]{:S(2)}) async-start(), calls=%async_computation.3 | async-start | bytes 6635520 | tf_op jit(solution)/shard_map/all_gather | solution.py:425
  11.3 138.0 %all-gather.10.cloned.1.call-start = ((), (), s32[]{:S(2)}) async-start(), calls=%async_computation.4 | async-start | bytes 14745600 | tf_op jit(solution)/shard_map/all_gather | solution.py:425
  12.7 591.5 %reduce-scatter.8.cloned.1.call-start = ((), (), s32[]{:S(2)}) async-start(), calls=%async_computation.12 | async-start | bytes 3276800 | tf_op jit(solution)/shard_map/reduce_scatter | solution.py:522
  19.2 19.6 %copy-start.26 = (f32[512,16]{0,1:T(8,128)}, f32[512,16]{0,1:T(8,128)S(1)}, u32[]{:S(2)}) copy-start(f32[512,16]{0,1:T(8,128)S(1)} %get-tuple-element.109) | copy-start | bytes 98308
  19.2 20.5 %copy-start.24 = (f32[512,16]{0,1:T(8,128)}, f32[512,16]{0,1:T(8,128)S(1)}, u32[]{:S(2)}) copy-start(f32[512,16]{0,1:T(8,128)S(1)} %get-tuple-element.110) | copy-start | bytes 98308
  19.3 13.7 %copy-start.42 = (bf16[256]{0:T(256)(128)(2,1)S(1)}, bf16[256]{0:T(256)(128)(2,1)}, u32[]{:S(2)}) copy-start(bf16[256]{0:T(256)(128)(2,1)} %param.15) | copy-start | bytes 1540
  32.0 6.9 copy-start.10
  32.0 3.8 copy-start.40
  32.1 8.5 collective-permute-start.1
  35.5 8.0 collective-permute-start
  35.8 3.1 copy-start.36
  80.6 8.5 copy-start.17
  80.6 3.7 copy-start.19
  83.8 5.4 copy-start.21
  450.6 15.4 %copy-start.14 = (f32[256,2560]{1,0:T(8,128)S(1)}, f32[256,2560]{1,0:T(8,128)}, u32[]{:S(2)}) copy-start(f32[256,2560]{1,0:T(8,128)} %get-tuple-element.48) | copy-start | bytes 7864324
  454.1 11.9 collective-permute-start.11
  470.0 134.2 %reduce-scatter.6.cloned.1.call-start = ((), (), s32[]{:S(2)}) async-start(), calls=%async_computation.11 | async-start | bytes 2457600 | tf_op jit(solution)/shard_map/reduce_scatter | solution.py:521
  470.0 6.5 copy-start.20
  476.2 10.1 collective-permute-start.9
  486.1 7.1 collective-permute-start.8
  492.7 111.6 %reduce-scatter.4.cloned.1.call-start = ((), (), s32[]{:S(2)}) async-start(), calls=%async_computation.10 | async-start | bytes 4915200 | tf_op jit(solution)/shard_map/reduce_scatter | solution.py:520
  503.2 182.6 %all-gather.18.cloned.1.call-start = ((), (), s32[]{:S(2)}) async-start(), calls=%async_computation.8 | async-start | bytes 13107200 | tf_op jit(solution)/shard_map/all_gather | solution.py:477
  551.7 235.3 %all-gather.14.cloned.1.call-start = ((), (), s32[]{:S(2)}) async-start(), calls=%async_computation.6 | async-start | bytes 13107200 | tf_op jit(solution)/shard_map/all_gather | solution.py:482
  552.4 336.3 %all-gather.16.cloned.1.call-start = ((), (), s32[]{:S(2)}) async-start(), calls=%async_computation.7 | async-start | bytes 13107200 | tf_op jit(solution)/shard_map/all_gather | solution.py:482
  553.2 457.3 %all-gather.20.cloned.1.call-start = ((), (), s32[]{:S(2)}) async-start(), calls=%async_computation.9 | async-start | bytes 16220160 | tf_op jit(solution)/shard_map/all_gather | solution.py:500
  555.9 5.7 copy-start.12
  561.6 7.1 copy-start.18
  561.8 17.7 %copy-start.11 = (bf16[3,512,1056]{1,2,0:T(8,128)(2,1)S(1)}, bf16[3,512,1056]{1,2,0:T(8,128)(2,1)}, u32[]{:S(2)}) copy-start(bf16[3,512,1056]{1,2,0:T(8,128)(2,1)} %copy-done.10) | copy-start | bytes 9732100
  561.8 17.7 %copy-start.22 = (bf16[40,32,768]{2,1,0:T(8,128)(2,1)S(1)}, bf16[40,32,768]{2,1,0:T(8,128)(2,1)}, u32[]{:S(2)}) copy-start(bf16[40,32,768]{2,1,0:T(8,128)(2,1)} %copy-done.21) | copy-start | bytes 5898244
  561.8 17.7 %copy-start.35 = (f32[3,512]{1,0:T(4,128)S(1)}, f32[3,512]{1,0:T(4,128)}, u32[]{:S(2)}) copy-start(f32[3,512]{1,0:T(4,128)} %copy-done.34) | copy-start | bytes 18436
  561.8 17.7 %copy-start.37 = (f32[768]{0:T(1024)S(1)}, f32[768]{0:T(1024)}, u32[]{:S(2)}) copy-start(f32[768]{0:T(1024)} %copy-done.36) | copy-start | bytes 9220
  561.8 17.7 %copy-start.43 = (bf16[3,512,1280]{2,1,0:T(8,128)(2,1)S(1)}, bf16[3,512,1280]{2,1,0:T(8,128)(2,1)}, u32[]{:S(2)}) copy-start(bf16[3,512,1280]{2,1,0:T(8,128)(2,1)} %get-tuple-element.45) | copy-start | bytes 11796484
  561.9 27.3 %collective-permute-start.2 = (f32[3,512,288]{1,2,0:T(8,128)S(1)}, f32[3,512,288]{1,2,0:T(8,128)S(1)}, u32[]{:S(2)}, u32[]{:S(2)}) collective-permute-start(f32[3,512,288]{1,2,0:T(8,128)S(1)} %broadcast_select_fusion), channel_id=1, source_target_pairs={{0,1},{1,0},{2,3},{3,2},{4,5},{5,4},{6,7},{7,6}} | collective-permute-start | bytes 5308424 | tf_op jit(solution)/shard_map/ppermute | solution.py:492
  579.6 8.3 copy-start.33
  593.3 3.6 collective-permute-start.4
  596.9 4.7 collective-permute-start.5
  598.3 3.8 collective-permute-start.6
  599.2 3.8 collective-permute-start.7
  604.2 118.0 %collective-permute-start.12 = (f32[2,128,640]{2,1,0:T(8,128)}, f32[2,128,640]{2,1,0:T(8,128)}, u32[]{:S(2)}, u32[]{:S(2)}) collective-permute-start(f32[2,128,640]{2,1,0:T(8,128)} %reduce-scatter.8.cloned.1.call-done), channel_id=1, source_target_pairs={{0,1},{1,0},{2,3},{3,2},{4,5},{5,4},{6,7},{7,6}} | collective-permute-start | bytes 1966088 | tf_op jit(solution)/shard_map/ppermute | solution.py:526
  606.8 120.8 %collective-permute-start.10 = (f32[10,96,384]{2,1,0:T(8,128)}, f32[10,96,384]{2,1,0:T(8,128)}, u32[]{:S(2)}, u32[]{:S(2)}) collective-permute-start(f32[10,96,384]{2,1,0:T(8,128)} %pad_maximum_fusion.4), channel_id=1, source_target_pairs={{0,1},{1,0},{2,3},{3,2},{4,5},{5,4},{6,7},{7,6}} | collective-permute-start | bytes 4423688 | tf_op jit(solution)/shard_map/ppermute | solution.py:526
  888.7 2.5 copy-start.15
  938.0 230.2 %collective-permute-start.13 = (f32[640,2560]{1,0:T(8,128)}, f32[640,2560]{1,0:T(8,128)}, u32[]{:S(2)}, u32[]{:S(2)}) collective-permute-start(f32[640,2560]{1,0:T(8,128)} %convolution_bitcast_fusion.1), channel_id=1, source_target_pairs={{0,1},{1,0},{2,3},{3,2},{4,5},{5,4},{6,7},{7,6}} | collective-permute-start | bytes 19660808 | tf_op jit(solution)/shard_map/ppermute | solution.py:541
  1053.0 124.0 %collective-permute-start.3 = (f32[2560,1056]{0,1:T(8,128)}, f32[2560,1056]{0,1:T(8,128)}, u32[]{:S(2)}, u32[]{:S(2)}) collective-permute-start(f32[2560,1056]{0,1:T(8,128)} %convolution_bitcast_fusion), channel_id=1, source_target_pairs={{0,1},{1,0},{2,3},{3,2},{4,5},{5,4},{6,7},{7,6}} | collective-permute-start | bytes 32440328 | tf_op jit(solution)/shard_map/ppermute | solution.py:544
  1087.4 34.4 %copy-start.16 = (bf16[2560,768]{0,1:T(8,128)(2,1)S(1)}, bf16[2560,768]{0,1:T(8,128)(2,1)}, u32[]{:S(2)}) copy-start(bf16[2560,768]{0,1:T(8,128)(2,1)} %copy.100) | copy-start | bytes 11796484
  1087.4 34.4 %copy-start.41 = (bf16[2560,288]{0,1:T(8,128)(2,1)S(1)}, bf16[2560,288]{0,1:T(8,128)(2,1)}, u32[]{:S(2)}) copy-start(bf16[2560,288]{0,1:T(8,128)(2,1)} %param.14) | copy-start | bytes 4423684
  1187.2 13.9 %copy-start.1 = (bf16[10,64,2560]{2,1,0:T(8,128)(2,1)S(1)}, bf16[10,64,2560]{2,1,0:T(8,128)(2,1)}, u32[]{:S(2)}) copy-start(bf16[10,64,2560]{2,1,0:T(8,128)(2,1)} %param.19) | copy-start | bytes 9830404
  (20 other events, 30.6 us)
Sparse Core Ops, SparseCore 0:
  10.4 27.3 all-gather.11
  40.2 37.9 all-gather.7
  80.6 68.6 all-gather.9
  470.1 33.9 reduce-scatter.7
  507.0 28.5 reduce-scatter.5
  539.0 44.8 reduce-scatter.3
  586.2 99.5 all-gather.17
  687.6 99.3 all-gather.13
  789.3 99.3 all-gather.15
  890.4 120.0 all-gather.19

commit v3 on v1

v3 whole, which is shorter than its diff:
```python
import functools

import jax
import jax.numpy as jnp
from jax import lax
from jax.experimental import pallas as pl
from jax.experimental.pallas import tpu as pltpu
from jax.sharding import PartitionSpec as P


EPS = 1e-6
THETA = 10000.0
NEG_BIG = -1e30
LOG2E = 1.4426950408889634
F32 = jnp.float32
BF16 = jnp.bfloat16
LANES = 128
GROUP = 4
VMEM_LIMIT = 56 * 1024 * 1024

NN = (((1,), (0,)), ((), ()))
NT = (((1,), (1,)), ((), ()))


def mm(a, b, dims=NN):
    return lax.dot_general(a, b, dims, preferred_element_type=F32)


def rope_tables(positions, rope_dim):
    inv_freq = 1.0 / (THETA ** (jnp.arange(rope_dim // 2, dtype=F32) * 2.0 / rope_dim))
    angles = positions.astype(F32)[:, None] * inv_freq[None, :]
    return jnp.cos(angles), jnp.sin(angles)


def apply_rope(values, cos_tab, sin_tab):
    half_dim = values.shape[-1] // 2
    lead_half = values[..., :half_dim]
    tail_half = values[..., half_dim:]
    return jnp.concatenate([lead_half * cos_tab - tail_half * sin_tab, tail_half * cos_tab + lead_half * sin_tab], axis=-1)


def unrope(grad_vals, cos_tab, sin_tab):
    half_dim = grad_vals.shape[-1] // 2
    lead_half = grad_vals[..., :half_dim]
    tail_half = grad_vals[..., half_dim:]
    return jnp.concatenate([lead_half * cos_tab + tail_half * sin_tab, tail_half * cos_tab - lead_half * sin_tab], axis=-1)


def norm_f32(raw_vals, gain_vec):
    inv_rms = lax.rsqrt(jnp.mean(raw_vals * raw_vals, axis=-1, keepdims=True) + EPS)
    return raw_vals * inv_rms * gain_vec


def attn_kernel(grad, first, scale, *refs):
    it = iter(refs)

    def take(n):
        return [next(it) for _ in range(n)]

    rank_ref, qn_ref, qp_ref, ckv_ref, ckvt_ref, kpe_ref, wuk_ref, wuv_ref, cos_ref, sin_ref = take(10)
    if grad:
        do_ref, kpet_ref = take(2)
        if not first:
            dwk_in, dwv_in = take(6)[:2]
    o_ref = next(it)
    if grad:
        dqn_ref, dqp_ref, dc_ref, dkp_ref, dwk_ref, dwv_ref = take(6)
    k_s, vt_s, e_s, p_s, qm_s = take(5)
    if grad:
        kt_s, v_s, g_s, ds_s, dom_s, dk_s, dv_s = take(7)

    qrows = qn_ref.shape[1]
    blk = qrows // 2
    sub = blk // 2
    half = LANES // 2
    quarter = LANES // 4
    lane = lax.broadcasted_iota(jnp.int32, (1, LANES), 1)
    lane2 = lax.broadcasted_iota(jnp.int32, (1, 2 * LANES), 1)
    coef = scale * LOG2E

    ckv = ckv_ref[0]
    ckvt = ckvt_ref[0]
    wuk = wuk_ref[...]
    wuv = wuv_ref[...]
    k_s[...] = mm(ckv, wuk, NT).astype(BF16)
    vt_s[...] = mm(wuv, ckvt).astype(BF16)
    if grad:
        kt_s[...] = mm(wuk, ckvt).astype(BF16)
        v_s[...] = mm(ckv, wuv, NT).astype(BF16)

    def swap(u):
        shift = quarter // 2
        return jnp.where(lane % quarter < shift, pltpu.roll(u, LANES - shift, 1), pltpu.roll(u, shift, 1))

    qpu = qp_ref[0].astype(F32)
    cos = cos_ref[...]
    sin = sin_ref[...]
    qpr = (qpu * cos + swap(qpu) * sin).astype(BF16)
    zero = jnp.zeros((), BF16)

    def pair_lanes(h):
        return slice(h // 2 * LANES, h // 2 * LANES + LANES)

    for h in range(GROUP):
        qm_s[h, :, :LANES] = jnp.where(lane // half == h % 2, qn_ref[0, :, pair_lanes(h)], zero)
        qm_s[h, :, LANES:] = jnp.where(lane // quarter == h, qpr, zero)
        if grad:
            dom_s[h] = jnp.where(lane2 // half == h, do_ref[0], zero)

    def fold(x, op):
        return op(x.reshape(x.shape[0] // 8, 8, x.shape[1]), axis=0)

    def run(lo, hi):
        units = [(qrows - blk, hi * blk, h) for h in range(GROUP)] + [(0, lo * blk, h) for h in range(GROUP)]
        o_t = {}
        dq_t = {}

        def scores(i):
            row0, nk, h = units[i]
            kop = jnp.concatenate([k_s[:nk, pair_lanes(h)], kpe_ref[0, :nk, :]], axis=1)
            e_s[i % 2, :nk, :] = mm(kop, qm_s[h, row0:row0 + blk, :], NT)

        def dprobs(i):
            row0, nk, h = units[i]
            g_s[i % 2, :nk, :] = mm(v_s[:nk, :], dom_s[h, row0:row0 + blk, :], NT)

        def vector_passes(i):
            _, nk, h = units[i]
            slot = i % 2
            st = {}
            cols = slice(h * blk, h * blk + blk)

            def put(key, val, op):
                st[key] = op(st[key], val) if key in st else val

            def top(c):
                x = e_s[slot, c:c + sub, :]
                if c >= nk - blk:
                    key = lax.broadcasted_iota(jnp.int32, (sub, blk), 0) + (c - nk + blk)
                    x = jnp.where(key <= lax.broadcasted_iota(jnp.int32, (sub, blk), 1), x, NEG_BIG)
                    e_s[slot, c:c + sub, :] = x
                put('m', fold(x, jnp.max), jnp.maximum)

            def expo(c):
                if c == 0:
                    st['max'] = jnp.max(st['m'], axis=0, keepdims=True)
                e = jnp.exp2((e_s[slot, c:c + sub, :] - st['max']) * coef)
                e_s[slot, c:c + sub, :] = e
                put('l', fold(e, jnp.sum), jnp.add)
                if grad:
                    put('d', fold(e * g_s[slot, c:c + sub, :], jnp.sum), jnp.add)

            def probs(c):
                if c == 0:
                    st['inv'] = 1.0 / jnp.sum(st['l'], axis=0, keepdims=True)
                    if grad:
                        st['dot'] = jnp.sum(st['d'], axis=0, keepdims=True) * st['inv']
                p = e_s[slot, c:c + sub, :] * st['inv']
                p_s[c:c + sub, cols] = p.astype(BF16)
                if grad:
                    ds_s[c:c + sub, cols] = (p * (g_s[slot, c:c + sub, :] - st['dot'])).astype(BF16)

            return [functools.partial(f, c) for f in (top, expo, probs) for c in range(0, nk, sub)]

        def out(i):
            row0, nk, h = units[i]
            o_t[h] = mm(vt_s[h * half:h * half + half, :nk], p_s[:nk, h * blk:h * blk + blk])
            if h % 2:
                o_ref[0, row0:row0 + blk, pair_lanes(h)] = jnp.concatenate([o_t[h - 1], o_t[h]], axis=0).T.astype(BF16)

        def dquery(i):
            row0, nk, h = units[i]
            kop_t = jnp.concatenate([kt_s[h * half:h * half + half, :nk], kpet_ref[0, :, :nk]], axis=0)
            dq_t[h] = mm(kop_t, ds_s[:nk, h * blk:h * blk + blk])
            rows = slice(row0, row0 + blk)
            if h % 2:
                dqn_ref[0, rows, pair_lanes(h)] = (jnp.concatenate([dq_t[h - 1][:half], dq_t[h][:half]], axis=0).T * scale).astype(BF16)
            if h == GROUP - 1:
                dqp = jnp.concatenate([dq_t[g][half:] for g in range(GROUP)], axis=0).T * scale
                dqp_ref[0, rows, :] = (dqp * cos[rows] - swap(dqp) * sin[rows]).astype(BF16)

        def dkeys(i, dst, lhs, rhs):
            row0, nk, h = units[i]
            cols = slice((h - 1) * blk, (h + 1) * blk)
            val = mm(lhs[:nk, cols], jnp.concatenate([rhs[h - 1, row0:row0 + blk, :], rhs[h, row0:row0 + blk, :]], axis=0))
            if row0:
                dst[h // 2, :nk, :] = val
                if nk < dst.shape[1]:
                    dst[h // 2, nk:, :] = jnp.zeros((dst.shape[1] - nk, dst.shape[2]), F32)
            else:
                dst[h // 2, :nk, :] += val

        def before(i):
            return [functools.partial(scores, i)] + ([functools.partial(dprobs, i)] if grad else [])

        def after(i):
            work = [functools.partial(out, i)]
            if grad:
                work.append(functools.partial(dquery, i))
                if units[i][-1] % 2:
                    work.append(functools.partial(dkeys, i, dv_s, p_s, dom_s))
                    work.append(functools.partial(dkeys, i, dk_s, ds_s, qm_s))
            return work

        for f in before(0):
            f()
        for i in range(len(units)):
            vec = vector_passes(i)
            mat = (before(i + 1) if i + 1 < len(units) else []) + (after(i - 1) if i else [])
            for c, f in enumerate(vec):
                for g in mat[c * len(mat) // len(vec):(c + 1) * len(mat) // len(vec)]:
                    g()
                f()
        for f in after(len(units) - 1):
            f()

    rank = rank_ref[0]

    @pl.when(rank == 0)
    def _():
        run(1, 4)

    @pl.when(rank == 1)
    def _():
        run(2, 3)

    if grad:
        dkb = (jnp.concatenate([dk_s[0, :, :LANES], dk_s[1, :, :LANES]], axis=1) * scale).astype(BF16)
        dvb = (dv_s[0] + dv_s[1]).astype(BF16)
        dkp = (dk_s[0, :, LANES:] + dk_s[1, :, LANES:]) * scale
        dc = mm(dkb, wuk) + mm(dvb, wuv)
        dwk = mm(ckvt, dkb)
        dwv = mm(ckvt, dvb)
        dwk_ref[...] = dwk if first else dwk_in[...] + dwk
        dwv_ref[...] = dwv if first else dwv_in[...] + dwv
        step = pl.program_id(0)

        @pl.when(step == 0)
        def _():
            dc_ref[0] = dc
            dkp_ref[0] = dkp

        @pl.when(step > 0)
        def _():
            dc_ref[0] += dc
            dkp_ref[0] += dkp


def attention(j, grad_args, prev, scale, rank_arr, qn, qp, ckv, ckvt, kpe4, wuk, wuv, cos, sin):
    nb, qrows, width = qn.shape
    nkeys, latent = ckv.shape[1:]
    step = GROUP * LANES // 2
    groups = width // step
    blk = qrows // 2
    grad = grad_args is not None
    first = prev is None

    def row(cols, at=j):
        return pl.BlockSpec((1, qrows, cols), lambda i: (at, 0, i))

    def whole(*shape):
        return pl.BlockSpec((1, *shape), lambda i: (j, 0, 0))

    weight = pl.BlockSpec((step, latent), lambda i: (i, 0))
    table = pl.BlockSpec((qrows, LANES), lambda i: (0, 0))
    dweight = pl.BlockSpec((latent, step), lambda i: (0, i))
    in_specs = [pl.BlockSpec(memory_space=pltpu.SMEM), row(step), row(LANES), whole(nkeys, latent), whole(latent, nkeys), whole(nkeys, LANES), weight, weight, table, table]
    args = [rank_arr, qn, qp, ckv, ckvt, kpe4, wuk, wuv, cos, sin]
    out_specs = [row(step, 0)]
    out_shape = [jax.ShapeDtypeStruct((1, qrows, width), BF16)]
    scratch = [
        pltpu.VMEM((nkeys, step), BF16), pltpu.VMEM((step, nkeys), BF16), pltpu.VMEM((2, nkeys, blk), F32),
        pltpu.VMEM((nkeys, GROUP * blk), BF16), pltpu.VMEM((GROUP, qrows, step), BF16),
    ]
    aliases = {}
    if grad:
        in_specs += [row(step), whole(LANES // 4, nkeys)]
        args += grad_args
        if not first:
            dqn, dqp, dc, dkp, dwk, dwv = prev
            base = len(args)
            in_specs += [dweight] * 2 + [pl.BlockSpec(memory_space=pl.ANY)] * 4
            args += [dwk, dwv, dqn, dqp, dc, dkp]
            aliases = {base + i: o for i, o in enumerate((5, 6, 1, 2, 3, 4))}
        out_specs += [row(step), row(LANES), whole(nkeys, latent), whole(nkeys, LANES), dweight, dweight]
        out_shape += [
            jax.ShapeDtypeStruct((nb, qrows, width), BF16), jax.ShapeDtypeStruct((nb, qrows, width // 2), BF16),
            jax.ShapeDtypeStruct((nb, nkeys, latent), F32), jax.ShapeDtypeStruct((nb, nkeys, LANES), F32),
            jax.ShapeDtypeStruct((latent, width), F32), jax.ShapeDtypeStruct((latent, width), F32),
        ]
        scratch += [
            pltpu.VMEM((step, nkeys), BF16), pltpu.VMEM((nkeys, step), BF16), pltpu.VMEM((2, nkeys, blk), F32),
            pltpu.VMEM((nkeys, GROUP * blk), BF16), pltpu.VMEM((GROUP, qrows, step), BF16),
            pltpu.VMEM((2, nkeys, step), F32), pltpu.VMEM((2, nkeys, step), F32),
        ]
    pairs = 5 * GROUP * groups * blk * blk
    return pl.pallas_call(
        functools.partial(attn_kernel, grad, first, scale),
        grid=(groups,),
        in_specs=in_specs,
        out_specs=out_specs,
        out_shape=out_shape,
        scratch_shapes=scratch,
        input_output_aliases=aliases,
        name="attn_fwd_bwd" if grad else "attn_fwd",
        compiler_params=pltpu.CompilerParams(dimension_semantics=("arbitrary",), vmem_limit_bytes=VMEM_LIMIT),
        cost_estimate=pl.CostEstimate(flops=pairs * step * (12 if grad else 4), bytes_accessed=20 * nb * qrows * width, transcendentals=pairs),
    )(*args)


def out_kernel(o_ref, w_ref, *rest):
    y_ref = rest[-1]
    w = w_ref[...]
    for t in range(o_ref.shape[0]):
        y_ref[t, 0] = mm(o_ref[t], w).astype(BF16)


def out_proj(j, nb, o_all, w_o, prev):
    tp, rows, width = o_all.shape
    dim = w_o.shape[1]
    in_specs = [pl.BlockSpec((tp, rows, width), lambda i: (0, 0, 0)), pl.BlockSpec((width, 256), lambda i: (0, i))]
    args = [o_all, w_o]
    aliases = {}
    if prev is not None:
        in_specs.append(pl.BlockSpec(memory_space=pl.ANY))
        args.append(prev)
        aliases = {2: 0}
    return pl.pallas_call(
        out_kernel,
        grid=(dim // 256,),
        in_specs=in_specs,
        out_specs=pl.BlockSpec((tp, 1, rows, 256), lambda i: (0, j, 0, i)),
        out_shape=jax.ShapeDtypeStruct((tp, nb, rows, dim), BF16),
        input_output_aliases=aliases,
        name="out_proj",
        compiler_params=pltpu.CompilerParams(dimension_semantics=("arbitrary",), vmem_limit_bytes=VMEM_LIMIT),
        cost_estimate=pl.CostEstimate(flops=2 * tp * rows * width * dim, bytes_accessed=2 * (2 * tp * rows * width + width * dim), transcendentals=0),
    )(*args)


def dwo_kernel(tp, col_ref, *refs):
    *o_refs, dy_ref, out_ref, ot_s = refs
    step = pl.program_id(0)
    per = o_refs[0].shape[0]
    rows = o_refs[0].shape[1]
    for j, o_ref in enumerate(o_refs):
        @pl.when(step // (tp // per) == j)
        def _():
            for t in range(per):
                ot_s[:, t * rows:(t + 1) * rows] = o_ref[t].astype(F32).T.astype(BF16)

    tile = 4 * LANES
    for n in range(0, out_ref.shape[1], tile):
        cols = slice(n, n + tile)
        val = mm(ot_s[...], jnp.concatenate([dy_ref[t, 0, :, cols] for t in range(per)], axis=0))

        @pl.when(step == 0)
        def _():
            out_ref[:, cols] = val

        @pl.when(step > 0)
        def _():
            out_ref[:, cols] += val


def grad_wo(o_all, dy, cols, col_arr):
    tp, rows, _ = o_all[0].shape
    nb = len(o_all)
    dim = dy.shape[-1]
    per = 2
    turns = tp // per

    def o_spec(j):
        return pl.BlockSpec((per, rows, cols), lambda i, col: (jnp.clip(i - j * turns, 0, turns - 1), 0, col[0]))

    return pl.pallas_call(
        functools.partial(dwo_kernel, tp),
        grid_spec=pltpu.PrefetchScalarGridSpec(
            num_scalar_prefetch=1,
            grid=(nb * turns,),
            in_specs=[o_spec(j) for j in range(nb)] + [pl.BlockSpec((per, 1, rows, dim), lambda i, col: (i % turns, i // turns, 0, 0))],
            out_specs=pl.BlockSpec((cols, dim), lambda i, col: (0, 0)),
            scratch_shapes=[pltpu.VMEM((cols, per * rows), BF16)],
        ),
        out_shape=jax.ShapeDtypeStruct((cols, dim), F32),
        name="grad_wo",
        compiler_params=pltpu.CompilerParams(dimension_semantics=("arbitrary",), vmem_limit_bytes=VMEM_LIMIT),
        cost_estimate=pl.CostEstimate(flops=2 * nb * tp * rows * cols * dim, bytes_accessed=2 * nb * tp * rows * (cols + dim), transcendentals=0),
    )(col_arr, *o_all, dy.reshape(tp, nb, rows, dim))


def join_kernel(a_ref, b_ref, q_ref, kv_ref):
    split = q_ref.shape[1]
    q_ref[...] = (a_ref[:split, :] + b_ref[:split, :]).T
    kv_ref[...] = (a_ref[split:, :] + b_ref[split:, :]).T


def join_cp(a, b, split):
    wide, dim = a.shape
    tile = 2 * LANES
    part = pl.BlockSpec((wide, tile), lambda i: (0, i))
    return pl.pallas_call(
        join_kernel,
        grid=(dim // tile,),
        in_specs=[part, part],
        out_specs=[pl.BlockSpec((tile, split), lambda i: (i, 0)), pl.BlockSpec((tile, wide - split), lambda i: (i, 0))],
        out_shape=[jax.ShapeDtypeStruct((dim, split), F32), jax.ShapeDtypeStruct((dim, wide - split), F32)],
        name="join_cp",
        compiler_params=pltpu.CompilerParams(dimension_semantics=("arbitrary",), vmem_limit_bytes=VMEM_LIMIT),
        cost_estimate=pl.CostEstimate(flops=wide * dim, bytes_accessed=12 * wide * dim, transcendentals=0),
    )(a, b)


def solution(mesh):
    cp_size = mesh.shape['cp']
    tp_size = mesh.shape['tp']
    swap_pairs = [(0, 1), (1, 0)]

    def per_device(hidden, grad_out, w_dq, g_q, w_dkv, g_kv, w_uq, w_uk, w_uv, w_o):
        cp_rank = lax.axis_index('cp')
        tp_rank = lax.axis_index('tp')
        n_batch, seq_local, dim = hidden.shape
        nb = n_batch // tp_size
        q_lora = w_dq.shape[1]
        kv_lora = g_kv.shape[0]
        nope = w_uk.shape[2]
        qk_dim = w_uq.shape[2]
        rope_dim = qk_dim - nope
        heads_dev = w_uq.shape[1]
        heads = heads_dev * tp_size
        v_dim = w_uv.shape[2]
        scale = qk_dim ** -0.5
        half_len = seq_local // 2
        half_heads = heads_dev // 2

        def swapped(val):
            return lax.ppermute(val, 'cp', swap_pairs)

        def gather_weight(w):
            half = lax.dynamic_slice_in_dim(w, cp_rank * half_heads, half_heads, 0)
            return lax.all_gather(half, ('tp', 'cp'), axis=0, tiled=True)

        slabs = q_lora // kv_lora
        wq_rows = jnp.transpose(w_uq.reshape(slabs, kv_lora, heads_dev, qk_dim), (2, 0, 3, 1)).reshape(heads_dev, slabs * qk_dim, kv_lora)
        w_up = gather_weight(jnp.concatenate([wq_rows, jnp.transpose(w_uk, (1, 2, 0)), jnp.transpose(w_uv, (1, 2, 0))], axis=1))
        wo_all = gather_weight(w_o).reshape(heads * v_dim, dim)

        def q_rows(lo, hi):
            parts = [w_up[:, s * qk_dim + lo:s * qk_dim + hi] for s in range(slabs)]
            return jnp.concatenate(parts, axis=2).reshape(heads * (hi - lo), q_lora)

        wqn = q_rows(0, nope)
        wqp = q_rows(nope, qk_dim)
        wuk = w_up[:, slabs * qk_dim:slabs * qk_dim + nope].reshape(heads * nope, kv_lora)
        wuv = w_up[:, slabs * qk_dim + nope:].reshape(heads * v_dim, kv_lora)

        local_idx = jnp.arange(seq_local, dtype=jnp.int32)
        block_id = jnp.where(local_idx < half_len, cp_rank, 2 * cp_size - 1 - cp_rank)
        positions = block_id * half_len + local_idx % half_len
        cos_tab, sin_tab = rope_tables(positions, rope_dim)
        cos128 = jnp.tile(cos_tab, (1, 8))
        sin128 = jnp.tile(jnp.concatenate([-sin_tab, sin_tab], axis=1), (1, 4))

        w_cat = jnp.concatenate([w_dq, w_dkv], axis=1)
        x_own = lax.dynamic_slice_in_dim(hidden, tp_rank * nb, nb, 0)
        dy_own = lax.dynamic_slice_in_dim(grad_out, tp_rank * nb, nb, 0)

        raw = jnp.einsum('btd,dq->btq', x_own, w_cat, preferred_element_type=F32).astype(BF16)
        cq_f32 = raw[..., :q_lora].astype(F32)
        ckv_f32 = raw[..., q_lora:q_lora + kv_lora].astype(F32)
        gq_f32 = g_q.astype(F32)
        gkv_f32 = g_kv.astype(F32)
        c_q = norm_f32(cq_f32, gq_f32).astype(BF16)
        c_kv = norm_f32(ckv_f32, gkv_f32).astype(BF16)
        k_pe = apply_rope(raw[..., q_lora + kv_lora:].astype(F32), cos_tab, sin_tab).astype(BF16)

        def by_position(own, other):
            lo = jnp.where(cp_rank == 0, own[:, :half_len], other[:, :half_len])
            lo2 = jnp.where(cp_rank == 0, other[:, :half_len], own[:, :half_len])
            hi = jnp.where(cp_rank == 0, other[:, half_len:], own[:, half_len:])
            hi2 = jnp.where(cp_rank == 0, own[:, half_len:], other[:, half_len:])
            return jnp.concatenate([lo, lo2, hi, hi2], axis=1)

        other_kv, other_pe = lax.ppermute((c_kv, k_pe), 'cp', swap_pairs)
        ckv_seq = by_position(c_kv, other_kv)
        kpe_seq = by_position(k_pe, other_pe)
        ckvt_seq = jnp.swapaxes(ckv_seq, 1, 2)
        kpet_seq = jnp.swapaxes(kpe_seq, 1, 2)
        kpe4 = jnp.tile(kpe_seq, (1, 1, 4))

        qn = jnp.einsum('btq,fq->btf', c_q, wqn, preferred_element_type=F32).astype(BF16)
        qp = jnp.einsum('btq,fq->btf', c_q, wqp, preferred_element_type=F32).astype(BF16)
        grad_o = jnp.einsum('btd,fd->btf', dy_own, wo_all, preferred_element_type=F32).astype(BF16)

        rank_arr = cp_rank.astype(jnp.int32).reshape(1)
        attn_args = (rank_arr, qn, qp, ckv_seq, ckvt_seq, kpe4, wuk, wuv, cos128, sin128)
        prev = None
        o_all = [None] * nb
        o_first = attention(0, None, None, scale, *attn_args)[0]
        o_all[0] = lax.all_gather(o_first, 'tp', axis=0, tiled=True)
        for j in (*range(1, nb), 0):
            res = attention(j, [grad_o, kpet_seq], prev, scale, *attn_args)
            prev = res[1:]
            if j:
                o_all[j] = lax.all_gather(res[0], 'tp', axis=0, tiled=True)
        dqn, dqp, dc_seq, dkp_seq, dwk, dwv = prev

        dkp_seq = dkp_seq[..., :32] + dkp_seq[..., 32:64] + dkp_seq[..., 64:96] + dkp_seq[..., 96:]
        lat = jnp.concatenate([dc_seq, dkp_seq], axis=-1)
        b0, b1, b2, b3 = (lat[:, i * half_len:(i + 1) * half_len] for i in range(4))
        outer = jnp.concatenate([b0, b3], axis=1)
        inner = jnp.concatenate([b1, b2], axis=1)
        mine = jnp.where(cp_rank == 0, outer, inner)
        theirs = jnp.where(cp_rank == 0, inner, outer)
        lat = mine + lax.ppermute(theirs, 'cp', swap_pairs)
        grad_cq = jnp.einsum('btf,fq->btq', dqn, wqn, preferred_element_type=F32) + jnp.einsum('btf,fq->btq', dqp, wqp, preferred_element_type=F32)

        norm_q_pull = jax.vjp(norm_f32, cq_f32, gq_f32)[1]
        grad_cq_raw, grad_g_q = norm_q_pull(grad_cq)
        norm_kv_pull = jax.vjp(norm_f32, ckv_f32, gkv_f32)[1]
        grad_ckv_raw, grad_g_kv = norm_kv_pull(lat[..., :kv_lora])
        grad_raw = jnp.concatenate([grad_cq_raw, grad_ckv_raw, unrope(lat[..., kv_lora:], cos_tab, sin_tab)], axis=-1).astype(BF16)
        grad_raw = lax.all_gather(grad_raw, 'tp', axis=0, tiled=True)
        part = jnp.concatenate([grad_g_q, grad_g_kv])
        part = part + swapped(part)
        parts = jnp.stack([part] + [lax.ppermute(part, 'tp', [(s, (s + k) % tp_size) for s in range(tp_size)]) for k in range(1, tp_size)])
        grad_g = sum(lax.dynamic_index_in_dim(parts, (tp_rank - s) % tp_size, 0, keepdims=False) for s in range(tp_size))

        q_half = q_lora // 2
        cq_mine = lax.dynamic_slice_in_dim(c_q, cp_rank * q_half, q_half, 2)
        cq_theirs = lax.dynamic_slice_in_dim(c_q, (1 - cp_rank) * q_half, q_half, 2)

        def dw_of(dq, cq):
            return jnp.einsum('btf,btq->fq', dq, cq, preferred_element_type=F32)

        dwqn = dw_of(dqn, cq_mine) + swapped(dw_of(dqn, cq_theirs))
        dwqp = dw_of(dqp, cq_mine) + swapped(dw_of(dqp, cq_theirs))
        c_half = kv_lora // 2
        dw_kv = jnp.stack([dwk, dwv])
        kv_mine = lax.dynamic_slice_in_dim(dw_kv, cp_rank * c_half, c_half, 1)
        kv_theirs = lax.dynamic_slice_in_dim(dw_kv, (1 - cp_rank) * c_half, c_half, 1)
        dw_kv = kv_mine + swapped(kv_theirs)
        dwqn = lax.psum_scatter(dwqn, 'tp', scatter_dimension=0, tiled=True)
        dwqp = lax.psum_scatter(dwqp, 'tp', scatter_dimension=0, tiled=True)
        dw_kv = lax.psum_scatter(dw_kv, 'tp', scatter_dimension=2, tiled=True)
        dwq = jnp.concatenate([dwqn.reshape(heads_dev, nope, q_half), dwqp.reshape(heads_dev, rope_dim, q_half)], axis=1)

        def join(part, axis):
            other = lax.ppermute(part, 'cp', swap_pairs)
            return jnp.concatenate([jnp.where(cp_rank == 0, part, other), jnp.where(cp_rank == 0, other, part)], axis=axis)

        grad_w_uq = jnp.transpose(join(dwq, 2), (2, 0, 1))
        dw_kv = join(dw_kv, 1)
        grad_w_uk = dw_kv[0].reshape(kv_lora, heads_dev, nope)
        grad_w_uv = dw_kv[1].reshape(kv_lora, heads_dev, v_dim)

        y = None
        for j in range(nb):
            y = out_proj(j, nb, o_all[j], wo_all, y)
        attn_out = y.reshape(n_batch, seq_local, dim)
        cols = heads_dev * v_dim
        dwo = grad_wo(o_all, grad_out, cols, tp_rank.astype(jnp.int32).reshape(1))
        grad_w_o = (dwo + lax.ppermute(dwo, 'cp', swap_pairs)).reshape(heads_dev, v_dim, dim)

        dw_cat = jnp.einsum('btq,btd->qd', grad_raw, hidden, preferred_element_type=F32)
        grad_w_dq, grad_w_dkv = join_cp(dw_cat, lax.ppermute(dw_cat, 'cp', swap_pairs), q_lora)
        grad_hidden = jnp.einsum('btq,dq->btd', grad_raw, w_cat, preferred_element_type=F32).astype(BF16)
        return (attn_out, grad_hidden, grad_w_dq, grad_g[:q_lora], grad_w_dkv, grad_g[q_lora:], grad_w_uq, grad_w_uk, grad_w_uv, grad_w_o)

    seq_spec = P(None, 'cp', None)
    full_spec = P()
    head_spec = P(None, 'tp', None)
    out_head_spec = P('tp', None, None)
    all_specs = (seq_spec, seq_spec, full_spec, full_spec, full_spec, full_spec, head_spec, head_spec, head_spec, out_head_spec)
    return jax.shard_map(per_device, mesh=mesh, in_specs=all_specs, out_specs=all_specs, check_vma=False)
```

time: 1220 us -> 1170 us (0.959)
  Pallas kernels: 368 us -> 434 us
  matrix products: 233 us -> 193 us
  blocking collectives: 23 us -> 0 us
  waiting for transfers between devices: 444 us -> 421 us
  other arithmetic: 59.8 us -> 38.1 us
  local copies, waits for them, and re-layouts: 63.5 us -> 49.5 us
    pallas_call x3 -> x6, Pallas kernels: 265 us -> 330 us  [the longest x4 277 us: attention(): pl.pallas_call(functools.partial(attn_kernel, grad, first, scale), grid=(...]
    all_gather x1, waiting for transfers between devices: 38.7 us -> 84.3 us  [per_device(): grad_raw = lax.all_gather(grad_raw, 'tp', axis=0, tiled=True)]
    reduce_scatter x1, waiting for transfers between devices: 34.6 us -> 0.01 us  [per_device(): dw_kv = lax.psum_scatter(dw_kv, 'tp', scatter_dimension=2, tiled=True)]
    dot_general x2 -> x1, matrix products: 74.4 us -> 42.5 us  [per_device(): jnp.einsum('btq,btd->qd', grad_raw, hidden, preferred_element_type=F32)]
    psum x1 -> x0, blocking collectives: 23 us -> none  [per_device(): grad_g = lax.psum(jnp.concatenate([grad_g_q, grad_g_kv]), ('tp', 'cp'))]
    another operation x4 -> x0, local copies, waits for them, and re-layouts: 18.3 us -> none  [per_device(): jnp.stack([lax.dynamic_slice_in_dim(o, tp_rank * cols, cols, 2) for o in...]
    all_gather x3 -> x2, waiting for transfers between devices: 78.4 us -> 61.8 us  [gather_weight(): return lax.all_gather(half, ('tp', 'cp'), axis=0, tiled=True)]
    reduce_scatter x1, waiting for transfers between devices: 17.3 us -> 1 us  [per_device(): dwqn = lax.psum_scatter(dwqn, 'tp', scatter_dimension=0, tiled=True)]
  transfers between devices with their start and end apart: 20 -> 23, of which waited for: 10 -> 13; matrix products, arithmetic and copies ran while one was open for 23% -> 19% of each run, Pallas kernels for 8% -> 15%
where the time goes in v3:
time: 1170 us; the launch traced here: 1160 us
  Pallas kernels  434 us (37%)
  waiting for transfers between devices  421 us (36%)
  matrix products  193 us (16%)
  local copies, waits for them, and re-layouts  49.5 us (4%)
  other arithmetic  38.1 us (3%)
  between operations  14.7 us (1%)
    pallas_call x4, Pallas kernels, attention(): pl.pallas_call(functools.partial(attn_kernel, grad, first, scale), grid=(...  277 us
    all_gather x2, waiting for transfers between devices, per_device(): o_all[j] = lax.all_gather(res[0], 'tp', axis=0, tiled=True)  162 us
    pallas_call x3, Pallas kernels, out_proj(): pl.pallas_call(out_kernel, grid=(dim // 256,), in_specs=in_specs, out_spe...  103 us
    all_gather x1, waiting for transfers between devices, per_device(): o_all[0] = lax.all_gather(o_first, 'tp', axis=0, tiled=True)  99 us
    all_gather x1, waiting for transfers between devices, per_device(): grad_raw = lax.all_gather(grad_raw, 'tp', axis=0, tiled=True)  84.3 us
    all_gather x2, waiting for transfers between devices, gather_weight(): return lax.all_gather(half, ('tp', 'cp'), axis=0, tiled=True)  61.8 us
    dot_general x1, matrix products, per_device(): jnp.einsum('btq,dq->btd', grad_raw, w_cat, preferred_element_type=F32)  46.3 us
    dot_general x1, matrix products, per_device(): jnp.einsum('btq,btd->qd', grad_raw, hidden, preferred_element_type=F32)  42.5 us
  transfers between devices with their start and end apart: 23, of which 13 were waited for; matrix products, arithmetic and copies ran while one was open for 19% of the time, Pallas kernels for 15%

profile of v3, /device:TPU:0, one launch (start us, length us, event | category | flops | bytes accessed | tf_op | source)
XLA Modules:
  0.0 1159.7 jit_solution(303500648840829902)
XLA Ops:
  7.2 4.5 reshape.222
  11.8 2.9 copy.139
  14.7 2.2 fusion.31
  18.4 6.3 copy.138
  24.9 13.1 %fusion.14 = bf16[3,512,1056]{1,2,0:T(8,128)(2,1)S(1)} fusion(bf16[12,512,2560]{2,1,0:T(8,128)(2,1)} %param.10, s32[]{:T(128)S(6)} %select_n.146, bf16[2560,288]{0,1:T(8,128)(2,1)} %param.14, bf16[2560,768]{0,1:T(8,128)(2,1)} %copy.138), kind=kOutput, calls=%fused_computation.26 | convolution fusion | flops 8317157376 | bytes 16515076 | tf_op jit(solution)/shard_map/btd,dq->btq/dot_general | solution.py:468
  42.9 2.1 fusion.9
  54.2 15.0 %all-gather.7.cloned.1.call-done = bf16[40,416,256]{2,1,0:T(8,128)(2,1)} async-done(((bf16[5,416,256]{2,1,0:T(8,128)(2,1)}), bf16[40,416,256]{2,1,0:T(8,128)(2,1)}) %all-gather.7.cloned.1.call-update) | async-done | bytes 8519696 | tf_op jit(solution)/shard_map/all_gather | solution.py:441
  69.2 1.6 fusion.58
  71.0 6.3 fusion.57
  77.7 2.3 copy-done.9
  80.0 4.8 convolution_convert_fusion.2.refs_2_
  84.8 8.6 convolution_convert_fusion.1.refs_1_
  93.4 46.8 %all-gather.9.cloned.1.call-done = bf16[40,64,2560]{2,1,0:T(8,128)(2,1)} async-done(((bf16[5,64,2560]{2,1,0:T(8,128)(2,1)}), bf16[40,64,2560]{2,1,0:T(8,128)(2,1)}) %all-gather.9.cloned.1.call-update) | async-done | bytes 13107216 | tf_op jit(solution)/shard_map/all_gather | solution.py:441
  140.2 26.8 %fusion.4.refs_10_ = bf16[3,512,2560]{2,1,0:T(8,128)(2,1)} fusion(bf16[2560,2560,1]{1,0,2:T(8,128)(2,1)} %bitcast.117, bf16[12,512,2560]{2,1,0:T(8,128)(2,1)} %param.11, s32[]{:T(128)S(6)} %select_n.146), kind=kOutput, calls=%fused_computation.11 | convolution fusion | flops 20136591360 | bytes 28835844 | tf_op jit(solution)/shard_map/btd,fd->btf/dot_general | solution.py:493
  167.1 80.7 %attn_fwd_bwd.3 = (bf16[1,512,2560]{2,1,0:T(8,128)(2,1)}, bf16[3,512,2560]{2,1,0:T(8,128)(2,1)}, bf16[3,512,1280]{2,1,0:T(8,128)(2,1)}, f32[3,1024,256]{2,1,0:T(...) custom-call(s32[1]{0:T(128)} %bitcast.refs_0_, ...), custom_call_target="tpu_custom_call" | custom-call | flops 40265318400 | bytes 78643200 | tf_op jit(solution)/shard_map/attn_fwd_bwd/pallas_call | solution.py:297
  247.8 81.6 %attn_fwd_bwd.4 = (bf16[1,512,2560]{2,1,0:T(8,128)(2,1)}, bf16[3,512,2560]{2,1,0:T(8,128)(2,1)}, bf16[3,512,1280]{2,1,0:T(8,128)(2,1)}, f32[3,1024,256]{2,1,0:T(...) custom-call(s32[1]{0:T(128)} %bitcast.refs_0_, ...), custom_call_target="tpu_custom_call", output_to_operand_aliasing={{5}: (12, {}), {6}: (13, {}), {1}: (14, {}), {2}: (15, {}),... | custom-call | flops 40265318400 | bytes 78643200 | tf_op jit(solution)/shard_map/attn_fwd_bwd/pallas_call | solution.py:297
  329.5 81.5 %attn_fwd_bwd.5 = (bf16[1,512,2560]{2,1,0:T(8,128)(2,1)}, bf16[3,512,2560]{2,1,0:T(8,128)(2,1)}, bf16[3,512,1280]{2,1,0:T(8,128)(2,1)}, f32[3,1024,256]{2,1,0:T(...) custom-call(s32[1]{0:T(128)} %bitcast.refs_0_, ...), custom_call_target="tpu_custom_call", output_to_operand_aliasing={{5}: (12, {}), {6}: (13, {}), {1}: (14, {}), {2}: (15, {}),... | custom-call | flops 40265318400 | bytes 78643200 | tf_op jit(solution)/shard_map/attn_fwd_bwd/pallas_call | solution.py:297
  410.9 3.5 fusion.19
  414.5 4.0 collective-permute-start.11
  418.5 4.9 collective-permute-done.11
  423.4 3.9 fusion.21
  429.0 5.6 convolution_bitcast_fusion.3
  435.0 9.6 convolution_bitcast_fusion.1
  444.9 6.4 fusion.18
  451.7 9.8 fusion.17
  461.6 33.6 %attn_fwd.1 = bf16[1,512,2560]{2,1,0:T(8,128)(2,1)} custom-call(s32[1]{0:T(128)} %bitcast.refs_0_, bf16[3,512,2560]{2,1,0:T(8,128)(2,1)} %convolution_convert_fusion.1.refs_1_, bf16[3,512,1280]{2,1,0:T(8,128)(2,1)} %convolution_convert_fusion.2.refs_2_, bf16[3,1024,256]{2,1,0:T(8,128)(2,1)} %copy.146.refs_3_, ...), custom_call_target="tpu_custom_call" | custom-call | flops 13421772800 | bytes 78643200 | tf_op jit(solution)/shard_map/attn_fwd/pallas_call | solution.py:297
  496.7 2.4 copy.164
  499.1 3.4 copy.160
  506.1 11.2 fusion.59
  517.4 8.4 fusion.10
  528.6 1.8 pad_maximum_fusion.1
  537.0 2.2 collective-permute-done.5
  541.4 2.6 pad_maximum_fusion.5
  544.0 99.0 %all-gather.15.cloned.1.call-done.o_ref.refs_0_ = bf16[4,512,2560]{2,1,0:T(8,128)(2,1)} async-done(((bf16[1,512,2560]{2,1,0:T(8,128)(2,1)}), bf16[4,512,2560]{2,1,0:T(8,128)(2,1)}) %all-gather.15.cloned.1.call-update) | async-done | bytes 10485776 | tf_op jit(solution)/shard_map/all_gather | solution.py:500
  643.0 34.6 %out_proj.3.rest_0_ = bf16[4,3,512,2560]{3,2,1,0:T(8,128)(2,1)} custom-call(bf16[4,512,2560]{2,1,0:T(8,128)(2,1)} %all-gather.15.cloned.1.call-done.o_ref.refs_0_, bf16[2560,2560]{1,0:T(8,128)(2,1)} %bitcast.118), custom_call_target="tpu_custom_call" | custom-call | flops 26843545600 | bytes 34078720 | tf_op jit(solution)/shard_map/out_proj/pallas_call | solution.py:328
  680.1 1.6 broadcast_select_fusion.2
  681.6 1.8 maximum_bitcast_fusion.3
  683.5 61.3 %all-gather.13.cloned.1.call-done.o_ref.refs_1_ = bf16[4,512,2560]{2,1,0:T(8,128)(2,1)} async-done(((bf16[1,512,2560]{2,1,0:T(8,128)(2,1)}), bf16[4,512,2560]{2,1,0:T(8,128)(2,1)}) %all-gather.13.cloned.1.call-update) | async-done | bytes 10485776 | tf_op jit(solution)/shard_map/all_gather | solution.py:505
  744.8 101.2 %all-gather.11.cloned.1.call-done.o_ref.refs_2_ = bf16[4,512,2560]{2,1,0:T(8,128)(2,1)} async-done(((bf16[1,512,2560]{2,1,0:T(8,128)(2,1)}), bf16[4,512,2560]{2,1,0:T(8,128)(2,1)}) %all-gather.11.cloned.1.call-update) | async-done | bytes 10485776 | tf_op jit(solution)/shard_map/all_gather | solution.py:505
  846.0 38.1 %grad_wo.1 = f32[640,2560]{1,0:T(8,128)} custom-call(s32[1]{0:T(128)} %bitcast.39.col_ref, bf16[4,512,2560]{2,1,0:T(8,128)(2,1)} %all-gather.15.cloned.1.call-done.o_ref.refs_0_, bf16[4,512,2560]{2,1,0:T(8,128)(2,1)} %all-gather.13.cloned.1.call-done.o_ref.refs_1_, bf16[4,512,2560]{2,1,0:T(8,128)(2,1)} %all-gather.11.cloned.1.call-done.o_ref.refs_2_, ...), custom_call_target="tpu_custom_call" | custom-call | flops 20132659200 | bytes 39321600 | tf_op jit(solution)/shard_map/grad_wo/pallas_call | solution.py:376
  884.1 84.3 %all-gather.17.cloned.1.call-done = bf16[12,512,1056]{1,2,0:T(8,128)(2,1)} async-done(((bf16[3,512,1056]{1,2,0:T(8,128)(2,1)}), bf16[12,512,1056]{1,2,0:T(8,128)(2,1)}) %all-gather.17.cloned.1.call-update) | async-done | bytes 12976144 | tf_op jit(solution)/shard_map/all_gather | solution.py:523
  968.4 42.5 %convolution_bitcast_fusion.a_ref = f32[1056,2560]{1,0:T(8,128)} fusion(bf16[12,512,1056]{1,2,0:T(8,128)(2,1)} %all-gather.17.cloned.1.call-done, bf16[12,512,2560]{2,1,0:T(8,128)(2,1)} %param.10), kind=kOutput, calls=%fused_computation.1 | convolution fusion | flops 33218887680 | bytes 55246848 | tf_op jit(solution)/shard_map/btq,btd->qd/dot_general | solution.py:565
  1011.0 34.2 %out_proj.4.rest_0_ = bf16[4,3,512,2560]{3,2,1,0:T(8,128)(2,1)} custom-call(bf16[4,512,2560]{2,1,0:T(8,128)(2,1)} %all-gather.13.cloned.1.call-done.o_ref.refs_1_, bf16[2560,2560]{1,0:T(8,128)(2,1)} %bitcast.119, bf16[4,3,512,2560]{3,2,1,0:T(8,128)(2,1)} %out_proj.3.rest_0_), custom_call_target="tpu_custom_call", output_to_operand_aliasing={{}: (2, {})} | custom-call | flops 26843545600 | bytes 34078720 | tf_op jit(solution)/shard_map/out_proj/pallas_call | solution.py:328
  1045.2 34.6 %out_proj.5 = bf16[4,3,512,2560]{3,2,1,0:T(8,128)(2,1)} custom-call(bf16[4,512,2560]{2,1,0:T(8,128)(2,1)} %all-gather.11.cloned.1.call-done.o_ref.refs_2_, bf16[2560,2560]{1,0:T(8,128)(2,1)} %bitcast.120, bf16[4,3,512,2560]{3,2,1,0:T(8,128)(2,1)} %out_proj.4.rest_0_), custom_call_target="tpu_custom_call", output_to_operand_aliasing={{}: (2, {})} | custom-call | flops 26843545600 | bytes 34078720 | tf_op jit(solution)/shard_map/out_proj/pallas_call | solution.py:328
  1079.8 46.3 %convolution_convert_fusion = bf16[12,512,2560]{2,1,0:T(8,128)(2,1)} fusion(bf16[12,512,1056]{1,2,0:T(8,128)(2,1)} %all-gather.17.cloned.1.call-done, bf16[2560,288]{0,1:T(8,128)(2,1)S(1)} %copy-done.32, bf16[2560,768]{0,1:T(8,128)(2,1)S(1)} %copy-done.5), kind=kOutput, calls=%fused_computation | convolution fusion | flops 33245429760 | bytes 49840128 | tf_op jit(solution)/shard_map/btq,dq->btd/dot_general | solution.py:567
  1126.1 6.9 add.174
  1133.1 14.6 %join_cp.1 = (f32[2560,768]{1,0:T(8,128)}, f32[2560,288]{1,0:T(8,128)}) custom-call(f32[1056,2560]{1,0:T(8,128)} %convolution_bitcast_fusion.a_ref, f32[1056,2560]{1,0:T(8,128)} %collective-permute-done.3.b_ref), custom_call_target="tpu_custom_call" | custom-call | flops 2703360 | bytes 32440320 | tf_op jit(solution)/shard_map/join_cp/pallas_call | solution.py:402
  1147.7 5.2 copy.175
  (167 shorter events, 37.9 us)
Async XLA Ops:
  7.2 9.8 copy-start
  7.2 62.0 %all-gather.7.cloned.1.call-start = ((), (), s32[]{:S(2)}) async-start(), calls=%async_computation.3 | async-start | bytes 9584640 | tf_op jit(solution)/shard_map/all_gather | solution.py:441
  17.0 123.3 %all-gather.9.cloned.1.call-start = ((), (), s32[]{:S(2)}) async-start(), calls=%async_computation.4 | async-start | bytes 14745600 | tf_op jit(solution)/shard_map/all_gather | solution.py:441
  18.3 522.1 %reduce-scatter.8.cloned.1.call-start = ((), (), s32[]{:S(2)}) async-start(), calls=%async_computation.11 | async-start | bytes 3276800 | tf_op jit(solution)/shard_map/reduce_scatter | solution.py:545
  24.9 20.0 %copy-start.17 = (f32[512,16]{0,1:T(8,128)}, f32[512,16]{0,1:T(8,128)S(1)}, u32[]{:S(2)}) copy-start(f32[512,16]{0,1:T(8,128)S(1)} %get-tuple-element.129) | copy-start | bytes 98308
  24.9 20.9 %copy-start.15 = (f32[512,16]{0,1:T(8,128)}, f32[512,16]{0,1:T(8,128)S(1)}, u32[]{:S(2)}) copy-start(f32[512,16]{0,1:T(8,128)S(1)} %get-tuple-element.130) | copy-start | bytes 98308
  24.9 14.0 %copy-start.33 = (bf16[256]{0:T(256)(128)(2,1)S(1)}, bf16[256]{0:T(256)(128)(2,1)}, u32[]{:S(2)}) copy-start(bf16[256]{0:T(256)(128)(2,1)} %param.15) | copy-start | bytes 1540
  38.1 4.8 copy-start.2
  38.1 3.7 copy-start.31
  38.2 8.5 collective-permute-start.1
  39.0 2.5 copy-start.29
  41.5 8.1 collective-permute-start
  41.8 3.2 copy-start.27
  71.0 6.7 copy-start.11
  77.3 2.8 copy-start.9
  77.7 7.1 copy-start.6
  410.9 12.4 %copy-start.4 = (f32[256,2560]{1,0:T(8,128)S(1)}, f32[256,2560]{1,0:T(8,128)}, u32[]{:S(2)}) copy-start(f32[256,2560]{1,0:T(8,128)} %get-tuple-element.52) | copy-start | bytes 7864324
  414.5 8.9 collective-permute-start.11
  427.3 113.1 %reduce-scatter.6.cloned.1.call-start = ((), (), s32[]{:S(2)}) async-start(), calls=%async_computation.10 | async-start | bytes 2457600 | tf_op jit(solution)/shard_map/reduce_scatter | solution.py:544
  434.6 10.3 collective-permute-start.9
  444.6 7.1 collective-permute-start.8
  451.3 90.1 %reduce-scatter.4.cloned.1.call-start = ((), (), s32[]{:S(2)}) async-start(), calls=%async_computation.9 | async-start | bytes 4915200 | tf_op jit(solution)/shard_map/reduce_scatter | solution.py:543
  461.5 181.5 %all-gather.15.cloned.1.call-start = ((), (), s32[]{:S(2)}) async-start(), calls=%async_computation.7 | async-start | bytes 13107200 | tf_op jit(solution)/shard_map/all_gather | solution.py:500
  495.2 249.6 %all-gather.13.cloned.1.call-start = ((), (), s32[]{:S(2)}) async-start(), calls=%async_computation.6 | async-start | bytes 13107200 | tf_op jit(solution)/shard_map/all_gather | solution.py:505
  495.9 350.0 %all-gather.11.cloned.1.call-start = ((), (), s32[]{:S(2)}) async-start(), calls=%async_computation.5 | async-start | bytes 13107200 | tf_op jit(solution)/shard_map/all_gather | solution.py:505
  496.7 471.8 %all-gather.17.cloned.1.call-start = ((), (), s32[]{:S(2)}) async-start(), calls=%async_computation.8 | async-start | bytes 16220160 | tf_op jit(solution)/shard_map/all_gather | solution.py:523
  504.3 13.0 %copy-start.3 = (bf16[3,512,1056]{1,2,0:T(8,128)(2,1)S(1)}, bf16[3,512,1056]{1,2,0:T(8,128)(2,1)}, u32[]{:S(2)}) copy-start(bf16[3,512,1056]{1,2,0:T(8,128)(2,1)} %copy-done.2) | copy-start | bytes 9732100
  504.3 13.0 %copy-start.12 = (bf16[40,32,768]{2,1,0:T(8,128)(2,1)S(1)}, bf16[40,32,768]{2,1,0:T(8,128)(2,1)}, u32[]{:S(2)}) copy-start(bf16[40,32,768]{2,1,0:T(8,128)(2,1)} %copy-done.11) | copy-start | bytes 5898244
  504.3 13.0 %copy-start.26 = (f32[3,512]{1,0:T(4,128)S(1)}, f32[3,512]{1,0:T(4,128)}, u32[]{:S(2)}) copy-start(f32[3,512]{1,0:T(4,128)} %copy-done.25) | copy-start | bytes 18436
  504.3 13.0 %copy-start.28 = (f32[768]{0:T(1024)S(1)}, f32[768]{0:T(1024)}, u32[]{:S(2)}) copy-start(f32[768]{0:T(1024)} %copy-done.27) | copy-start | bytes 9220
  504.3 13.0 %copy-start.34 = (bf16[3,512,1280]{2,1,0:T(8,128)(2,1)S(1)}, bf16[3,512,1280]{2,1,0:T(8,128)(2,1)}, u32[]{:S(2)}) copy-start(bf16[3,512,1280]{2,1,0:T(8,128)(2,1)} %get-tuple-element.47) | copy-start | bytes 11796484
  504.3 22.6 %collective-permute-start.2 = (f32[3,512,288]{1,2,0:T(8,128)S(1)}, f32[3,512,288]{1,2,0:T(8,128)S(1)}, u32[]{:S(2)}, u32[]{:S(2)}) collective-permute-start(f32[3,512,288]{1,2,0:T(8,128)S(1)} %broadcast_select_fusion), channel_id=1, source_target_pairs={{0,1},{1,0},{2,3},{3,2},{4,5},{5,4},{6,7},{7,6}} | collective-permute-start | bytes 5308424 | tf_op jit(solution)/shard_map/ppermute | solution.py:515
  517.3 8.4 copy-start.24
  530.5 1.5 collective-permute-start.4
  531.9 3.8 collective-permute-start.7
  533.2 3.8 collective-permute-start.6
  534.5 4.7 collective-permute-start.5
  540.4 137.3 %collective-permute-start.12 = (f32[2,128,640]{2,1,0:T(8,128)}, f32[2,128,640]{2,1,0:T(8,128)S(1)}, u32[]{:S(2)}, u32[]{:S(2)}) collective-permute-start(f32[2,128,640]{2,1,0:T(8,128)} %reduce-scatter.8.cloned.1.call-done), channel_id=1, source_target_pairs={{0,1},{1,0},{2,3},{3,2},{4,5},{5,4},{6,7},{7,6}} | collective-permute-start | bytes 1966088 | tf_op jit(solution)/shard_map/ppermute | solution.py:549
  544.0 136.0 %collective-permute-start.10 = (f32[10,96,384]{2,1,0:T(8,128)}, f32[10,96,384]{2,1,0:T(8,128)}, u32[]{:S(2)}, u32[]{:S(2)}) collective-permute-start(f32[10,96,384]{2,1,0:T(8,128)} %pad_maximum_fusion.5), channel_id=1, source_target_pairs={{0,1},{1,0},{2,3},{3,2},{4,5},{5,4},{6,7},{7,6}} | collective-permute-start | bytes 4423688 | tf_op jit(solution)/shard_map/ppermute | solution.py:549
  643.0 34.6 %copy-start.14 = (f32[2,128,640]{2,1,0:T(8,128)S(1)}, f32[2,128,640]{2,1,0:T(8,128)}, u32[]{:S(2)}) copy-start(f32[2,128,640]{2,1,0:T(8,128)} %reduce-scatter.8.cloned.1.call-done) | copy-start | bytes 1966084
  677.8 2.3 copy-start.8
  884.1 242.0 %collective-permute-start.13 = (f32[640,2560]{1,0:T(8,128)}, f32[640,2560]{1,0:T(8,128)}, u32[]{:S(2)}, u32[]{:S(2)}) collective-permute-start(f32[640,2560]{1,0:T(8,128)} %grad_wo.1), channel_id=1, source_target_pairs={{0,1},{1,0},{2,3},{3,2},{4,5},{5,4},{6,7},{7,6}} | collective-permute-start | bytes 19660808 | tf_op jit(solution)/shard_map/ppermute | solution.py:563
  1011.0 122.1 %collective-permute-start.3 = (f32[1056,2560]{1,0:T(8,128)}, f32[1056,2560]{1,0:T(8,128)}, u32[]{:S(2)}, u32[]{:S(2)}) collective-permute-start(f32[1056,2560]{1,0:T(8,128)} %convolution_bitcast_fusion.a_ref), channel_id=1, source_target_pairs={{0,1},{1,0},{2,3},{3,2},{4,5},{5,4},{6,7},{7,6}} | collective-permute-start | bytes 32440328 | tf_op jit(solution)/shard_map/ppermute | solution.py:566
  1045.2 34.6 %copy-start.5 = (bf16[2560,768]{0,1:T(8,128)(2,1)S(1)}, bf16[2560,768]{0,1:T(8,128)(2,1)}, u32[]{:S(2)}) copy-start(bf16[2560,768]{0,1:T(8,128)(2,1)} %copy.138) | copy-start | bytes 11796484
  1045.2 34.6 %copy-start.32 = (bf16[2560,288]{0,1:T(8,128)(2,1)S(1)}, bf16[2560,288]{0,1:T(8,128)(2,1)}, u32[]{:S(2)}) copy-start(bf16[2560,288]{0,1:T(8,128)(2,1)} %param.14) | copy-start | bytes 4423684
  1045.2 80.9 %slice-start = ((s8[6553600]{0:T(1024)(128)(4,1)}), s8[2359296]{0:T(1024)(128)(4,1)S(1)}, s32[]{:S(2)}) async-start(s8[6553600]{0:T(1024)(128)(4,1)} %bitcast.85), calls=%async_computation.12 | async-start | bytes 4718592
  1079.8 46.3 %slice-start.1 = ((s8[6553600]{0:T(1024)(128)(4,1)}), s8[4194304]{0:T(1024)(128)(4,1)S(1)}, s32[]{:S(2)}) async-start(s8[6553600]{0:T(1024)(128)(4,1)} %bitcast.85), calls=%async_computation.13 | async-start | bytes 8388608
  1147.7 5.3 copy-start.1
  (12 other events, 15.1 us)
Sparse Core Ops, SparseCore 0:
  17.1 52.0 all-gather.6
  71.6 68.6 all-gather.8
  427.4 34.0 reduce-scatter.7
  464.4 28.5 reduce-scatter.5
  496.3 45.0 reduce-scatter.3
  543.6 99.3 all-gather.14
  645.4 99.3 all-gather.12
  746.6 99.3 all-gather.10
  848.3 120.0 all-gather.16

commit v4 on v3

--- a/solution.py
+++ b/solution.py
@@ -67,7 +67,7 @@
         dqn_ref, dqp_ref, dc_ref, dkp_ref, dwk_ref, dwv_ref = take(6)
     k_s, vt_s, e_s, p_s, qm_s = take(5)
     if grad:
-        kt_s, v_s, g_s, ds_s, dom_s, dk_s, dv_s = take(7)
+        kt_s, v_s, g_s, ds_s, dom_s, dk_s, dv_s, dqp_s = take(8)
 
     qrows = qn_ref.shape[1]
     blk = qrows // 2
@@ -112,8 +112,6 @@
 
     def run(lo, hi):
         units = [(qrows - blk, hi * blk, h) for h in range(GROUP)] + [(0, lo * blk, h) for h in range(GROUP)]
-        o_t = {}
-        dq_t = {}
 
         def scores(i):
             row0, nk, h = units[i]
@@ -122,7 +120,7 @@
 
         def dprobs(i):
             row0, nk, h = units[i]
-            g_s[i % 2, :nk, :] = mm(v_s[:nk, :], dom_s[h, row0:row0 + blk, :], NT)
+            g_s[i % 2, :nk, :] = mm(v_s[:nk, pair_lanes(h)], dom_s[h, row0:row0 + blk, pair_lanes(h)], NT)
 
         def vector_passes(i):
             _, nk, h = units[i]
@@ -164,20 +162,22 @@
 
         def out(i):
             row0, nk, h = units[i]
-            o_t[h] = mm(vt_s[h * half:h * half + half, :nk], p_s[:nk, h * blk:h * blk + blk])
-            if h % 2:
-                o_ref[0, row0:row0 + blk, pair_lanes(h)] = jnp.concatenate([o_t[h - 1], o_t[h]], axis=0).T.astype(BF16)
+            parts = [mm(vt_s[g * half:g * half + half, :nk], p_s[:nk, g * blk:g * blk + blk]) for g in (h - 1, h)]
+            o_ref[0, row0:row0 + blk, pair_lanes(h)] = jnp.concatenate(parts, axis=0).T.astype(BF16)
 
         def dquery(i):
             row0, nk, h = units[i]
-            kop_t = jnp.concatenate([kt_s[h * half:h * half + half, :nk], kpet_ref[0, :, :nk]], axis=0)
-            dq_t[h] = mm(kop_t, ds_s[:nk, h * blk:h * blk + blk])
             rows = slice(row0, row0 + blk)
-            if h % 2:
-                dqn_ref[0, rows, pair_lanes(h)] = (jnp.concatenate([dq_t[h - 1][:half], dq_t[h][:half]], axis=0).T * scale).astype(BF16)
+            parts = []
+            for g in (h - 1, h):
+                kop_t = jnp.concatenate([kt_s[g * half:g * half + half, :nk], kpet_ref[0, :, :nk]], axis=0)
+                dq = mm(kop_t, ds_s[:nk, g * blk:g * blk + blk])
+                parts.append(dq[:half])
+                dqp_s[g * quarter:g * quarter + quarter, :] = dq[half:]
+            dqn_ref[0, rows, pair_lanes(h)] = (jnp.concatenate(parts, axis=0).T * scale).astype(BF16)
             if h == GROUP - 1:
-                dqp = jnp.concatenate([dq_t[g][half:] for g in range(GROUP)], axis=0).T * scale
-                dqp_ref[0, rows, :] = (dqp * cos[rows] - swap(dqp) * sin[rows]).astype(BF16)
+                dqp = dqp_s[...].T * scale
+                dqp_ref[0, rows, :] = (dqp * cos_ref[rows, :] - swap(dqp) * sin_ref[rows, :]).astype(BF16)
 
         def dkeys(i, dst, lhs, rhs):
             row0, nk, h = units[i]
@@ -194,24 +194,27 @@
             return [functools.partial(scores, i)] + ([functools.partial(dprobs, i)] if grad else [])
 
         def after(i):
-            work = [functools.partial(out, i)]
-            if grad:
-                work.append(functools.partial(dquery, i))
-                if units[i][-1] % 2:
-                    work.append(functools.partial(dkeys, i, dv_s, p_s, dom_s))
-                    work.append(functools.partial(dkeys, i, dk_s, ds_s, qm_s))
-            return work
+            return [functools.partial(out, i)] + ([functools.partial(dquery, i)] if grad else [])
+
+        def after_keys(i):
+            return [functools.partial(dkeys, i, dv_s, p_s, dom_s), functools.partial(dkeys, i, dk_s, ds_s, qm_s)] if grad else []
+
+        def region(i):
+            for u in (i, i + 1):
+                vec = vector_passes(u)
+                mat = before(u + 1) if u + 1 < len(units) else []
+                if i:
+                    mat = mat + (after(i - 1) if u == i else after_keys(i - 1))
+                for c, f in enumerate(vec):
+                    for g in mat[c * len(mat) // len(vec):(c + 1) * len(mat) // len(vec)]:
+                        g()
+                    f()
 
         for f in before(0):
             f()
-        for i in range(len(units)):
-            vec = vector_passes(i)
-            mat = (before(i + 1) if i + 1 < len(units) else []) + (after(i - 1) if i else [])
-            for c, f in enumerate(vec):
-                for g in mat[c * len(mat) // len(vec):(c + 1) * len(mat) // len(vec)]:
-                    g()
-                f()
-        for f in after(len(units) - 1):
+        for i in range(0, len(units), 2):
+            region(i)
+        for f in after(len(units) - 1) + after_keys(len(units) - 1):
             f()
 
     rank = rank_ref[0]
@@ -291,7 +294,7 @@
         scratch += [
             pltpu.VMEM((step, nkeys), BF16), pltpu.VMEM((nkeys, step), BF16), pltpu.VMEM((2, nkeys, blk), F32),
             pltpu.VMEM((nkeys, GROUP * blk), BF16), pltpu.VMEM((GROUP, qrows, step), BF16),
-            pltpu.VMEM((2, nkeys, step), F32), pltpu.VMEM((2, nkeys, step), F32),
+            pltpu.VMEM((2, nkeys, step), F32), pltpu.VMEM((2, nkeys, step), F32), pltpu.VMEM((LANES, blk), F32),
         ]
     pairs = 5 * GROUP * groups * blk * blk
     return pl.pallas_call(
@@ -318,7 +321,8 @@
 def out_proj(j, nb, o_all, w_o, prev):
     tp, rows, width = o_all.shape
     dim = w_o.shape[1]
-    in_specs = [pl.BlockSpec((tp, rows, width), lambda i: (0, 0, 0)), pl.BlockSpec((width, 256), lambda i: (0, i))]
+    tile = 4 * LANES
+    in_specs = [pl.BlockSpec((tp, rows, width), lambda i: (0, 0, 0)), pl.BlockSpec((width, tile), lambda i: (0, i))]
     args = [o_all, w_o]
     aliases = {}
     if prev is not None:
@@ -327,9 +331,9 @@
         aliases = {2: 0}
     return pl.pallas_call(
         out_kernel,
-        grid=(dim // 256,),
+        grid=(dim // tile,),
         in_specs=in_specs,
-        out_specs=pl.BlockSpec((tp, 1, rows, 256), lambda i: (0, j, 0, i)),
+        out_specs=pl.BlockSpec((tp, 1, rows, tile), lambda i: (0, j, 0, i)),
         out_shape=jax.ShapeDtypeStruct((tp, nb, rows, dim), BF16),
         input_output_aliases=aliases,
         name="out_proj",
@@ -367,7 +371,7 @@
     tp, rows, _ = o_all[0].shape
     nb = len(o_all)
     dim = dy.shape[-1]
-    per = 2
+    per = tp
     turns = tp // per
 
     def o_spec(j):
@@ -384,7 +388,7 @@
         ),
         out_shape=jax.ShapeDtypeStruct((cols, dim), F32),
         name="grad_wo",
-        compiler_params=pltpu.CompilerParams(dimension_semantics=("arbitrary",), vmem_limit_bytes=VMEM_LIMIT),
+        compiler_params=pltpu.CompilerParams(dimension_semantics=("arbitrary",), vmem_limit_bytes=VMEM_LIMIT * 9 // 8),
         cost_estimate=pl.CostEstimate(flops=2 * nb * tp * rows * cols * dim, bytes_accessed=2 * nb * tp * rows * (cols + dim), transcendentals=0),
     )(col_arr, *o_all, dy.reshape(tp, nb, rows, dim))
 
@@ -392,7 +396,7 @@
 def join_kernel(a_ref, b_ref, q_ref, kv_ref):
     split = q_ref.shape[1]
     q_ref[...] = (a_ref[:split, :] + b_ref[:split, :]).T
-    kv_ref[...] = (a_ref[split:, :] + b_ref[split:, :]).T
+    kv_ref[...] = a_ref[split:, :] + b_ref[split:, :]
 
 
 def join_cp(a, b, split):
@@ -403,8 +407,8 @@
         join_kernel,
         grid=(dim // tile,),
         in_specs=[part, part],
-        out_specs=[pl.BlockSpec((tile, split), lambda i: (i, 0)), pl.BlockSpec((tile, wide - split), lambda i: (i, 0))],
-        out_shape=[jax.ShapeDtypeStruct((dim, split), F32), jax.ShapeDtypeStruct((dim, wide - split), F32)],
+        out_specs=[pl.BlockSpec((tile, split), lambda i: (i, 0)), pl.BlockSpec((wide - split, tile), lambda i: (0, i))],
+        out_shape=[jax.ShapeDtypeStruct((dim, split), F32), jax.ShapeDtypeStruct((wide - split, dim), F32)],
         name="join_cp",
         compiler_params=pltpu.CompilerParams(dimension_semantics=("arbitrary",), vmem_limit_bytes=VMEM_LIMIT),
         cost_estimate=pl.CostEstimate(flops=wide * dim, bytes_accessed=12 * wide * dim, transcendentals=0),
@@ -436,14 +440,18 @@
         def swapped(val):
             return lax.ppermute(val, 'cp', swap_pairs)
 
-        def gather_weight(w):
-            half = lax.dynamic_slice_in_dim(w, cp_rank * half_heads, half_heads, 0)
+        def own_half(w):
+            return lax.dynamic_slice_in_dim(w, cp_rank * half_heads, half_heads, 0)
+
+        def gather_weight(half):
             return lax.all_gather(half, ('tp', 'cp'), axis=0, tiled=True)
 
         slabs = q_lora // kv_lora
-        wq_rows = jnp.transpose(w_uq.reshape(slabs, kv_lora, heads_dev, qk_dim), (2, 0, 3, 1)).reshape(heads_dev, slabs * qk_dim, kv_lora)
-        w_up = gather_weight(jnp.concatenate([wq_rows, jnp.transpose(w_uk, (1, 2, 0)), jnp.transpose(w_uv, (1, 2, 0))], axis=1))
-        wo_all = gather_weight(w_o).reshape(heads * v_dim, dim)
+        wq_rows = own_half(jnp.transpose(w_uq, (1, 2, 0)))
+        up_rows = [wq_rows[..., s * kv_lora:(s + 1) * kv_lora] for s in range(slabs)]
+        up_rows += [own_half(jnp.transpose(w, (1, 2, 0))) for w in (w_uk, w_uv)]
+        w_up = gather_weight(jnp.concatenate(up_rows, axis=1))
+        wo_all = gather_weight(own_half(w_o)).reshape(heads * v_dim, dim)
 
         def q_rows(lo, hi):
             parts = [w_up[:, s * qk_dim + lo:s * qk_dim + hi] for s in range(slabs)]
@@ -563,9 +571,9 @@
         grad_w_o = (dwo + lax.ppermute(dwo, 'cp', swap_pairs)).reshape(heads_dev, v_dim, dim)
 
         dw_cat = jnp.einsum('btq,btd->qd', grad_raw, hidden, preferred_element_type=F32)
-        grad_w_dq, grad_w_dkv = join_cp(dw_cat, lax.ppermute(dw_cat, 'cp', swap_pairs), q_lora)
+        grad_w_dq, dw_dkv = join_cp(dw_cat, lax.ppermute(dw_cat, 'cp', swap_pairs), q_lora)
         grad_hidden = jnp.einsum('btq,dq->btd', grad_raw, w_cat, preferred_element_type=F32).astype(BF16)
-        return (attn_out, grad_hidden, grad_w_dq, grad_g[:q_lora], grad_w_dkv, grad_g[q_lora:], grad_w_uq, grad_w_uk, grad_w_uv, grad_w_o)
+        return (attn_out, grad_hidden, grad_w_dq, grad_g[:q_lora], dw_dkv.T, grad_g[q_lora:], grad_w_uq, grad_w_uk, grad_w_uv, grad_w_o)
 
     seq_spec = P(None, 'cp', None)
     full_spec = P()

time: 1170 us -> 1150 us (0.983)
  Pallas kernels: 434 us -> 422 us
  transfers between devices with their start and end apart: 23 -> 23, of which waited for: 13 -> 13; matrix products, arithmetic and copies ran while one was open for 19% -> 20% of each run, Pallas kernels for 15% -> 15%
where the time goes in v4:
time: 1150 us; the launch traced here: 1140 us
  waiting for transfers between devices  424 us (37%)
  Pallas kernels  422 us (37%)
  matrix products  194 us (17%)
  local copies, waits for them, and re-layouts  40.9 us (4%)
  other arithmetic  35.9 us (3%)
  between operations  15 us (1%)
    pallas_call x4, Pallas kernels, attention(): pl.pallas_call(functools.partial(attn_kernel, grad, first, scale), grid=(...  270 us
    all_gather x2, waiting for transfers between devices, per_device(): o_all[j] = lax.all_gather(res[0], 'tp', axis=0, tiled=True)  163 us
    pallas_call x3, Pallas kernels, out_proj(): pl.pallas_call(out_kernel, grid=(dim // tile,), in_specs=in_specs, out_sp...  102 us
    all_gather x1, waiting for transfers between devices, per_device(): o_all[0] = lax.all_gather(o_first, 'tp', axis=0, tiled=True)  99 us
    all_gather x1, waiting for transfers between devices, per_device(): grad_raw = lax.all_gather(grad_raw, 'tp', axis=0, tiled=True)  86.4 us
    all_gather x2, waiting for transfers between devices, gather_weight(): return lax.all_gather(half, ('tp', 'cp'), axis=0, tiled=True)  61.1 us
    dot_general x1, matrix products, per_device(): jnp.einsum('btq,dq->btd', grad_raw, w_cat, preferred_element_type=F32)  46.5 us
    dot_general x1, matrix products, per_device(): jnp.einsum('btq,btd->qd', grad_raw, hidden, preferred_element_type=F32)  42.7 us
  transfers between devices with their start and end apart: 23, of which 13 were waited for; matrix products, arithmetic and copies ran while one was open for 20% of the time, Pallas kernels for 15%

profile of v4, /device:TPU:0, one launch (start us, length us, event | category | flops | bytes accessed | tf_op | source)
XLA Modules:
  0.0 1136.2 jit_solution(2909941078176311866)
XLA Ops:
  9.7 2.7 constant_dynamic-slice_fusion
  12.5 6.3 copy.97
  19.1 12.9 %fusion.14 = bf16[3,512,1056]{1,2,0:T(8,128)(2,1)S(1)} fusion(bf16[12,512,2560]{2,1,0:T(8,128)(2,1)} %param.10, s32[]{:T(128)S(6)} %select_n.148, bf16[2560,288]{0,1:T(8,128)(2,1)} %param.14, bf16[2560,768]{0,1:T(8,128)(2,1)} %copy.97), kind=kOutput, calls=%fused_computation.26 | convolution fusion | flops 8317157376 | bytes 16515076 | tf_op jit(solution)/shard_map/btd,dq->btq/dot_general | solution.py:476
  36.8 2.1 fusion.9
  45.0 1.6 fusion.54
  46.6 1.6 copy.104.refs_3_
  48.2 14.3 %all-gather.7.cloned.1.call-done = bf16[40,416,256]{2,1,0:T(8,128)(2,1)} async-done(((bf16[5,416,256]{2,1,0:T(8,128)(2,1)}), bf16[40,416,256]{2,1,0:T(8,128)(2,1)}) %all-gather.7.cloned.1.call-update) | async-done | bytes 8519696 | tf_op jit(solution)/shard_map/all_gather | solution.py:447
  62.5 1.6 fusion.56
  64.3 6.3 fusion.55
  71.0 2.3 copy-done.7
  73.3 4.8 convolution_convert_fusion.2.refs_2_
  78.1 8.6 convolution_convert_fusion.1.refs_1_
  86.8 46.8 %all-gather.9.cloned.1.call-done = bf16[40,64,2560]{2,1,0:T(8,128)(2,1)} async-done(((bf16[5,64,2560]{2,1,0:T(8,128)(2,1)}), bf16[40,64,2560]{2,1,0:T(8,128)(2,1)}) %all-gather.9.cloned.1.call-update) | async-done | bytes 13107216 | tf_op jit(solution)/shard_map/all_gather | solution.py:447
  133.5 27.0 %fusion.4.refs_10_ = bf16[3,512,2560]{2,1,0:T(8,128)(2,1)} fusion(bf16[2560,2560,1]{1,0,2:T(8,128)(2,1)} %bitcast.114, bf16[12,512,2560]{2,1,0:T(8,128)(2,1)} %param.11, s32[]{:T(128)S(6)} %select_n.148), kind=kOutput, calls=%fused_computation.11 | convolution fusion | flops 20136591360 | bytes 28835844 | tf_op jit(solution)/shard_map/btd,fd->btf/dot_general | solution.py:501
  160.6 78.2 %attn_fwd_bwd.3 = (bf16[1,512,2560]{2,1,0:T(8,128)(2,1)}, bf16[3,512,2560]{2,1,0:T(8,128)(2,1)}, bf16[3,512,1280]{2,1,0:T(8,128)(2,1)}, f32[3,1024,256]{2,1,0:T(...) custom-call(s32[1]{0:T(128)} %bitcast.refs_0_, ...), custom_call_target="tpu_custom_call" | custom-call | flops 40265318400 | bytes 78643200 | tf_op jit(solution)/shard_map/attn_fwd_bwd/pallas_call | solution.py:300
  238.8 79.2 %attn_fwd_bwd.4 = (bf16[1,512,2560]{2,1,0:T(8,128)(2,1)}, bf16[3,512,2560]{2,1,0:T(8,128)(2,1)}, bf16[3,512,1280]{2,1,0:T(8,128)(2,1)}, f32[3,1024,256]{2,1,0:T(...) custom-call(s32[1]{0:T(128)} %bitcast.refs_0_, ...), custom_call_target="tpu_custom_call", output_to_operand_aliasing={{5}: (12, {}), {6}: (13, {}), {1}: (14, {}), {2}: (15, {}),... | custom-call | flops 40265318400 | bytes 78643200 | tf_op jit(solution)/shard_map/attn_fwd_bwd/pallas_call | solution.py:300
  318.0 78.7 %attn_fwd_bwd.5 = (bf16[1,512,2560]{2,1,0:T(8,128)(2,1)}, bf16[3,512,2560]{2,1,0:T(8,128)(2,1)}, bf16[3,512,1280]{2,1,0:T(8,128)(2,1)}, f32[3,1024,256]{2,1,0:T(...) custom-call(s32[1]{0:T(128)} %bitcast.refs_0_, ...), custom_call_target="tpu_custom_call", output_to_operand_aliasing={{5}: (12, {}), {6}: (13, {}), {1}: (14, {}), {2}: (15, {}),... | custom-call | flops 40265318400 | bytes 78643200 | tf_op jit(solution)/shard_map/attn_fwd_bwd/pallas_call | solution.py:300
  396.7 3.5 fusion.19
  400.3 5.2 collective-permute-done.11
  405.5 3.9 fusion.21
  409.5 1.6 copy-done.8
  411.1 5.6 convolution_bitcast_fusion.3
  416.9 9.6 convolution_bitcast_fusion.1
  427.1 6.4 fusion.18
  433.8 9.8 fusion.17
  443.7 33.6 %attn_fwd.1 = bf16[1,512,2560]{2,1,0:T(8,128)(2,1)} custom-call(s32[1]{0:T(128)} %bitcast.refs_0_, bf16[3,512,2560]{2,1,0:T(8,128)(2,1)} %convolution_convert_fusion.1.refs_1_, bf16[3,512,1280]{2,1,0:T(8,128)(2,1)} %convolution_convert_fusion.2.refs_2_, bf16[3,1024,256]{2,1,0:T(8,128)(2,1)} %copy.104.refs_3_, ...), custom_call_target="tpu_custom_call" | custom-call | flops 13421772800 | bytes 78643200 | tf_op jit(solution)/shard_map/attn_fwd/pallas_call | solution.py:300
  478.8 2.4 copy.122
  481.2 3.4 copy.118
  486.4 1.8 copy-done.5
  488.2 11.2 fusion.57
  499.4 8.4 fusion.10
  510.7 1.8 pad_maximum_fusion.1
  519.0 2.1 collective-permute-done.5
  523.5 2.6 pad_maximum_fusion.5
  526.1 99.0 %all-gather.15.cloned.1.call-done.o_ref.refs_0_ = bf16[4,512,2560]{2,1,0:T(8,128)(2,1)} async-done(((bf16[1,512,2560]{2,1,0:T(8,128)(2,1)}), bf16[4,512,2560]{2,1,0:T(8,128)(2,1)}) %all-gather.15.cloned.1.call-update) | async-done | bytes 10485776 | tf_op jit(solution)/shard_map/all_gather | solution.py:508
  625.2 34.2 %out_proj.3.rest_0_ = bf16[4,3,512,2560]{3,2,1,0:T(8,128)(2,1)} custom-call(bf16[4,512,2560]{2,1,0:T(8,128)(2,1)} %all-gather.15.cloned.1.call-done.o_ref.refs_0_, bf16[2560,2560]{1,0:T(8,128)(2,1)} %bitcast.115), custom_call_target="tpu_custom_call" | custom-call | flops 26843545600 | bytes 34078720 | tf_op jit(solution)/shard_map/out_proj/pallas_call | solution.py:332
  661.8 1.6 broadcast_select_fusion.2
  663.4 1.8 maximum_bitcast_fusion.3
  665.2 61.7 %all-gather.13.cloned.1.call-done.o_ref.refs_1_ = bf16[4,512,2560]{2,1,0:T(8,128)(2,1)} async-done(((bf16[1,512,2560]{2,1,0:T(8,128)(2,1)}), bf16[4,512,2560]{2,1,0:T(8,128)(2,1)}) %all-gather.13.cloned.1.call-update) | async-done | bytes 10485776 | tf_op jit(solution)/shard_map/all_gather | solution.py:513
  726.9 101.2 %all-gather.11.cloned.1.call-done.o_ref.refs_2_ = bf16[4,512,2560]{2,1,0:T(8,128)(2,1)} async-done(((bf16[1,512,2560]{2,1,0:T(8,128)(2,1)}), bf16[4,512,2560]{2,1,0:T(8,128)(2,1)}) %all-gather.11.cloned.1.call-update) | async-done | bytes 10485776 | tf_op jit(solution)/shard_map/all_gather | solution.py:513
  828.1 36.1 %grad_wo.1 = f32[640,2560]{1,0:T(8,128)} custom-call(s32[1]{0:T(128)} %bitcast.39.col_ref, bf16[4,512,2560]{2,1,0:T(8,128)(2,1)} %all-gather.15.cloned.1.call-done.o_ref.refs_0_, bf16[4,512,2560]{2,1,0:T(8,128)(2,1)} %all-gather.13.cloned.1.call-done.o_ref.refs_1_, bf16[4,512,2560]{2,1,0:T(8,128)(2,1)} %all-gather.11.cloned.1.call-done.o_ref.refs_2_, ...), custom_call_target="tpu_custom_call" | custom-call | flops 20132659200 | bytes 39321600 | tf_op jit(solution)/shard_map/grad_wo/pallas_call | solution.py:380
  864.2 86.4 %all-gather.17.cloned.1.call-done = bf16[12,512,1056]{1,2,0:T(8,128)(2,1)} async-done(((bf16[3,512,1056]{1,2,0:T(8,128)(2,1)}), bf16[12,512,1056]{1,2,0:T(8,128)(2,1)}) %all-gather.17.cloned.1.call-update) | async-done | bytes 12976144 | tf_op jit(solution)/shard_map/all_gather | solution.py:531
  950.6 42.7 %convolution_bitcast_fusion.a_ref = f32[1056,2560]{1,0:T(8,128)} fusion(bf16[12,512,1056]{1,2,0:T(8,128)(2,1)} %all-gather.17.cloned.1.call-done, bf16[12,512,2560]{2,1,0:T(8,128)(2,1)} %param.10), kind=kOutput, calls=%fused_computation.1 | convolution fusion | flops 33218887680 | bytes 55246848 | tf_op jit(solution)/shard_map/btq,btd->qd/dot_general | solution.py:573
  993.3 34.1 %out_proj.4.rest_0_ = bf16[4,3,512,2560]{3,2,1,0:T(8,128)(2,1)} custom-call(bf16[4,512,2560]{2,1,0:T(8,128)(2,1)} %all-gather.13.cloned.1.call-done.o_ref.refs_1_, bf16[2560,2560]{1,0:T(8,128)(2,1)} %bitcast.116, bf16[4,3,512,2560]{3,2,1,0:T(8,128)(2,1)} %out_proj.3.rest_0_), custom_call_target="tpu_custom_call", output_to_operand_aliasing={{}: (2, {})} | custom-call | flops 26843545600 | bytes 34078720 | tf_op jit(solution)/shard_map/out_proj/pallas_call | solution.py:332
  1027.3 34.2 %out_proj.5 = bf16[4,3,512,2560]{3,2,1,0:T(8,128)(2,1)} custom-call(bf16[4,512,2560]{2,1,0:T(8,128)(2,1)} %all-gather.11.cloned.1.call-done.o_ref.refs_2_, bf16[2560,2560]{1,0:T(8,128)(2,1)} %bitcast.117, bf16[4,3,512,2560]{3,2,1,0:T(8,128)(2,1)} %out_proj.4.rest_0_), custom_call_target="tpu_custom_call", output_to_operand_aliasing={{}: (2, {})} | custom-call | flops 26843545600 | bytes 34078720 | tf_op jit(solution)/shard_map/out_proj/pallas_call | solution.py:332
  1061.6 46.5 %convolution_convert_fusion = bf16[12,512,2560]{2,1,0:T(8,128)(2,1)} fusion(bf16[12,512,1056]{1,2,0:T(8,128)(2,1)} %all-gather.17.cloned.1.call-done, bf16[2560,288]{0,1:T(8,128)(2,1)S(1)} %copy-done.33, bf16[2560,768]{0,1:T(8,128)(2,1)S(1)} %copy-done.3), kind=kOutput, calls=%fused_computation | convolution fusion | flops 33245429760 | bytes 49840128 | tf_op jit(solution)/shard_map/btq,dq->btd/dot_general | solution.py:575
  1108.1 6.9 add.176
  1115.0 14.2 %join_cp.1 = (f32[2560,768]{1,0:T(8,128)}, f32[288,2560]{1,0:T(8,128)}) custom-call(f32[1056,2560]{1,0:T(8,128)} %convolution_bitcast_fusion.a_ref, f32[1056,2560]{1,0:T(8,128)} %collective-permute-done.3.b_ref), custom_call_target="tpu_custom_call" | custom-call | flops 2703360 | bytes 32440320 | tf_op jit(solution)/shard_map/join_cp/pallas_call | solution.py:406
  (171 shorter events, 32.4 us)
Async XLA Ops:
  7.2 55.3 %all-gather.7.cloned.1.call-start = ((), (), s32[]{:S(2)}) async-start(), calls=%async_computation.3 | async-start | bytes 9584640 | tf_op jit(solution)/shard_map/all_gather | solution.py:447
  9.6 123.9 %all-gather.9.cloned.1.call-start = ((), (), s32[]{:S(2)}) async-start(), calls=%async_computation.4 | async-start | bytes 14745600 | tf_op jit(solution)/shard_map/all_gather | solution.py:447
  12.4 509.8 %reduce-scatter.8.cloned.1.call-start = ((), (), s32[]{:S(2)}) async-start(), calls=%async_computation.11 | async-start | bytes 3276800 | tf_op jit(solution)/shard_map/reduce_scatter | solution.py:553
  19.1 19.8 %copy-start.16 = (f32[512,16]{0,1:T(8,128)}, f32[512,16]{0,1:T(8,128)S(1)}, u32[]{:S(2)}) copy-start(f32[512,16]{0,1:T(8,128)S(1)} %get-tuple-element.99) | copy-start | bytes 98308
  19.1 20.7 %copy-start.14 = (f32[512,16]{0,1:T(8,128)}, f32[512,16]{0,1:T(8,128)S(1)}, u32[]{:S(2)}) copy-start(f32[512,16]{0,1:T(8,128)S(1)} %get-tuple-element.100) | copy-start | bytes 98308
  19.1 13.8 %copy-start.34 = (bf16[256]{0:T(256)(128)(2,1)S(1)}, bf16[256]{0:T(256)(128)(2,1)}, u32[]{:S(2)}) copy-start(bf16[256]{0:T(256)(128)(2,1)} %param.15) | copy-start | bytes 1540
  32.0 4.8 copy-start
  32.0 3.6 copy-start.32
  32.1 8.5 collective-permute-start.1
  32.9 2.5 copy-start.30
  35.4 8.1 collective-permute-start
  35.7 3.2 copy-start.28
  36.8 2.1 copy-start.26
  64.3 6.7 copy-start.9
  70.6 2.8 copy-start.7
  71.0 7.1 copy-start.4
  396.7 8.8 copy-start.2
  400.3 5.3 collective-permute-start.11
  409.5 112.8 %reduce-scatter.6.cloned.1.call-start = ((), (), s32[]{:S(2)}) async-start(), calls=%async_computation.10 | async-start | bytes 2457600 | tf_op jit(solution)/shard_map/reduce_scatter | solution.py:552
  416.7 10.3 collective-permute-start.9
  426.5 7.3 collective-permute-start.8
  433.4 90.1 %reduce-scatter.4.cloned.1.call-start = ((), (), s32[]{:S(2)}) async-start(), calls=%async_computation.9 | async-start | bytes 4915200 | tf_op jit(solution)/shard_map/reduce_scatter | solution.py:551
  443.6 181.6 %all-gather.15.cloned.1.call-start = ((), (), s32[]{:S(2)}) async-start(), calls=%async_computation.7 | async-start | bytes 13107200 | tf_op jit(solution)/shard_map/all_gather | solution.py:508
  477.2 249.7 %all-gather.13.cloned.1.call-start = ((), (), s32[]{:S(2)}) async-start(), calls=%async_computation.6 | async-start | bytes 13107200 | tf_op jit(solution)/shard_map/all_gather | solution.py:513
  478.0 350.1 %all-gather.11.cloned.1.call-start = ((), (), s32[]{:S(2)}) async-start(), calls=%async_computation.5 | async-start | bytes 13107200 | tf_op jit(solution)/shard_map/all_gather | solution.py:513
  478.8 471.8 %all-gather.17.cloned.1.call-start = ((), (), s32[]{:S(2)}) async-start(), calls=%async_computation.8 | async-start | bytes 16220160 | tf_op jit(solution)/shard_map/all_gather | solution.py:531
  486.3 13.1 %copy-start.1 = (bf16[3,512,1056]{1,2,0:T(8,128)(2,1)S(1)}, bf16[3,512,1056]{1,2,0:T(8,128)(2,1)}, u32[]{:S(2)}) copy-start(bf16[3,512,1056]{1,2,0:T(8,128)(2,1)} %copy-done) | copy-start | bytes 9732100
  486.3 13.1 %copy-start.10 = (bf16[40,32,768]{2,1,0:T(8,128)(2,1)S(1)}, bf16[40,32,768]{2,1,0:T(8,128)(2,1)}, u32[]{:S(2)}) copy-start(bf16[40,32,768]{2,1,0:T(8,128)(2,1)} %copy-done.9) | copy-start | bytes 5898244
  486.3 13.1 %copy-start.27 = (f32[3,512]{1,0:T(4,128)S(1)}, f32[3,512]{1,0:T(4,128)}, u32[]{:S(2)}) copy-start(f32[3,512]{1,0:T(4,128)} %copy-done.26) | copy-start | bytes 18436
  486.3 13.1 %copy-start.29 = (f32[768]{0:T(1024)S(1)}, f32[768]{0:T(1024)}, u32[]{:S(2)}) copy-start(f32[768]{0:T(1024)} %copy-done.28) | copy-start | bytes 9220
  486.3 13.1 %copy-start.35 = (bf16[3,512,1280]{2,1,0:T(8,128)(2,1)S(1)}, bf16[3,512,1280]{2,1,0:T(8,128)(2,1)}, u32[]{:S(2)}) copy-start(bf16[3,512,1280]{2,1,0:T(8,128)(2,1)} %get-tuple-element.47) | copy-start | bytes 11796484
  486.3 22.6 %collective-permute-start.2 = (f32[3,512,288]{1,2,0:T(8,128)S(1)}, f32[3,512,288]{1,2,0:T(8,128)S(1)}, u32[]{:S(2)}, u32[]{:S(2)}) collective-permute-start(f32[3,512,288]{1,2,0:T(8,128)S(1)} %broadcast_select_fusion), channel_id=1, source_target_pairs={{0,1},{1,0},{2,3},{3,2},{4,5},{5,4},{6,7},{7,6}} | collective-permute-start | bytes 5308424 | tf_op jit(solution)/shard_map/ppermute | solution.py:523
  499.4 8.4 copy-start.25
  512.5 1.2 collective-permute-start.4
  513.7 3.8 collective-permute-start.7
  515.1 3.8 collective-permute-start.6
  516.3 4.7 collective-permute-start.5
  522.3 137.1 %collective-permute-start.12 = (f32[2,128,640]{2,1,0:T(8,128)}, f32[2,128,640]{2,1,0:T(8,128)S(1)}, u32[]{:S(2)}, u32[]{:S(2)}) collective-permute-start(f32[2,128,640]{2,1,0:T(8,128)} %reduce-scatter.8.cloned.1.call-done), channel_id=1, source_target_pairs={{0,1},{1,0},{2,3},{3,2},{4,5},{5,4},{6,7},{7,6}} | collective-permute-start | bytes 1966088 | tf_op jit(solution)/shard_map/ppermute | solution.py:557
  526.1 135.6 %collective-permute-start.10 = (f32[10,96,384]{2,1,0:T(8,128)}, f32[10,96,384]{2,1,0:T(8,128)}, u32[]{:S(2)}, u32[]{:S(2)}) collective-permute-start(f32[10,96,384]{2,1,0:T(8,128)} %pad_maximum_fusion.5), channel_id=1, source_target_pairs={{0,1},{1,0},{2,3},{3,2},{4,5},{5,4},{6,7},{7,6}} | collective-permute-start | bytes 4423688 | tf_op jit(solution)/shard_map/ppermute | solution.py:557
  625.2 34.2 %copy-start.13 = (f32[2,128,640]{2,1,0:T(8,128)S(1)}, f32[2,128,640]{2,1,0:T(8,128)}, u32[]{:S(2)}) copy-start(f32[2,128,640]{2,1,0:T(8,128)} %reduce-scatter.8.cloned.1.call-done) | copy-start | bytes 1966084
  659.5 2.3 copy-start.6
  659.5 2.3 copy-start.11
  864.2 243.9 %collective-permute-start.13 = (f32[640,2560]{1,0:T(8,128)}, f32[640,2560]{1,0:T(8,128)}, u32[]{:S(2)}, u32[]{:S(2)}) collective-permute-start(f32[640,2560]{1,0:T(8,128)} %grad_wo.1), channel_id=1, source_target_pairs={{0,1},{1,0},{2,3},{3,2},{4,5},{5,4},{6,7},{7,6}} | collective-permute-start | bytes 19660808 | tf_op jit(solution)/shard_map/ppermute | solution.py:571
  993.3 121.8 %collective-permute-start.3 = (f32[1056,2560]{1,0:T(8,128)}, f32[1056,2560]{1,0:T(8,128)}, u32[]{:S(2)}, u32[]{:S(2)}) collective-permute-start(f32[1056,2560]{1,0:T(8,128)} %convolution_bitcast_fusion.a_ref), channel_id=1, source_target_pairs={{0,1},{1,0},{2,3},{3,2},{4,5},{5,4},{6,7},{7,6}} | collective-permute-start | bytes 32440328 | tf_op jit(solution)/shard_map/ppermute | solution.py:574
  1027.3 34.2 %copy-start.3 = (bf16[2560,768]{0,1:T(8,128)(2,1)S(1)}, bf16[2560,768]{0,1:T(8,128)(2,1)}, u32[]{:S(2)}) copy-start(bf16[2560,768]{0,1:T(8,128)(2,1)} %copy.97) | copy-start | bytes 11796484
  1027.3 34.2 %copy-start.33 = (bf16[2560,288]{0,1:T(8,128)(2,1)S(1)}, bf16[2560,288]{0,1:T(8,128)(2,1)}, u32[]{:S(2)}) copy-start(bf16[2560,288]{0,1:T(8,128)(2,1)} %param.14) | copy-start | bytes 4423684
  1027.3 80.8 %slice-start = ((s8[6553600]{0:T(1024)(128)(4,1)}), s8[2359296]{0:T(1024)(128)(4,1)S(1)}, s32[]{:S(2)}) async-start(s8[6553600]{0:T(1024)(128)(4,1)} %bitcast.84), calls=%async_computation.12 | async-start | bytes 4718592
  1061.5 46.6 %slice-start.1 = ((s8[6553600]{0:T(1024)(128)(4,1)}), s8[4194304]{0:T(1024)(128)(4,1)S(1)}, s32[]{:S(2)}) async-start(s8[6553600]{0:T(1024)(128)(4,1)} %bitcast.84), calls=%async_computation.13 | async-start | bytes 8388608
  (13 other events, 14.6 us)
Sparse Core Ops, SparseCore 0:
  10.4 52.0 all-gather.6
  64.9 68.6 all-gather.8
  409.6 33.9 reduce-scatter.7
  446.5 28.5 reduce-scatter.5
  478.5 45.0 reduce-scatter.3
  525.7 99.3 all-gather.14
  627.5 99.3 all-gather.12
  728.7 99.3 all-gather.10
  830.4 120.0 all-gather.16

commit v5 on v4

--- a/solution.py
+++ b/solution.py
@@ -311,6 +311,26 @@
     )(*args)
 
 
+def place_kernel(src_ref, y_ref):
+    for t in range(src_ref.shape[0]):
+        y_ref[t, 0] = src_ref[t]
+
+
+def place(nb, src):
+    tp, rows, dim = src.shape
+    tile = 4 * LANES
+    return pl.pallas_call(
+        place_kernel,
+        grid=(dim // tile,),
+        in_specs=[pl.BlockSpec((tp, rows, tile), lambda i: (0, 0, i))],
+        out_specs=pl.BlockSpec((tp, 1, rows, tile), lambda i: (0, 0, 0, i)),
+        out_shape=jax.ShapeDtypeStruct((tp, nb, rows, dim), src.dtype),
+        name="place",
+        compiler_params=pltpu.CompilerParams(dimension_semantics=("arbitrary",), vmem_limit_bytes=VMEM_LIMIT),
+        cost_estimate=pl.CostEstimate(flops=4 * tp * rows * dim, bytes_accessed=4 * tp * rows * dim, transcendentals=0),
+    )(src)
+
+
 def out_kernel(o_ref, w_ref, *rest):
     y_ref = rest[-1]
     w = w_ref[...]
@@ -375,7 +395,8 @@
     turns = tp // per
 
     def o_spec(j):
-        return pl.BlockSpec((per, rows, cols), lambda i, col: (jnp.clip(i - j * turns, 0, turns - 1), 0, col[0]))
+        whole = o_all[j].shape[2] == cols
+        return pl.BlockSpec((per, rows, cols), lambda i, col: (jnp.clip(i - j * turns, 0, turns - 1), 0, 0 if whole else col[0]))
 
     return pl.pallas_call(
         functools.partial(dwo_kernel, tp),
@@ -440,6 +461,9 @@
         def swapped(val):
             return lax.ppermute(val, 'cp', swap_pairs)
 
+        def shifted(val, k):
+            return lax.ppermute(val, 'tp', [(s, (s + k) % tp_size) for s in range(tp_size)])
+
         def own_half(w):
             return lax.dynamic_slice_in_dim(w, cp_rank * half_heads, half_heads, 0)
 
@@ -503,9 +527,13 @@
         rank_arr = cp_rank.astype(jnp.int32).reshape(1)
         attn_args = (rank_arr, qn, qp, ckv_seq, ckvt_seq, kpe4, wuk, wuv, cos128, sin128)
         prev = None
+        cols = heads_dev * v_dim
         o_all = [None] * nb
         o_first = attention(0, None, None, scale, *attn_args)[0]
-        o_all[0] = lax.all_gather(o_first, 'tp', axis=0, tiled=True)
+        own_cols = [lax.dynamic_slice_in_dim(o_first[0], (tp_rank + k) % tp_size * cols, cols, 1) for k in range(tp_size)]
+        own_cols = own_cols[:1] + [shifted(own_cols[k], k) for k in range(1, tp_size)]
+        y_first = jnp.einsum('btf,fd->btd', o_first, wo_all, preferred_element_type=F32).astype(BF16)
+        y_first = lax.all_gather(y_first, 'tp', axis=0, tiled=True)
         for j in (*range(1, nb), 0):
             res = attention(j, [grad_o, kpet_seq], prev, scale, *attn_args)
             prev = res[1:]
@@ -531,7 +559,7 @@
         grad_raw = lax.all_gather(grad_raw, 'tp', axis=0, tiled=True)
         part = jnp.concatenate([grad_g_q, grad_g_kv])
         part = part + swapped(part)
-        parts = jnp.stack([part] + [lax.ppermute(part, 'tp', [(s, (s + k) % tp_size) for s in range(tp_size)]) for k in range(1, tp_size)])
+        parts = jnp.stack([part] + [shifted(part, k) for k in range(1, tp_size)])
         grad_g = sum(lax.dynamic_index_in_dim(parts, (tp_rank - s) % tp_size, 0, keepdims=False) for s in range(tp_size))
 
         q_half = q_lora // 2
@@ -554,7 +582,7 @@
         dwq = jnp.concatenate([dwqn.reshape(heads_dev, nope, q_half), dwqp.reshape(heads_dev, rope_dim, q_half)], axis=1)
 
         def join(part, axis):
-            other = lax.ppermute(part, 'cp', swap_pairs)
+            other = swapped(part)
             return jnp.concatenate([jnp.where(cp_rank == 0, part, other), jnp.where(cp_rank == 0, other, part)], axis=axis)
 
         grad_w_uq = jnp.transpose(join(dwq, 2), (2, 0, 1))
@@ -562,16 +590,18 @@
         grad_w_uk = dw_kv[0].reshape(kv_lora, heads_dev, nope)
         grad_w_uv = dw_kv[1].reshape(kv_lora, heads_dev, v_dim)
 
-        y = None
-        for j in range(nb):
+        y = place(nb, y_first)
+        for j in range(1, nb):
             y = out_proj(j, nb, o_all[j], wo_all, y)
+        own_cols = jnp.stack(own_cols)
+        o_all[0] = jnp.stack([lax.dynamic_index_in_dim(own_cols, (tp_rank - s) % tp_size, 0, keepdims=False) for s in range(tp_size)])
         attn_out = y.reshape(n_batch, seq_local, dim)
-        cols = heads_dev * v_dim
         dwo = grad_wo(o_all, grad_out, cols, tp_rank.astype(jnp.int32).reshape(1))
         grad_w_o = (dwo + lax.ppermute(dwo, 'cp', swap_pairs)).reshape(heads_dev, v_dim, dim)
 
         dw_cat = jnp.einsum('btq,btd->qd', grad_raw, hidden, preferred_element_type=F32)
-        grad_w_dq, dw_dkv = join_cp(dw_cat, lax.ppermute(dw_cat, 'cp', swap_pairs), q_lora)
+        dw_other = lax.ppermute(dw_cat, 'cp', swap_pairs)
+        grad_w_dq, dw_dkv = join_cp(dw_cat, dw_other, q_lora)
         grad_hidden = jnp.einsum('btq,dq->btd', grad_raw, w_cat, preferred_element_type=F32).astype(BF16)
         return (attn_out, grad_hidden, grad_w_dq, grad_g[:q_lora], dw_dkv.T, grad_g[q_lora:], grad_w_uq, grad_w_uk, grad_w_uv, grad_w_o)
 

time: 1150 us -> 1170 us (1.017)
  Pallas kernels: 422 us -> 398 us
  waiting for transfers between devices: 424 us -> 443 us
    ppermute x6 -> x7, waiting for transfers between devices: 4.61 us -> 42.9 us  [the longest x6 42.9 us: shifted(): lax.ppermute(val, 'tp', [(s, (s + k) % tp_size) for s in range(tp_size)])]
    all_gather x1, waiting for transfers between devices: 99 us -> 64.8 us  [per_device(): y_first = lax.all_gather(y_first, 'tp', axis=0, tiled=True)]
    pallas_call x3 -> x2, Pallas kernels: 102 us -> 68.2 us  [out_proj(): pl.pallas_call(out_kernel, grid=(dim // tile,), in_specs=in_specs, out_sp...]
    all_gather x1, waiting for transfers between devices: 86.4 us -> 112 us  [per_device(): grad_raw = lax.all_gather(grad_raw, 'tp', axis=0, tiled=True)]
    dot_general x0 -> x1, matrix products: none -> 11.9 us  [per_device(): jnp.einsum('btf,fd->btd', o_first, wo_all, preferred_element_type=F32)]
  transfers between devices with their start and end apart: 23 -> 26, of which waited for: 13 -> 12; matrix products, arithmetic and copies ran while one was open for 20% -> 21% of each run, Pallas kernels for 15% -> 13%
where the time goes in v5:
time: 1170 us; the launch traced here: 1160 us
  waiting for transfers between devices  443 us (38%)
  Pallas kernels  398 us (34%)
  matrix products  203 us (17%)
  local copies, waits for them, and re-layouts  45.9 us (4%)
  other arithmetic  40.8 us (3%)
  between operations  15.1 us (1%)
    pallas_call x4, Pallas kernels, attention(): pl.pallas_call(functools.partial(attn_kernel, grad, first, scale), grid=(...  269 us
    all_gather x2, waiting for transfers between devices, per_device(): o_all[j] = lax.all_gather(res[0], 'tp', axis=0, tiled=True)  153 us
    all_gather x1, waiting for transfers between devices, per_device(): grad_raw = lax.all_gather(grad_raw, 'tp', axis=0, tiled=True)  112 us
    pallas_call x2, Pallas kernels, out_proj(): pl.pallas_call(out_kernel, grid=(dim // tile,), in_specs=in_specs, out_sp...  68.2 us
    all_gather x1, waiting for transfers between devices, per_device(): y_first = lax.all_gather(y_first, 'tp', axis=0, tiled=True)  64.8 us
    all_gather x2, waiting for transfers between devices, gather_weight(): return lax.all_gather(half, ('tp', 'cp'), axis=0, tiled=True)  61.3 us
    dot_general x1, matrix products, per_device(): jnp.einsum('btq,dq->btd', grad_raw, w_cat, preferred_element_type=F32)  46.5 us
    ppermute x6, waiting for transfers between devices, shifted(): lax.ppermute(val, 'tp', [(s, (s + k) % tp_size) for s in range(tp_size)])  42.9 us
  transfers between devices with their start and end apart: 26, of which 12 were waited for; matrix products, arithmetic and copies ran while one was open for 21% of the time, Pallas kernels for 13%

profile of v5, /device:TPU:0, one launch (start us, length us, event | category | flops | bytes accessed | tf_op | source)
XLA Modules:
  0.0 1156.8 jit_solution(12022244012776146257)
XLA Ops:
  9.7 2.7 constant_dynamic-slice_fusion.9
  12.5 6.3 copy.97
  19.1 13.0 %fusion.14 = bf16[3,512,1056]{1,2,0:T(8,128)(2,1)S(1)} fusion(bf16[12,512,2560]{2,1,0:T(8,128)(2,1)} %param.10, s32[]{:T(128)S(6)} %select_n.187, bf16[2560,288]{0,1:T(8,128)(2,1)} %param.14, bf16[2560,768]{0,1:T(8,128)(2,1)} %copy.97), kind=kOutput, calls=%fused_computation.26 | convolution fusion | flops 8317157376 | bytes 16515076 | tf_op jit(solution)/shard_map/btd,dq->btq/dot_general | solution.py:500
  36.8 2.0 fusion.9
  48.0 14.5 %all-gather.8.cloned.1.call-done = bf16[40,416,256]{2,1,0:T(8,128)(2,1)} async-done(((bf16[5,416,256]{2,1,0:T(8,128)(2,1)}), bf16[40,416,256]{2,1,0:T(8,128)(2,1)}) %all-gather.8.cloned.1.call-update) | async-done | bytes 8519696 | tf_op jit(solution)/shard_map/all_gather | solution.py:471
  64.3 6.3 fusion.59
  71.0 2.3 copy-done.8
  73.4 4.8 convolution_convert_fusion.2.refs_2_
  78.1 8.6 convolution_convert_fusion.1.refs_1_
  86.8 46.8 %all-gather.10.cloned.1.call-done = bf16[40,64,2560]{2,1,0:T(8,128)(2,1)} async-done(((bf16[5,64,2560]{2,1,0:T(8,128)(2,1)}), bf16[40,64,2560]{2,1,0:T(8,128)(2,1)}) %all-gather.10.cloned.1.call-update) | async-done | bytes 13107216 | tf_op jit(solution)/shard_map/all_gather | solution.py:471
  133.5 27.0 %fusion.4.refs_10_ = bf16[3,512,2560]{2,1,0:T(8,128)(2,1)} fusion(bf16[2560,2560,1]{1,0,2:T(8,128)(2,1)} %bitcast.133, bf16[12,512,2560]{2,1,0:T(8,128)(2,1)} %param.11, s32[]{:T(128)S(6)} %select_n.187), kind=kOutput, calls=%fused_computation.11 | convolution fusion | flops 20136591360 | bytes 28835844 | tf_op jit(solution)/shard_map/btd,fd->btf/dot_general | solution.py:525
  160.6 78.2 %attn_fwd_bwd.3 = (bf16[1,512,2560]{2,1,0:T(8,128)(2,1)}, bf16[3,512,2560]{2,1,0:T(8,128)(2,1)}, bf16[3,512,1280]{2,1,0:T(8,128)(2,1)}, f32[3,1024,256]{2,1,0:T(...) custom-call(s32[1]{0:T(128)} %bitcast.refs_0_, ...), custom_call_target="tpu_custom_call" | custom-call | flops 40265318400 | bytes 78643200 | tf_op jit(solution)/shard_map/attn_fwd_bwd/pallas_call | solution.py:300
  238.8 79.2 %attn_fwd_bwd.4 = (bf16[1,512,2560]{2,1,0:T(8,128)(2,1)}, bf16[3,512,2560]{2,1,0:T(8,128)(2,1)}, bf16[3,512,1280]{2,1,0:T(8,128)(2,1)}, f32[3,1024,256]{2,1,0:T(...) custom-call(s32[1]{0:T(128)} %bitcast.refs_0_, ...), custom_call_target="tpu_custom_call", output_to_operand_aliasing={{5}: (12, {}), {6}: (13, {}), {1}: (14, {}), {2}: (15, {}),... | custom-call | flops 40265318400 | bytes 78643200 | tf_op jit(solution)/shard_map/attn_fwd_bwd/pallas_call | solution.py:300
  318.0 78.8 %attn_fwd_bwd.5 = (bf16[1,512,2560]{2,1,0:T(8,128)(2,1)}, bf16[3,512,2560]{2,1,0:T(8,128)(2,1)}, bf16[3,512,1280]{2,1,0:T(8,128)(2,1)}, f32[3,1024,256]{2,1,0:T(...) custom-call(s32[1]{0:T(128)} %bitcast.refs_0_, ...), custom_call_target="tpu_custom_call", output_to_operand_aliasing={{5}: (12, {}), {6}: (13, {}), {1}: (14, {}), {2}: (15, {}),... | custom-call | flops 40265318400 | bytes 78643200 | tf_op jit(solution)/shard_map/attn_fwd_bwd/pallas_call | solution.py:300
  396.8 5.7 convolution_bitcast_fusion.3
  402.5 6.2 convolution_bitcast_fusion.1
  409.3 6.3 fusion.18
  416.0 10.1 fusion.17
  426.2 1.8 copy-done.2
  428.0 3.0 fusion.19
  431.4 4.9 collective-permute-done.11
  436.3 3.9 fusion.21
  441.6 33.2 %attn_fwd.1 = bf16[1,512,2560]{2,1,0:T(8,128)(2,1)} custom-call(s32[1]{0:T(128)} %bitcast.refs_0_, bf16[3,512,2560]{2,1,0:T(8,128)(2,1)} %convolution_convert_fusion.1.refs_1_, bf16[3,512,1280]{2,1,0:T(8,128)(2,1)} %convolution_convert_fusion.2.refs_2_, bf16[3,1024,256]{2,1,0:T(8,128)(2,1)} %copy.104.refs_3_, ...), custom_call_target="tpu_custom_call" | custom-call | flops 13421772800 | bytes 78643200 | tf_op jit(solution)/shard_map/attn_fwd/pallas_call | solution.py:300
  474.8 11.9 %convolution_convert_fusion.3 = bf16[512,2560]{1,0:T(8,128)(2,1)} fusion(bf16[2560,2560]{1,0:T(8,128)(2,1)} %bitcast.134, bf16[1,512,2560]{2,1,0:T(8,128)(2,1)} %attn_fwd.1), kind=kOutput, calls=%fused_computation.29 | convolution fusion | flops 6712197120 | bytes 18350080 | tf_op jit(solution)/shard_map/btf,fd->btd/dot_general | solution.py:535
  487.2 2.4 copy.122
  489.6 3.1 copy.118
  496.3 11.1 fusion.61
  507.4 8.5 fusion.10
  518.8 2.0 pad_maximum_fusion.1
  527.5 16.2 %collective-permute-done.13 = bf16[512,640]{1,0:T(8,128)(2,1)S(1)} collective-permute-done((bf16[512,640]{1,0:T(8,128)(2,1)}, bf16[512,640]{1,0:T(8,128)(2,1)S(1)}, u32[]{:S(2)}, u32[]{:S(2)}) %collective-permute-start.13) | collective-permute-done | bytes 655392 | tf_op jit(solution)/shard_map/ppermute | solution.py:465
  543.7 25.9 %collective-permute-done.14 = bf16[512,640]{1,0:T(8,128)(2,1)S(1)} collective-permute-done((bf16[512,640]{1,0:T(8,128)(2,1)}, bf16[512,640]{1,0:T(8,128)(2,1)S(1)}, u32[]{:S(2)}, u32[]{:S(2)}) %collective-permute-start.14) | collective-permute-done | bytes 655392 | tf_op jit(solution)/shard_map/ppermute | solution.py:465
  571.2 1.9 pad_maximum_fusion.2
  573.2 2.6 pad_maximum_fusion.7
  581.5 2.4 collective-permute-start.7
  583.9 3.4 pad_maximum_fusion.3.refs_0_
  592.5 1.8 maximum_bitcast_fusion.3
  594.3 51.5 %all-gather.12.cloned.1.call-done.o_ref.refs_2_ = bf16[4,512,2560]{2,1,0:T(8,128)(2,1)} async-done(((bf16[1,512,2560]{2,1,0:T(8,128)(2,1)}), bf16[4,512,2560]{2,1,0:T(8,128)(2,1)}) %all-gather.12.cloned.1.call-update) | async-done | bytes 10485776 | tf_op jit(solution)/shard_map/all_gather | solution.py:541
  645.8 101.7 %all-gather.14.cloned.1.call-done.o_ref.refs_1_ = bf16[4,512,2560]{2,1,0:T(8,128)(2,1)} async-done(((bf16[1,512,2560]{2,1,0:T(8,128)(2,1)}), bf16[4,512,2560]{2,1,0:T(8,128)(2,1)}) %all-gather.14.cloned.1.call-update) | async-done | bytes 10485776 | tf_op jit(solution)/shard_map/all_gather | solution.py:541
  747.5 36.4 %grad_wo.1 = f32[640,2560]{1,0:T(8,128)} custom-call(s32[1]{0:T(128)} %bitcast.41.col_ref, bf16[4,512,640]{2,1,0:T(8,128)(2,1)} %pad_maximum_fusion.3.refs_0_, bf16[4,512,2560]{2,1,0:T(8,128)(2,1)} %all-gather.14.cloned.1.call-done.o_ref.refs_1_, bf16[4,512,2560]{2,1,0:T(8,128)(2,1)} %all-gather.12.cloned.1.call-done.o_ref.refs_2_, ...), custom_call_target="tpu_custom_call" | custom-call | flops 20132659200 | bytes 39321600 | tf_op jit(solution)/shard_map/grad_wo/pallas_call | solution.py:401
  783.9 64.8 %all-gather.18.cloned.1.call-done = bf16[2048,2560]{1,0:T(8,128)(2,1)} async-done(((bf16[512,2560]{1,0:T(8,128)(2,1)}), bf16[2048,2560]{1,0:T(8,128)(2,1)}) %all-gather.18.cloned.1.call-update) | async-done | bytes 10485776 | tf_op jit(solution)/shard_map/all_gather | solution.py:536
  848.7 10.0 place.1.rest_0_
  858.7 112.5 %all-gather.16.cloned.1.call-done = bf16[12,512,1056]{1,2,0:T(8,128)(2,1)} async-done(((bf16[3,512,1056]{1,2,0:T(8,128)(2,1)}), bf16[12,512,1056]{1,2,0:T(8,128)(2,1)}) %all-gather.16.cloned.1.call-update) | async-done | bytes 12976144 | tf_op jit(solution)/shard_map/all_gather | solution.py:559
  971.2 42.7 %convolution_bitcast_fusion.a_ref = f32[1056,2560]{1,0:T(8,128)} fusion(bf16[12,512,1056]{1,2,0:T(8,128)(2,1)} %all-gather.16.cloned.1.call-done, bf16[12,512,2560]{2,1,0:T(8,128)(2,1)} %param.10), kind=kOutput, calls=%fused_computation.1 | convolution fusion | flops 33218887680 | bytes 55246848 | tf_op jit(solution)/shard_map/btq,btd->qd/dot_general | solution.py:602
  1013.9 34.1 %out_proj.2.rest_0_ = bf16[4,3,512,2560]{3,2,1,0:T(8,128)(2,1)} custom-call(bf16[4,512,2560]{2,1,0:T(8,128)(2,1)} %all-gather.14.cloned.1.call-done.o_ref.refs_1_, bf16[2560,2560]{1,0:T(8,128)(2,1)} %bitcast.135, bf16[4,3,512,2560]{3,2,1,0:T(8,128)(2,1)} %place.1.rest_0_), custom_call_target="tpu_custom_call", output_to_operand_aliasing={{}: (2, {})} | custom-call | flops 26843545600 | bytes 34078720 | tf_op jit(solution)/shard_map/out_proj/pallas_call | solution.py:352
  1047.9 34.2 %out_proj.3 = bf16[4,3,512,2560]{3,2,1,0:T(8,128)(2,1)} custom-call(bf16[4,512,2560]{2,1,0:T(8,128)(2,1)} %all-gather.12.cloned.1.call-done.o_ref.refs_2_, bf16[2560,2560]{1,0:T(8,128)(2,1)} %bitcast.136, bf16[4,3,512,2560]{3,2,1,0:T(8,128)(2,1)} %out_proj.2.rest_0_), custom_call_target="tpu_custom_call", output_to_operand_aliasing={{}: (2, {})} | custom-call | flops 26843545600 | bytes 34078720 | tf_op jit(solution)/shard_map/out_proj/pallas_call | solution.py:352
  1082.1 46.5 %convolution_convert_fusion = bf16[12,512,2560]{2,1,0:T(8,128)(2,1)} fusion(bf16[12,512,1056]{1,2,0:T(8,128)(2,1)} %all-gather.16.cloned.1.call-done, bf16[2560,288]{0,1:T(8,128)(2,1)S(1)} %copy-done.37, bf16[2560,768]{0,1:T(8,128)(2,1)S(1)} %copy-done.3), kind=kOutput, calls=%fused_computation | convolution fusion | flops 33245429760 | bytes 49840128 | tf_op jit(solution)/shard_map/btq,dq->btd/dot_general | solution.py:605
  1128.7 6.9 add.226
  1135.6 14.2 %join_cp.1 = (f32[2560,768]{1,0:T(8,128)}, f32[288,2560]{1,0:T(8,128)}) custom-call(f32[1056,2560]{1,0:T(8,128)} %convolution_bitcast_fusion.a_ref, f32[1056,2560]{1,0:T(8,128)} %collective-permute-done.3.b_ref), custom_call_target="tpu_custom_call" | custom-call | flops 2703360 | bytes 32440320 | tf_op jit(solution)/shard_map/join_cp/pallas_call | solution.py:427
  (192 shorter events, 47.2 us)
Async XLA Ops:
  7.2 55.3 %all-gather.8.cloned.1.call-start = ((), (), s32[]{:S(2)}) async-start(), calls=%async_computation.3 | async-start | bytes 9584640 | tf_op jit(solution)/shard_map/all_gather | solution.py:471
  9.6 123.9 %all-gather.10.cloned.1.call-start = ((), (), s32[]{:S(2)}) async-start(), calls=%async_computation.4 | async-start | bytes 14745600 | tf_op jit(solution)/shard_map/all_gather | solution.py:471
  12.4 560.7 %reduce-scatter.6.cloned.1.call-start = ((), (), s32[]{:S(2)}) async-start(), calls=%async_computation.9 | async-start | bytes 2457600 | tf_op jit(solution)/shard_map/reduce_scatter | solution.py:580
  19.1 19.7 %copy-start.20 = (f32[512,16]{0,1:T(8,128)}, f32[512,16]{0,1:T(8,128)S(1)}, u32[]{:S(2)}) copy-start(f32[512,16]{0,1:T(8,128)S(1)} %get-tuple-element.107) | copy-start | bytes 98308
  19.1 20.6 %copy-start.18 = (f32[512,16]{0,1:T(8,128)}, f32[512,16]{0,1:T(8,128)S(1)}, u32[]{:S(2)}) copy-start(f32[512,16]{0,1:T(8,128)S(1)} %get-tuple-element.108) | copy-start | bytes 98308
  19.1 13.8 %copy-start.38 = (bf16[256]{0:T(256)(128)(2,1)S(1)}, bf16[256]{0:T(256)(128)(2,1)}, u32[]{:S(2)}) copy-start(bf16[256]{0:T(256)(128)(2,1)} %param.15) | copy-start | bytes 1540
  32.1 4.7 copy-start
  32.1 3.6 copy-start.36
  32.2 8.4 collective-permute-start.1
  35.4 8.0 collective-permute-start
  35.7 3.1 copy-start.32
  64.3 6.7 copy-start.10
  71.0 7.1 copy-start.4
  317.9 78.8 %copy-start.9 = (bf16[3,512,768]{1,2,0:T(8,128)(2,1)S(1)}, bf16[3,512,768]{1,2,0:T(8,128)(2,1)}, u32[]{:S(2)}) copy-start(bf16[3,512,768]{1,2,0:T(8,128)(2,1)} %fusion.9) | copy-start | bytes 7077892
  396.8 5.8 copy-start.40
  402.5 6.7 collective-permute-start.9
  408.8 7.3 collective-permute-start.8
  415.6 157.6 %reduce-scatter.4.cloned.1.call-start = ((), (), s32[]{:S(2)}) async-start(), calls=%async_computation.8 | async-start | bytes 4915200 | tf_op jit(solution)/shard_map/reduce_scatter | solution.py:579
  426.2 151.4 %reduce-scatter.8.cloned.1.call-start = ((), (), s32[]{:S(2)}) async-start(), calls=%async_computation.10 | async-start | bytes 3276800 | tf_op jit(solution)/shard_map/reduce_scatter | solution.py:581
  431.0 5.3 collective-permute-start.11
  440.3 205.5 %all-gather.12.cloned.1.call-start = ((), (), s32[]{:S(2)}) async-start(), calls=%async_computation.5 | async-start | bytes 13107200 | tf_op jit(solution)/shard_map/all_gather | solution.py:541
  440.8 306.7 %all-gather.14.cloned.1.call-start = ((), (), s32[]{:S(2)}) async-start(), calls=%async_computation.6 | async-start | bytes 13107200 | tf_op jit(solution)/shard_map/all_gather | solution.py:541
  441.6 407.1 %all-gather.18.cloned.1.call-start = ((), (), s32[]{:S(2)}) async-start(), calls=%async_computation.11 | async-start | bytes 13107200 | tf_op jit(solution)/shard_map/all_gather | solution.py:536
  486.8 484.4 %all-gather.16.cloned.1.call-start = ((), (), s32[]{:S(2)}) async-start(), calls=%async_computation.7 | async-start | bytes 16220160 | tf_op jit(solution)/shard_map/all_gather | solution.py:559
  494.4 13.0 %copy-start.1 = (bf16[3,512,1056]{1,2,0:T(8,128)(2,1)S(1)}, bf16[3,512,1056]{1,2,0:T(8,128)(2,1)}, u32[]{:S(2)}) copy-start(bf16[3,512,1056]{1,2,0:T(8,128)(2,1)} %copy-done) | copy-start | bytes 9732100
  494.4 13.0 %copy-start.11 = (bf16[40,32,768]{2,1,0:T(8,128)(2,1)S(1)}, bf16[40,32,768]{2,1,0:T(8,128)(2,1)}, u32[]{:S(2)}) copy-start(bf16[40,32,768]{2,1,0:T(8,128)(2,1)} %copy-done.10) | copy-start | bytes 5898244
  494.4 13.0 %copy-start.31 = (f32[3,512]{1,0:T(4,128)S(1)}, f32[3,512]{1,0:T(4,128)}, u32[]{:S(2)}) copy-start(f32[3,512]{1,0:T(4,128)} %copy-done.30) | copy-start | bytes 18436
  494.5 13.0 %copy-start.33 = (f32[768]{0:T(1024)S(1)}, f32[768]{0:T(1024)}, u32[]{:S(2)}) copy-start(f32[768]{0:T(1024)} %copy-done.32) | copy-start | bytes 9220
  494.5 13.0 %copy-start.39 = (bf16[3,512,1280]{2,1,0:T(8,128)(2,1)S(1)}, bf16[3,512,1280]{2,1,0:T(8,128)(2,1)}, u32[]{:S(2)}) copy-start(bf16[3,512,1280]{2,1,0:T(8,128)(2,1)} %get-tuple-element.47) | copy-start | bytes 11796484
  494.5 22.7 %collective-permute-start.2 = (f32[3,512,288]{1,2,0:T(8,128)S(1)}, f32[3,512,288]{1,2,0:T(8,128)S(1)}, u32[]{:S(2)}, u32[]{:S(2)}) collective-permute-start(f32[3,512,288]{1,2,0:T(8,128)S(1)} %broadcast_select_fusion), channel_id=1, source_target_pairs={{0,1},{1,0},{2,3},{3,2},{4,5},{5,4},{6,7},{7,6}} | collective-permute-start | bytes 5308424 | tf_op jit(solution)/shard_map/ppermute | solution.py:551
  507.4 8.6 copy-start.29
  523.9 19.8 %collective-permute-start.13 = (bf16[512,640]{1,0:T(8,128)(2,1)}, bf16[512,640]{1,0:T(8,128)(2,1)S(1)}, u32[]{:S(2)}, u32[]{:S(2)}) collective-permute-start(bf16[512,640]{1,0:T(8,128)(2,1)} %get-tuple-element.85), channel_id=1, source_target_pairs={{0,2},{2,4},{4,6},{6,0},{1,3},{3,5},{5,7},{7,1}} | collective-permute-start | bytes 1966088 | tf_op jit(solution)/shard_map/ppermute | solution.py:465
  525.2 44.4 %collective-permute-start.14 = (bf16[512,640]{1,0:T(8,128)(2,1)}, bf16[512,640]{1,0:T(8,128)(2,1)S(1)}, u32[]{:S(2)}, u32[]{:S(2)}) collective-permute-start(bf16[512,640]{1,0:T(8,128)(2,1)} %get-tuple-element.84), channel_id=1, source_target_pairs={{0,4},{2,6},{4,0},{6,2},{1,5},{3,7},{5,1},{7,3}} | collective-permute-start | bytes 1966088 | tf_op jit(solution)/shard_map/ppermute | solution.py:465
  525.8 44.6 %collective-permute-start.15 = (bf16[512,640]{1,0:T(8,128)(2,1)}, bf16[512,640]{1,0:T(8,128)(2,1)S(1)}, u32[]{:S(2)}, u32[]{:S(2)}) collective-permute-start(bf16[512,640]{1,0:T(8,128)(2,1)} %get-tuple-element.83), channel_id=1, source_target_pairs={{0,6},{2,0},{4,2},{6,4},{1,7},{3,1},{5,3},{7,5}} | collective-permute-start | bytes 1966088 | tf_op jit(solution)/shard_map/ppermute | solution.py:465
  543.7 26.7 %copy-start.14 = (bf16[512,640]{1,0:T(8,128)(2,1)}, bf16[512,640]{1,0:T(8,128)(2,1)S(1)}, u32[]{:S(2)}) copy-start(bf16[512,640]{1,0:T(8,128)(2,1)S(1)} %collective-permute-done.13) | copy-start | bytes 1966084
  575.8 15.1 %collective-permute-start.10 = (f32[10,96,384]{2,1,0:T(8,128)}, f32[10,96,384]{2,1,0:T(8,128)}, u32[]{:S(2)}, u32[]{:S(2)}) collective-permute-start(f32[10,96,384]{2,1,0:T(8,128)} %pad_maximum_fusion.7), channel_id=1, source_target_pairs={{0,1},{1,0},{2,3},{3,2},{4,5},{5,4},{6,7},{7,6}} | collective-permute-start | bytes 4423688 | tf_op jit(solution)/shard_map/ppermute | solution.py:462
  575.8 3.6 collective-permute-start.4
  577.6 10.9 collective-permute-start.12
  579.4 7.9 collective-permute-start.5
  580.9 6.4 collective-permute-start.6
  581.5 5.8 collective-permute-start.7
  583.9 4.7 copy-start.17
  783.9 344.8 %collective-permute-start.16 = (f32[640,2560]{1,0:T(8,128)}, f32[640,2560]{1,0:T(8,128)}, u32[]{:S(2)}, u32[]{:S(2)}) collective-permute-start(f32[640,2560]{1,0:T(8,128)} %grad_wo.1), channel_id=1, source_target_pairs={{0,1},{1,0},{2,3},{3,2},{4,5},{5,4},{6,7},{7,6}} | collective-permute-start | bytes 19660808 | tf_op jit(solution)/shard_map/ppermute | solution.py:600
  1013.9 121.8 %collective-permute-start.3 = (f32[1056,2560]{1,0:T(8,128)}, f32[1056,2560]{1,0:T(8,128)}, u32[]{:S(2)}, u32[]{:S(2)}) collective-permute-start(f32[1056,2560]{1,0:T(8,128)} %convolution_bitcast_fusion.a_ref), channel_id=1, source_target_pairs={{0,1},{1,0},{2,3},{3,2},{4,5},{5,4},{6,7},{7,6}} | collective-permute-start | bytes 32440328 | tf_op jit(solution)/shard_map/ppermute | solution.py:603
  1047.9 34.2 %copy-start.3 = (bf16[2560,768]{0,1:T(8,128)(2,1)S(1)}, bf16[2560,768]{0,1:T(8,128)(2,1)}, u32[]{:S(2)}) copy-start(bf16[2560,768]{0,1:T(8,128)(2,1)} %copy.97) | copy-start | bytes 11796484
  1047.9 34.2 %copy-start.37 = (bf16[2560,288]{0,1:T(8,128)(2,1)S(1)}, bf16[2560,288]{0,1:T(8,128)(2,1)}, u32[]{:S(2)}) copy-start(bf16[2560,288]{0,1:T(8,128)(2,1)} %param.14) | copy-start | bytes 4423684
  1047.9 80.8 %slice-start = ((s8[6553600]{0:T(1024)(128)(4,1)}), s8[2359296]{0:T(1024)(128)(4,1)S(1)}, s32[]{:S(2)}) async-start(s8[6553600]{0:T(1024)(128)(4,1)} %bitcast.100), calls=%async_computation.12 | async-start | bytes 4718592
  1082.1 46.6 %slice-start.1 = ((s8[6553600]{0:T(1024)(128)(4,1)}), s8[4194304]{0:T(1024)(128)(4,1)S(1)}, s32[]{:S(2)}) async-start(s8[6553600]{0:T(1024)(128)(4,1)} %bitcast.100), calls=%async_computation.13 | async-start | bytes 8388608
  (21 other events, 30.0 us)
Sparse Core Ops, SparseCore 0:
  10.4 52.0 all-gather.7
  64.9 68.6 all-gather.9
  415.7 28.5 reduce-scatter.5
  447.7 44.8 reduce-scatter.3
  495.4 35.4 reduce-scatter.7
  532.5 113.2 all-gather.11
  648.1 99.3 all-gather.13
  749.3 99.3 all-gather.17
  851.1 120.0 all-gather.15
